TPU v7x, 32 devices: a whole 2x2x4 slice. The times are simulated.
32 devices in a mesh: fsdp: 8 (over z, y), rep: 4 (over x, core).
Axes of the slice: x: 2, y: 2, z: 4, core: 2. Of those that a mesh axis runs over, the one named last changes fastest.
Arguments:
- latents: float32 [192, 4, 1024], P(('fsdp', 'rep')), may hold values from -6 to 6
- tsteps: int32 [192], P(('fsdp', 'rep')), may hold values from 0 to 999
- labels: int32 [192], P(('fsdp', 'rep')), may hold values from 0 to 1000
- noise: float32 [192, 4, 1024], P(('fsdp', 'rep')), may hold values from -6 to 6
- layer_in: float32 [2, 384, 5376], P(None, 'fsdp'), may hold values from -0.3125 to 0.3125
- layer_out: float32 [2, 1536, 384], P(None, 'fsdp'), may hold values from -0.15625 to 0.15625
- edge_mat: float32 [384, 2457], P('fsdp'), may hold values from -4 to 4
- layer_bias: float32 [2, 5376], replicated, may hold values from -2 to 2
- top_bias: float32 [1952], replicated, may hold values from -2 to 2
- in_rows: float32 [2, 384], P(None, 'fsdp'), may hold values from 0.0005 to 0.2
- in_cols: float32 [2, 5376], replicated, may hold values from 0.005 to 0.05
- out_rows: float32 [2, 1536], P(None, 'fsdp'), may hold values from 0.0005 to 0.2
- out_cols: float32 [2, 384], replicated, may hold values from 0.005 to 0.05
- edge_rows: float32 [384], P('fsdp'), may hold values from 0.0005 to 0.2
- edge_cols: float32 [2457], replicated, may hold values from 0.005 to 0.05
- layer_bias_v: float32 [2, 5376], replicated, may hold values from 0.005 to 0.05
- top_bias_v: float32 [1952], replicated, may hold values from 0.005 to 0.05
Outputs:
- loss: float32 [], replicated
- layer_in_new: float32 [2, 384, 5376], P(None, 'fsdp')
- layer_out_new: float32 [2, 1536, 384], P(None, 'fsdp')
- edge_mat_new: float32 [384, 2457], P('fsdp')
- layer_bias_new: float32 [2, 5376], replicated
- top_bias_new: float32 [1952], replicated
- in_rows_new: float32 [2, 384], P(None, 'fsdp')
- in_cols_new: float32 [2, 5376], replicated
- out_rows_new: float32 [2, 1536], P(None, 'fsdp')
- out_cols_new: float32 [2, 384], replicated
- edge_rows_new: float32 [384], P('fsdp')
- edge_cols_new: float32 [2457], replicated
- layer_bias_v_new: float32 [2, 5376], replicated
- top_bias_v_new: float32 [1952], replicated
- clip_roots: float32 [5], replicated
All inputs are finite; a program needn't handle non-finite values.
Results may differ from a plain program's by a relative error of at most 0.0015.
The roundings to bfloat16 on the way count: a program that leaves them out, or rounds other values in their place, can miss the bound.
Values may be sent and summed in bfloat16 or wider, within the bound.
A program may use at most 256 MiB of HBM per device.

v0:
```python
import math

import jax
import jax.numpy as jnp
from jax import lax
from jax.sharding import PartitionSpec as P

D = 384
HEADS = 6
HEAD_DIM = 64
FF = 1536
CHANNELS = 4
PATCH = 2
GRID = 32
TSTEPS = 1000
NCLS = 1001
FREQ = 256
MICRO = 3
PATCH_IN = 16


eps_norm = 1e-06
eps_stat = 1e-30
decay = 0.5
rate = 0.01
clip_level = 1.0


def round_value(values):
    return lax.optimization_barrier(values.astype(jnp.bfloat16)).astype(jnp.float32)


def rounders():
    rounding = jax.custom_vjp(round_value)

    def keep_forward(values):
        return (round_value(values), None)

    def pass_backward(kept, grad):
        return (grad,)

    rounding.defvjp(keep_forward, pass_backward)

    def unchanged(values):
        return values

    backing = jax.custom_vjp(unchanged)

    def back_forward(values):
        return (values, None)

    def back_backward(kept, grad):
        return (round_value(grad),)

    backing.defvjp(back_forward, back_backward)
    return (rounding, backing)


def low(values):
    return rounders()[0](values)


def low_back(values):
    return rounders()[1](values)


def mult(left, right, form):
    return jnp.einsum(form, left, right, preferred_element_type=jnp.float32)


def normalize(values):
    center = values - jnp.mean(values, axis=-1, keepdims=True)
    spread = jnp.mean(center * center, axis=-1, keepdims=True)
    return center * lax.rsqrt(spread + eps_norm)


def mix_weights(tsteps):
    betas = 0.0001 + (0.02 - 0.0001) * jnp.arange(TSTEPS, dtype=jnp.float32) / (TSTEPS - 1)
    alpha_bar = jnp.exp(jnp.cumsum(jnp.log(1.0 - betas)))
    picked = jnp.arange(TSTEPS)[None, :] == tsteps[:, None]
    return jnp.sum(jnp.where(picked, alpha_bar[None, :], 0.0), axis=1)


def patchify(latent_rows):
    images = latent_rows.shape[0]
    grid_side = GRID // PATCH
    shaped = latent_rows.reshape(images, CHANNELS, grid_side, PATCH, grid_side, PATCH)
    shaped = jnp.transpose(shaped, (0, 2, 4, 1, 3, 5))
    return shaped.reshape(images, grid_side * grid_side, CHANNELS * PATCH * PATCH)


def position_table():
    grid_side = GRID // PATCH
    quarter = D // 4
    omegas = 1.0 / 10000.0 ** (jnp.arange(quarter, dtype=jnp.float32) / quarter)
    places = jnp.arange(grid_side * grid_side)
    across = (places % grid_side).astype(jnp.float32)
    downward = (places // grid_side).astype(jnp.float32)

    def one_axis(coords):
        angles = coords[:, None] * omegas[None, :]
        return jnp.concatenate([jnp.sin(angles), jnp.cos(angles)], axis=1)

    return jnp.concatenate([one_axis(across), one_axis(downward)], axis=1)


def time_features(tsteps):
    half_freq = FREQ // 2
    frequencies = jnp.exp(-math.log(10000.0) * jnp.arange(half_freq, dtype=jnp.float32) / half_freq)
    angles = tsteps.astype(jnp.float32)[:, None] * frequencies[None, :]
    return jnp.concatenate([jnp.cos(angles), jnp.sin(angles)], axis=1)


def block(tokens, condition, weights, weights_down, biases):
    images = tokens.shape[0]
    tok_count = tokens.shape[1]
    modulation = low_back(mult(condition, weights[:, : 6 * D], "bd,de->be") + biases[: 6 * D])
    shift_attn = modulation[:, 0:D][:, None]
    scale_attn = modulation[:, D : 2 * D][:, None]
    gate_attn = modulation[:, 2 * D : 3 * D][:, None]
    shift_mlp = modulation[:, 3 * D : 4 * D][:, None]
    scale_mlp = modulation[:, 4 * D : 5 * D][:, None]
    gate_mlp = modulation[:, 5 * D : 6 * D][:, None]
    normed = low(normalize(tokens) * (1.0 + scale_attn) + shift_attn)
    bias_qkv = jnp.concatenate(
        [biases[6 * D : 7 * D], jnp.zeros_like(biases[:D]), biases[7 * D : 8 * D]]
    )
    project = low(low_back(mult(normed, weights[:, 6 * D : 9 * D], "btd,de->bte") + bias_qkv))
    queries = project[..., :D].reshape(images, tok_count, HEADS, HEAD_DIM)
    keys_all = project[..., D : 2 * D].reshape(images, tok_count, HEADS, HEAD_DIM)
    values_all = project[..., 2 * D :].reshape(images, tok_count, HEADS, HEAD_DIM)
    scores = low_back(mult(queries, keys_all, "bqhe,bkhe->bhqk") * HEAD_DIM ** (-0.5))
    weights_soft = low(jax.nn.softmax(scores, axis=-1))
    attended = low(low_back(mult(weights_soft, values_all, "bhqk,bkhe->bqhe"))).reshape(
        images, tok_count, D
    )
    branch = low_back(
        mult(attended, weights[:, 9 * D : 10 * D], "btd,de->bte") + biases[8 * D : 9 * D]
    )
    tokens = tokens + gate_attn * branch
    normed_mlp = low(normalize(tokens) * (1.0 + scale_mlp) + shift_mlp)
    inner = low_back(
        mult(normed_mlp, weights[:, 10 * D :], "btd,df->btf") + biases[9 * D : 9 * D + FF]
    )
    activated = low(jax.nn.gelu(inner, approximate=True))
    outward = low_back(mult(activated, weights_down, "btf,fd->btd") + biases[9 * D + FF :])
    return tokens + gate_mlp * outward


def image_loss(params, latents, tsteps, labels, noise):
    layer_in, layer_out, edge_mat, layer_bias, top_bias = params
    depth = layer_in.shape[0]
    alphas = mix_weights(tsteps)
    noisy = (
        jnp.sqrt(alphas)[:, None, None] * latents + jnp.sqrt(1.0 - alphas)[:, None, None] * noise
    )
    patches = low(patchify(noisy))
    target = patchify(noise)
    edge_low = low(edge_mat)
    start_freq = NCLS + PATCH_IN
    start_tail = start_freq + FREQ
    class_cols = edge_low[:, :NCLS]
    patch_cols = edge_low[:, NCLS:start_freq]
    freq_cols = edge_low[:, start_freq:start_tail]
    time_second = edge_low[:, start_tail : start_tail + D]
    final_cols = edge_low[:, start_tail + D : start_tail + 3 * D]
    head_cols = edge_low[:, start_tail + 3 * D :]
    tokens = (
        low_back(mult(patches, patch_cols, "btp,dp->btd") + top_bias[:D]) + position_table()[None]
    )
    features = low(time_features(tsteps))
    time_first = low_back(mult(features, freq_cols, "bf,df->bd") + top_bias[D : 2 * D])
    time_out = low_back(
        mult(low(jax.nn.silu(time_first)), time_second, "bd,de->be") + top_bias[2 * D : 3 * D]
    )
    class_emb = jnp.take(class_cols, labels, axis=1).T
    condition = low(jax.nn.silu(time_out + class_emb))
    for layer_index in range(depth):
        tokens = block(
            tokens,
            condition,
            low(layer_in[layer_index]),
            low(layer_out[layer_index]),
            layer_bias[layer_index],
        )
    closing = low_back(mult(condition, final_cols, "bd,de->be") + top_bias[3 * D : 5 * D])
    normed = low(normalize(tokens) * (1.0 + closing[:, None, D:]) + closing[:, None, :D])
    predicted = low_back(mult(normed, head_cols, "btd,dp->btp") + top_bias[5 * D :])
    misfit = predicted[..., :PATCH_IN] - target
    return jnp.sum(misfit * misfit)


def fetch_weights(layer_in, layer_out, edge_mat, again):
    gathered_in = []
    gathered_out = []
    for layer_index in range(layer_in.shape[0]):
        own_in = layer_in[layer_index].astype(jnp.bfloat16)
        own_out = layer_out[layer_index].astype(jnp.bfloat16)
        if again:
            full_in, full_out = (
                lax.all_gather(own_in, "fsdp", axis=0, tiled=True),
                lax.all_gather(own_out, "fsdp", axis=0, tiled=True),
            )
        else:
            full_in, full_out = (
                lax.all_gather(own_in, "fsdp", axis=0, tiled=True),
                lax.all_gather(own_out, "fsdp", axis=0, tiled=True),
            )
        gathered_in.append(full_in)
        gathered_out.append(full_out)
    if again:
        full_edge = lax.all_gather(edge_mat.astype(jnp.bfloat16), "fsdp", axis=0, tiled=True)
    else:
        full_edge = lax.all_gather(edge_mat.astype(jnp.bfloat16), "fsdp", axis=0, tiled=True)
    return (
        jnp.stack(gathered_in).astype(jnp.float32),
        jnp.stack(gathered_out).astype(jnp.float32),
        full_edge.astype(jnp.float32),
    )


def step_of(grad, rows_new, cols_new, rows_mean):
    second = rows_new[:, :, None] * cols_new[:, None, :] / rows_mean[:, None, None]
    return grad * lax.rsqrt(second)


def plain(weight, grad, moment):
    moment_new = decay * moment + (1.0 - decay) * (grad * grad + eps_stat)
    update = grad * lax.rsqrt(moment_new)
    root = jnp.sqrt(jnp.mean(update * update, axis=-1, keepdims=True))
    return (weight - rate * update / jnp.maximum(1.0, root / clip_level), moment_new)


def shards(
    latents,
    tsteps,
    labels,
    noise,
    layer_in,
    layer_out,
    edge_mat,
    layer_bias,
    top_bias,
    in_rows,
    in_cols,
    out_rows,
    out_cols,
    edge_rows,
    edge_cols,
    layer_bias_v,
    top_bias_v,
):
    per_micro = latents.shape[0] // MICRO
    loss_sum = jnp.zeros((), jnp.float32)
    gradients = None

    def add_grads(total_grads, grads_now):
        if total_grads is None:
            return grads_now
        return jax.tree.map(jnp.add, total_grads, grads_now)

    for micro_index in range(MICRO):
        start = micro_index * per_micro
        data_now = (
            latents[start : start + per_micro],
            tsteps[start : start + per_micro],
            labels[start : start + per_micro],
            noise[start : start + per_micro],
        )
        full_in, full_out, full_edge = fetch_weights(layer_in, layer_out, edge_mat, False)
        loss_part = image_loss((full_in, full_out, full_edge, layer_bias, top_bias), *data_now)
        loss_sum = loss_sum + loss_part
        again_in, again_out, again_edge = fetch_weights(layer_in, layer_out, edge_mat, True)
        params = (again_in, again_out, again_edge, layer_bias, top_bias)
        recomputed, pullback = jax.vjp(lambda params_now: image_loss(params_now, *data_now), params)
        (grads_now,) = pullback(jnp.ones_like(recomputed))
        gradients = add_grads(gradients, grads_now)
    grad_in_full, grad_out_full, grad_edge_full, grad_lbias, grad_tbias = gradients
    shard_in, shard_out, shard_edge = (
        lax.psum_scatter(grad_in_full, "fsdp", scatter_dimension=1, tiled=True),
        lax.psum_scatter(grad_out_full, "fsdp", scatter_dimension=1, tiled=True),
        lax.psum_scatter(grad_edge_full[None], "fsdp", scatter_dimension=1, tiled=True),
    )
    shard_in, shard_out, shard_edge = lax.psum((shard_in, shard_out, shard_edge), "rep")
    bias_in_sum, bias_top_sum, loss_total = lax.psum(
        (grad_lbias, grad_tbias, loss_sum), ("fsdp", "rep")
    )
    fsdp_count = lax.axis_size("fsdp")
    tok_total = latents.shape[0] * fsdp_count * lax.axis_size("rep") * (GRID // PATCH) ** 2
    scale_grad = 1.0 / (PATCH_IN * math.sqrt(tok_total))
    loss = loss_total / (tok_total * PATCH_IN)
    grad_in = shard_in * scale_grad
    grad_out = shard_out * scale_grad
    grad_edge = shard_edge * scale_grad
    full_rows_in = layer_in.shape[1] * fsdp_count
    full_rows_out = layer_out.shape[1] * fsdp_count
    full_rows_edge = edge_mat.shape[0] * fsdp_count
    square_in = grad_in * grad_in + eps_stat
    square_out = grad_out * grad_out + eps_stat
    square_edge = grad_edge * grad_edge + eps_stat
    rows_in_new = decay * in_rows + (1.0 - decay) * jnp.mean(square_in, axis=2)
    rows_out_new = decay * out_rows + (1.0 - decay) * jnp.mean(square_out, axis=2)
    rows_edge_new = decay * edge_rows[None] + (1.0 - decay) * jnp.mean(square_edge, axis=2)
    col_in, total_in, col_out, total_out, col_edge, total_edge = lax.psum(
        (
            jnp.sum(square_in, axis=1),
            jnp.sum(rows_in_new, axis=1),
            jnp.sum(square_out, axis=1),
            jnp.sum(rows_out_new, axis=1),
            jnp.sum(square_edge, axis=1),
            jnp.sum(rows_edge_new, axis=1),
        ),
        "fsdp",
    )
    cols_in_new = decay * in_cols + (1.0 - decay) * col_in / full_rows_in
    cols_out_new = decay * out_cols + (1.0 - decay) * col_out / full_rows_out
    cols_edge_new = decay * edge_cols[None] + (1.0 - decay) * col_edge / full_rows_edge
    update_in = step_of(grad_in, rows_in_new, cols_in_new, total_in / full_rows_in)
    update_out = step_of(grad_out, rows_out_new, cols_out_new, total_out / full_rows_out)
    update_edge = step_of(grad_edge, rows_edge_new, cols_edge_new, total_edge / full_rows_edge)
    sum_in, sum_out, sum_edge = lax.psum(
        (
            jnp.sum(update_in * update_in, axis=(1, 2)),
            jnp.sum(update_out * update_out, axis=(1, 2)),
            jnp.sum(update_edge * update_edge, axis=(1, 2)),
        ),
        "fsdp",
    )
    mean_sq_in = sum_in / (full_rows_in * grad_in.shape[2])
    mean_sq_out = sum_out / (full_rows_out * grad_out.shape[2])
    mean_sq_edge = sum_edge / (full_rows_edge * grad_edge.shape[2])
    roots_in = jnp.sqrt(mean_sq_in)
    roots_out = jnp.sqrt(mean_sq_out)
    roots_edge = jnp.sqrt(mean_sq_edge)
    factor_in = jnp.maximum(1.0, roots_in / clip_level)[:, None, None]
    factor_out = jnp.maximum(1.0, roots_out / clip_level)[:, None, None]
    factor_edge = jnp.maximum(1.0, roots_edge / clip_level)[:, None, None]
    in_new = layer_in - rate * update_in / factor_in
    out_new = layer_out - rate * update_out / factor_out
    edge_new = (edge_mat[None] - rate * update_edge / factor_edge)[0]
    clip_roots = jnp.concatenate([roots_in, roots_out, roots_edge])
    lbias_new, lbias_v_new = plain(layer_bias, bias_in_sum * scale_grad, layer_bias_v)
    tbias_new, tbias_v_new = plain(top_bias, bias_top_sum * scale_grad, top_bias_v)
    return (
        loss,
        in_new,
        out_new,
        edge_new,
        lbias_new,
        tbias_new,
        rows_in_new,
        cols_in_new,
        rows_out_new,
        cols_out_new,
        rows_edge_new[0],
        cols_edge_new[0],
        lbias_v_new,
        tbias_v_new,
        clip_roots,
    )


def solution(mesh):
    placed = (
        P(("fsdp", "rep"), None, None),
        P(("fsdp", "rep")),
        P(("fsdp", "rep")),
        P(("fsdp", "rep"), None, None),
        P(None, "fsdp", None),
        P(None, "fsdp", None),
        P("fsdp", None),
        P(),
        P(),
        P(None, "fsdp"),
        P(),
        P(None, "fsdp"),
        P(),
        P("fsdp"),
        P(),
        P(),
        P(),
    )
    return jax.shard_map(
        shards,
        mesh=mesh,
        in_specs=placed,
        out_specs=(
            P(),
            P(None, "fsdp", None),
            P(None, "fsdp", None),
            P("fsdp", None),
            P(),
            P(),
            P(None, "fsdp"),
            P(),
            P(None, "fsdp"),
            P(),
            P("fsdp"),
            P(),
            P(),
            P(),
            P(),
        ),
        check_vma=False,
    )
```

profile of v0, /device:TPU:0, one launch (start us, length us, event | category | flops | bytes accessed | tf_op | source)
XLA Modules:
  0.0 1379.9 jit_solution(4260965202607381053)
XLA Ops:
  37.0 17.1 %all-gather.18.cloned.1.call-done = bf16[1,1536,384]{2,1,0:T(8,128)(2,1)} async-done(((bf16[1,192,384]{2,1,0:T(8,128)(2,1)}), bf16[1,1536,384]{2,1,0:T(8,128)(2,1)}) %all-gather.18.cloned.1.call-update) | async-done | bytes 1179664 | tf_op jit(solution)/shard_map/all_gather | solution.py:207
  54.1 42.0 %all-gather.14.cloned.1.call-done = bf16[1,1536,384]{2,1,0:T(8,128)(2,1)} async-done(((bf16[1,192,384]{2,1,0:T(8,128)(2,1)}), bf16[1,1536,384]{2,1,0:T(8,128)(2,1)}) %all-gather.14.cloned.1.call-update) | async-done | bytes 1179664 | tf_op jit(solution)/shard_map/all_gather | solution.py:207
  96.1 48.7 %all-gather.10.cloned.1.call-done = bf16[384,2457]{1,0:T(8,128)(2,1)} async-done(((bf16[48,2457]{1,0:T(8,128)(2,1)}), bf16[384,2457]{1,0:T(8,128)(2,1)}) %all-gather.10.cloned.1.call-update) | async-done | bytes 1886992 | tf_op jit(solution)/shard_map/all_gather | solution.py:214
  166.5 51.5 %all-gather.12.cloned.1.call-done = bf16[1,384,5376]{2,1,0:T(8,128)(2,1)} async-done(((bf16[1,48,5376]{2,1,0:T(8,128)(2,1)}), bf16[1,384,5376]{2,1,0:T(8,128)(2,1)}) %all-gather.12.cloned.1.call-update) | async-done | bytes 4128784 | tf_op jit(solution)/shard_map/all_gather | solution.py:206
  223.5 67.7 %all-gather.16.cloned.1.call-done = bf16[1,384,5376]{2,1,0:T(8,128)(2,1)} async-done(((bf16[1,48,5376]{2,1,0:T(8,128)(2,1)}), bf16[1,384,5376]{2,1,0:T(8,128)(2,1)}) %all-gather.16.cloned.1.call-update) | async-done | bytes 4128784 | tf_op jit(solution)/shard_map/all_gather | solution.py:206
  340.5 4.7 multiply_convert_fusion.9
  355.6 5.1 fusion.389
  376.2 4.6 multiply_convert_fusion.7
  389.5 4.7 fusion.386
  402.8 4.8 multiply_convert_fusion.11
  417.7 4.7 fusion.392
  522.0 3.7 multiply_reduce_fusion.35
  687.2 6.5 add_bitcast_fusion.6
  693.7 9.1 copy.871
  764.8 5.1 add_bitcast_fusion
  769.8 12.6 add_bitcast_fusion.4
  782.4 11.1 add_bitcast_fusion.1
  793.6 20.9 %add_add_fusion = f32[2,384,5376]{2,1,0:T(8,128)} fusion(f32[1,384,5376]{2,1,0:T(8,128)} %add_bitcast_fusion, f32[1,384,5376]{2,1,0:T(8,128)} %get-tuple-element.452, f32[1,384,5376]{2,1,0:T(8,128)S(1)} %add_bitcast_fusion.2, f32[1,384,5376]{2,1,0:T(8,128)} %get-tuple-element.453, f32[1,384,5376]{2,1,0:T(8,128)} %get-tuple-element.454, ...), kind=kLoop, calls=%fused_computation.15 | loop fusion | flops 20643840 | bytes 66060288 | tf_op jit(solution)/shard_map/add | solution.py:260
  830.7 40.9 %all-reduce.176 = (f32[]{:T(128)}, f32[2,5376]{1,0:T(2,128)S(1)}, f32[1952]{0:T(1024)S(1)}) all-reduce(f32[]{:T(128)S(6)} %add.2146, f32[2,5376]{1,0:T(2,128)S(1)} %add_add_fusion.26, f32[1952]{0:T(1024)S(1)} %add_add_fusion.27), channel_id=1, replica_groups=mesh['fsdp'=8,'rep'=4] {'fsdp','rep'}, use_global_device_ids=true, to_apply=%region_50.52 | all-reduce | flops 12705 | bytes 101640 | tf_op jit(solution)/shard_map/psum | solution.py:285
  876.4 73.3 %reduce-scatter.5.cloned.1.call-done = f32[2,192,384]{2,1,0:T(8,128)} async-done(((f32[2,1536,384]{2,1,0:T(8,128)}), f32[2,192,384]{2,1,0:T(8,128)}) %reduce-scatter.5.cloned.1.call-update) | async-done | bytes 589840 | tf_op jit(solution)/shard_map/reduce_scatter | solution.py:281
  949.6 279.4 %reduce-scatter.3.cloned.1.call-done = f32[2,48,5376]{2,1,0:T(8,128)} async-done(((f32[2,384,5376]{2,1,0:T(8,128)}), f32[2,48,5376]{2,1,0:T(8,128)}) %reduce-scatter.3.cloned.1.call-update) | async-done | bytes 2064400 | tf_op jit(solution)/shard_map/reduce_scatter | solution.py:280
  1229.9 69.9 %all-reduce.185.cloned.1.call-done = (f32[2,48,5376]{2,1,0:T(8,128)}, f32[2,192,384]{2,1,0:T(8,128)}, f32[1,48,2457]{2,1,0:T(8,128)}) async-done(((f32[2,48,5376]{2,1,0:T(8,128)}, f32[2,192,384]{2,1,0:T(8,128)}, f32[1,48,2457]{2,1,0:T(8,128)}), (f32[2,48,5376]{2,1,0:T(8,128)}, f32[2,192,384]{2,1,0:T(8,128)}, f32[1,48,2457]{2,1,0:T(8,128)})) %all-reduce.185.cloned.1.call-update) | async-done | bytes 3125968 | tf_op jit(solution)/shard_map/psum | solution.py:284
  1305.7 37.6 %all-reduce.178 = (f32[2]{0:T(128)S(1)}, f32[2,5376]{1,0:T(2,128)S(1)}, f32[2]{0:T(128)S(1)}, f32[2,384]{1,0:T(2,128)S(1)}, f32[1]{0:T(128)}, /*index=5*/f32[1,2457]{1,0:T(1,128)S(1)}) all-reduce(f32[2]{0:T(128)S(1)} %get-tuple-element.165, f32[2,5376]{1,0:T(2,128)S(1)} %get-tuple-element.73, ...), channel_id=1, replica_groups=mesh['fsdp'=8,'rep'=4] {'fsdp'}, use_global_device_ids=true, to_apply=%region_159.162 | all-reduce | flops 13982 | bytes 111856 | tf_op jit(solution)/shard_map/psum | solution.py:304
  1346.0 17.8 %all-reduce.177 = (f32[2]{0:T(128)S(1)}, f32[2]{0:T(128)S(1)}, f32[1]{0:T(128)}) all-reduce(f32[2]{0:T(128)S(1)} %multiply_reduce_fusion.12, f32[2]{0:T(128)S(1)} %multiply_reduce_fusion.70, f32[1]{0:T(128)} %bitcast.206), channel_id=1, replica_groups=mesh['fsdp'=8,'rep'=4] {'fsdp'}, use_global_device_ids=true, to_apply=%region_161.164 | all-reduce | flops 5 | bytes 40 | tf_op jit(solution)/shard_map/psum | solution.py:321
  (1767 shorter events, 508.6 us)
Async XLA Ops:
  7.2 46.9 %all-gather.18.cloned.1.call-start = ((), (), s32[]{:S(2)}) async-start(), calls=%async_computation.8 | async-start | bytes 1327104 | tf_op jit(solution)/shard_map/all_gather | solution.py:207
  9.3 86.8 %all-gather.14.cloned.1.call-start = ((), (), s32[]{:S(2)}) async-start(), calls=%async_computation.6 | async-start | bytes 1327104 | tf_op jit(solution)/shard_map/all_gather | solution.py:207
  10.0 134.8 %all-gather.10.cloned.1.call-start = ((), (), s32[]{:S(2)}) async-start(), calls=%async_computation.2 | async-start | bytes 2211840 | tf_op jit(solution)/shard_map/all_gather | solution.py:214
  11.9 206.1 %all-gather.12.cloned.1.call-start = ((), (), s32[]{:S(2)}) async-start(), calls=%async_computation.5 | async-start | bytes 4644864 | tf_op jit(solution)/shard_map/all_gather | solution.py:206
  13.1 278.0 %all-gather.16.cloned.1.call-start = ((), (), s32[]{:S(2)}) async-start(), calls=%async_computation.7 | async-start | bytes 4644864 | tf_op jit(solution)/shard_map/all_gather | solution.py:206
  13.7 860.7 %all-reduce.183.cloned.1.call-start = ((), (), s32[]{:S(2)}) async-start(), calls=%async_computation.9 | async-start | bytes 7864320
  17.3 132.3 %copy-start.553 = (bf16[2,256]{1,0:T(2,128)(2,1)}, bf16[2,256]{1,0:T(2,128)(2,1)S(1)}, u32[]{:S(2)}) copy-start(bf16[2,256]{1,0:T(2,128)(2,1)S(1)} %pad_maximum_fusion.3) | copy-start | bytes 3076
  17.3 128.6 %copy-start.555 = (bf16[2,256]{1,0:T(2,128)(2,1)}, bf16[2,256]{1,0:T(2,128)(2,1)S(1)}, u32[]{:S(2)}) copy-start(bf16[2,256]{1,0:T(2,128)(2,1)S(1)} %pad_maximum_fusion.4) | copy-start | bytes 3076
  17.3 130.4 %copy-start.557 = (bf16[2,256]{1,0:T(2,128)(2,1)}, bf16[2,256]{1,0:T(2,128)(2,1)S(1)}, u32[]{:S(2)}) copy-start(bf16[2,256]{1,0:T(2,128)(2,1)S(1)} %pad_maximum_fusion.5) | copy-start | bytes 3076
  160.5 140.3 %copy-start.12 = (f32[2,256,384]{2,1,0:T(8,128)}, f32[2,256,384]{2,1,0:T(8,128)S(1)}, u32[]{:S(2)}) copy-start(f32[2,256,384]{2,1,0:T(8,128)S(1)} %get-tuple-element.368) | copy-start | bytes 2359300
  160.5 140.3 %copy-start.326 = (f32[2,256]{1,0:T(2,128)}, f32[2,256]{1,0:T(2,128)S(1)}, u32[]{:S(2)}) copy-start(f32[2,256]{1,0:T(2,128)S(1)} %broadcast_multiply_fusion.10) | copy-start | bytes 6148
  162.0 138.6 %copy-start.15 = (f32[2,256,384]{2,1,0:T(8,128)}, f32[2,256,384]{2,1,0:T(8,128)S(1)}, u32[]{:S(2)}) copy-start(f32[2,256,384]{2,1,0:T(8,128)S(1)} %get-tuple-element.351) | copy-start | bytes 2359300
  162.0 138.6 %copy-start.328 = (f32[2,256]{1,0:T(2,128)}, f32[2,256]{1,0:T(2,128)S(1)}, u32[]{:S(2)}) copy-start(f32[2,256]{1,0:T(2,128)S(1)} %broadcast_multiply_fusion.5) | copy-start | bytes 6148
  162.8 137.6 %copy-start.9 = (f32[2,256,384]{2,1,0:T(8,128)}, f32[2,256,384]{2,1,0:T(8,128)S(1)}, u32[]{:S(2)}) copy-start(f32[2,256,384]{2,1,0:T(8,128)S(1)} %get-tuple-element.385) | copy-start | bytes 2359300
  162.8 137.6 %copy-start.324 = (f32[2,256]{1,0:T(2,128)}, f32[2,256]{1,0:T(2,128)S(1)}, u32[]{:S(2)}) copy-start(f32[2,256]{1,0:T(2,128)S(1)} %broadcast_multiply_fusion.15) | copy-start | bytes 6148
  163.1 137.8 %copy-start.425 = (f32[2,256]{1,0:T(2,128)}, f32[2,256]{1,0:T(2,128)S(1)}, u32[]{:S(2)}) copy-start(f32[2,256]{1,0:T(2,128)S(1)} %fusion.287) | copy-start | bytes 6148
  163.6 137.0 %copy-start.427 = (f32[2,256]{1,0:T(2,128)}, f32[2,256]{1,0:T(2,128)S(1)}, u32[]{:S(2)}) copy-start(f32[2,256]{1,0:T(2,128)S(1)} %fusion.292) | copy-start | bytes 6148
  163.6 136.7 %copy-start.423 = (f32[2,256]{1,0:T(2,128)}, f32[2,256]{1,0:T(2,128)S(1)}, u32[]{:S(2)}) copy-start(f32[2,256]{1,0:T(2,128)S(1)} %fusion.282) | copy-start | bytes 6148
  702.9 246.8 %reduce-scatter.5.cloned.1.call-start = ((), (), s32[]{:S(2)}) async-start(), calls=%async_computation.4 | async-start | bytes 5308416 | tf_op jit(solution)/shard_map/reduce_scatter | solution.py:281
  729.2 499.9 %reduce-scatter.3.cloned.1.call-start = ((), (), s32[]{:S(2)}) async-start(), calls=%async_computation.3 | async-start | bytes 18579456 | tf_op jit(solution)/shard_map/reduce_scatter | solution.py:280
  814.5 485.3 %all-reduce.185.cloned.1.call-start = ((), (), s32[]{:S(2)}) async-start(), calls=%async_computation.10 | async-start | bytes 6291456 | tf_op jit(solution)/shard_map/psum | solution.py:284
  829.8 399.4 %copy-start.263 = (f32[2,5376]{1,0:T(2,128)S(1)}, f32[2,5376]{1,0:T(2,128)}, u32[]{:S(2)}) copy-start(f32[2,5376]{1,0:T(2,128)} %param.28) | copy-start | bytes 129028
  872.3 430.2 %copy-start.422 = (f32[1952]{0:T(1024)}, f32[1952]{0:T(1024)S(1)}, u32[]{:S(2)}) copy-start(f32[1952]{0:T(1024)S(1)} %get-tuple-element.158) | copy-start | bytes 23428
  874.4 428.1 %copy-start.264 = (f32[2,5376]{1,0:T(2,128)}, f32[2,5376]{1,0:T(2,128)S(1)}, u32[]{:S(2)}) copy-start(f32[2,5376]{1,0:T(2,128)S(1)} %get-tuple-element.160) | copy-start | bytes 129028
  (581 other events, 3426.9 us)
Sparse Core Ops, SparseCore 0:
  10.2 43.8 all-gather.17
  56.2 39.7 all-gather.13
  98.3 46.4 all-gather.9
  147.4 70.5 all-gather.11
  220.6 70.4 all-gather.15
  703.0 148.1 all-reduce.182
  854.8 94.7 reduce-scatter.4
  953.6 275.4 reduce-scatter.2
  1232.2 67.5 all-reduce.184
where the time goes:
time: 1390 us; the launch traced here: 1380 us
  waiting for transfers between devices  651 us (47%)
  matrix products  307 us (22%)
  other arithmetic  171 us (12%)
  local copies, waits for them, and re-layouts  127 us (9%)
  blocking collectives  96.2 us (7%)
  between operations  27.7 us (2%)
    dot_general x159, matrix products, mult(): return jnp.einsum(form, left, right, preferred_element_type=jnp.float32)  285 us
    reduce_scatter x1, waiting for transfers between devices, shards(): lax.psum_scatter(grad_in_full, 'fsdp', scatter_dimension=1, tiled=True)  279 us
    all_gather x2, waiting for transfers between devices, fetch_weights(): lax.all_gather(own_in, 'fsdp', axis=0, tiled=True)  119 us
    reduce_scatter x1, waiting for transfers between devices, shards(): lax.psum_scatter(grad_out_full, 'fsdp', scatter_dimension=1, tiled=True)  73.3 us
    psum x1, waiting for transfers between devices, shards(): lax.psum((shard_in, shard_out, shard_edge), 'rep')  69.9 us
    all_gather x2, waiting for transfers between devices, fetch_weights(): lax.all_gather(own_out, 'fsdp', axis=0, tiled=True)  59.1 us
    all_gather x1, waiting for transfers between devices, fetch_weights(): lax.all_gather(edge_mat.astype(jnp.bfloat16), 'fsdp', axis=0, tiled=True)  48.7 us
    psum x1, blocking collectives, shards(): lax.psum((grad_lbias, grad_tbias, loss_sum), ('fsdp', 'rep'))  40.9 us
  transfers between devices with their start and end apart: 9, of which 8 were waited for; matrix products, arithmetic and copies ran while one was open for 13% of the time, Pallas kernels for 0%

commit v1 on v0

--- a/solution.py
+++ b/solution.py
@@ -15,7 +15,7 @@
 TSTEPS = 1000
 NCLS = 1001
 FREQ = 256
-MICRO = 3
+MICRO = 1
 PATCH_IN = 16
 
 
@@ -267,13 +267,11 @@
             labels[start : start + per_micro],
             noise[start : start + per_micro],
         )
-        full_in, full_out, full_edge = fetch_weights(layer_in, layer_out, edge_mat, False)
-        loss_part = image_loss((full_in, full_out, full_edge, layer_bias, top_bias), *data_now)
-        loss_sum = loss_sum + loss_part
         again_in, again_out, again_edge = fetch_weights(layer_in, layer_out, edge_mat, True)
         params = (again_in, again_out, again_edge, layer_bias, top_bias)
         recomputed, pullback = jax.vjp(lambda params_now: image_loss(params_now, *data_now), params)
         (grads_now,) = pullback(jnp.ones_like(recomputed))
+        loss_sum = loss_sum + recomputed
         gradients = add_grads(gradients, grads_now)
     grad_in_full, grad_out_full, grad_edge_full, grad_lbias, grad_tbias = gradients
     shard_in, shard_out, shard_edge = (

time: 1390 us -> 1210 us (0.87)
  matrix products: 307 us -> 180 us
  other arithmetic: 171 us -> 128 us
  local copies, waits for them, and re-layouts: 127 us -> 84.3 us
  waiting for transfers between devices: 651 us -> 690 us
    dot_general x159 -> x53, matrix products: 285 us -> 163 us  [mult(): return jnp.einsum(form, left, right, preferred_element_type=jnp.float32)]
    unnamed x10, waiting for transfers between devices: 1.37 us -> 55.1 us
    all_gather x2, waiting for transfers between devices: 119 us -> 78.5 us  [fetch_weights(): lax.all_gather(own_in, 'fsdp', axis=0, tiled=True)]
    broadcast_in_dim x4 -> x2, other arithmetic: 32.2 us -> 3.61 us  [image_loss(): layer_in[layer_index]]
    add x4 -> x0, other arithmetic: 23.8 us -> none  [add_grads(): return jax.tree.map(jnp.add, total_grads, grads_now)]
    reduce_scatter x1, waiting for transfers between devices: 73.3 us -> 96.4 us  [shards(): lax.psum_scatter(grad_out_full, 'fsdp', scatter_dimension=1, tiled=True)]
    convert_element_type x33 -> x11, other arithmetic: 13 us -> 31.6 us  [low_back(): return rounders()[1](values)]
    unnamed x1187 -> x398, local copies, waits for them, and re-layouts: 31.5 us -> 18.7 us
  transfers between devices with their start and end apart: 9 -> 9, of which waited for: 8 -> 9; matrix products, arithmetic and copies ran while one was open for 13% -> 11% of each run, Pallas kernels for 0% -> 0%
where the time goes in v1:
time: 1210 us; the launch traced here: 1200 us
  waiting for transfers between devices  690 us (57%)
  matrix products  180 us (15%)
  other arithmetic  128 us (11%)
  blocking collectives  95.8 us (8%)
  local copies, waits for them, and re-layouts  84.3 us (7%)
  between operations  21.5 us (2%)
    reduce_scatter x1, waiting for transfers between devices, shards(): lax.psum_scatter(grad_in_full, 'fsdp', scatter_dimension=1, tiled=True)  279 us
    dot_general x53, matrix products, mult(): return jnp.einsum(form, left, right, preferred_element_type=jnp.float32)  163 us
    reduce_scatter x1, waiting for transfers between devices, shards(): lax.psum_scatter(grad_out_full, 'fsdp', scatter_dimension=1, tiled=True)  96.4 us
    all_gather x2, waiting for transfers between devices, fetch_weights(): lax.all_gather(own_in, 'fsdp', axis=0, tiled=True)  78.5 us
    psum x1, waiting for transfers between devices, shards(): lax.psum((shard_in, shard_out, shard_edge), 'rep')  69.8 us
    all_gather x2, waiting for transfers between devices, fetch_weights(): lax.all_gather(own_out, 'fsdp', axis=0, tiled=True)  61.8 us
    unnamed x10, waiting for transfers between devices  55.1 us
    all_gather x1, waiting for transfers between devices, fetch_weights(): lax.all_gather(edge_mat.astype(jnp.bfloat16), 'fsdp', axis=0, tiled=True)  49.2 us
  transfers between devices with their start and end apart: 9, of which 9 were waited for; matrix products, arithmetic and copies ran while one was open for 11% of the time, Pallas kernels for 0%

profile of v1, /device:TPU:0, one launch (start us, length us, event | category | flops | bytes accessed | tf_op | source)
XLA Modules:
  0.0 1200.6 jit_solution(1120847443775627572)
XLA Ops:
  34.2 19.8 %all-gather.14.cloned.1.call-done = bf16[1,1536,384]{2,1,0:T(8,128)(2,1)} async-done(((bf16[1,192,384]{2,1,0:T(8,128)(2,1)}), bf16[1,1536,384]{2,1,0:T(8,128)(2,1)}) %all-gather.14.cloned.1.call-update) | async-done | bytes 1179664 | tf_op jit(solution)/shard_map/all_gather | solution.py:202
  54.1 42.0 %all-gather.18.cloned.1.call-done = bf16[1,1536,384]{2,1,0:T(8,128)(2,1)} async-done(((bf16[1,192,384]{2,1,0:T(8,128)(2,1)}), bf16[1,1536,384]{2,1,0:T(8,128)(2,1)}) %all-gather.18.cloned.1.call-update) | async-done | bytes 1179664 | tf_op jit(solution)/shard_map/all_gather | solution.py:202
  96.1 49.2 %all-gather.10.cloned.1.call-done = bf16[384,2457]{1,0:T(8,128)(2,1)} async-done(((bf16[48,2457]{1,0:T(8,128)(2,1)}), bf16[384,2457]{1,0:T(8,128)(2,1)}) %all-gather.10.cloned.1.call-update) | async-done | bytes 1886992 | tf_op jit(solution)/shard_map/all_gather | solution.py:212
  158.5 59.5 %all-gather.12.cloned.1.call-done = bf16[1,384,5376]{2,1,0:T(8,128)(2,1)} async-done(((bf16[1,48,5376]{2,1,0:T(8,128)(2,1)}), bf16[1,384,5376]{2,1,0:T(8,128)(2,1)}) %all-gather.12.cloned.1.call-update) | async-done | bytes 4128784 | tf_op jit(solution)/shard_map/all_gather | solution.py:201
  232.1 8.5 fusion.151
  240.6 7.0 divide_convert_fusion.1
  258.8 8.6 multiply_convert_fusion.3
  272.1 19.0 %all-gather.16.cloned.1.call-done = bf16[1,384,5376]{2,1,0:T(8,128)(2,1)} async-done(((bf16[1,48,5376]{2,1,0:T(8,128)(2,1)}), bf16[1,384,5376]{2,1,0:T(8,128)(2,1)}) %all-gather.16.cloned.1.call-update) | async-done | bytes 4128784 | tf_op jit(solution)/shard_map/all_gather | solution.py:201
  304.3 8.6 fusion.152
  312.9 7.1 divide_convert_fusion
  344.0 7.7 fusion.15
  371.7 9.0 multiply_reduce_fusion.1
  381.4 11.2 multiply_convert_fusion.1
  424.3 7.6 fusion.8
  452.9 9.0 multiply_reduce_fusion
  462.5 11.1 multiply_convert_fusion
  514.9 9.0 copy.265
  575.6 40.4 %all-reduce.60 = (f32[]{:T(128)}, f32[2,5376]{1,0:T(2,128)S(1)}, f32[1952]{0:T(1024)S(1)}) all-reduce(f32[]{:T(128)} %get-tuple-element.145, f32[2,5376]{1,0:T(2,128)S(1)} %pad_add_fusion.2, f32[1952]{0:T(1024)S(1)} %pad_add_fusion.5), channel_id=1, replica_groups=mesh['fsdp'=8,'rep'=4] {'fsdp','rep'}, use_global_device_ids=true, to_apply=%region_18.19 | all-reduce | flops 12705 | bytes 101640 | tf_op jit(solution)/shard_map/psum | solution.py:283
  618.9 53.7 %all-reduce.67.cloned.1.call-done = f32[1,384,2457]{2,0,1:T(1,128)} async-done(((f32[1,384,2457]{2,0,1:T(1,128)}), f32[1,384,2457]{2,0,1:T(1,128)}) %all-reduce.67.cloned.1.call-update) | async-done | bytes 3773968
  674.5 96.4 %reduce-scatter.5.cloned.1.call-done = f32[2,192,384]{2,1,0:T(8,128)} async-done(((f32[2,1536,384]{2,1,0:T(8,128)}), f32[2,192,384]{2,1,0:T(8,128)}) %reduce-scatter.5.cloned.1.call-update) | async-done | bytes 589840 | tf_op jit(solution)/shard_map/reduce_scatter | solution.py:279
  770.9 279.4 %reduce-scatter.3.cloned.1.call-done = f32[2,48,5376]{2,1,0:T(8,128)} async-done(((f32[2,384,5376]{2,1,0:T(8,128)}), f32[2,48,5376]{2,1,0:T(8,128)}) %reduce-scatter.3.cloned.1.call-update) | async-done | bytes 2064400 | tf_op jit(solution)/shard_map/reduce_scatter | solution.py:278
  1051.2 69.8 %all-reduce.69.cloned.1.call-done = (f32[2,48,5376]{2,1,0:T(8,128)}, f32[2,192,384]{2,1,0:T(8,128)}, f32[1,48,2457]{2,1,0:T(8,128)}) async-done(((f32[2,48,5376]{2,1,0:T(8,128)}, f32[2,192,384]{2,1,0:T(8,128)}, f32[1,48,2457]{2,1,0:T(8,128)}), (f32[2,48,5376]{2,1,0:T(8,128)}, f32[2,192,384]{2,1,0:T(8,128)}, f32[1,48,2457]{2,1,0:T(8,128)})) %all-reduce.69.cloned.1.call-update) | async-done | bytes 3125968 | tf_op jit(solution)/shard_map/psum | solution.py:282
  1126.9 37.6 %all-reduce.62 = (f32[2]{0:T(128)S(1)}, f32[2,5376]{1,0:T(2,128)S(1)}, f32[2]{0:T(128)S(1)}, f32[2,384]{1,0:T(2,128)S(1)}, f32[1]{0:T(128)}, /*index=5*/f32[1,2457]{1,0:T(1,128)S(1)}) all-reduce(f32[2]{0:T(128)S(1)} %get-tuple-element.116, f32[2,5376]{1,0:T(2,128)S(1)} %get-tuple-element.75, ...), channel_id=1, replica_groups=mesh['fsdp'=8,'rep'=4] {'fsdp'}, use_global_device_ids=true, to_apply=%region_47.48 | all-reduce | flops 13982 | bytes 111856 | tf_op jit(solution)/shard_map/psum | solution.py:302
  1167.2 17.8 %all-reduce.61 = (f32[2]{0:T(128)S(1)}, f32[2]{0:T(128)S(1)}, f32[1]{0:T(128)}) all-reduce(f32[2]{0:T(128)S(1)} %multiply_reduce_fusion.23, f32[2]{0:T(128)S(1)} %multiply_reduce_fusion.24, f32[1]{0:T(128)} %bitcast.67), channel_id=1, replica_groups=mesh['fsdp'=8,'rep'=4] {'fsdp'}, use_global_device_ids=true, to_apply=%region_49.50 | all-reduce | flops 5 | bytes 40 | tf_op jit(solution)/shard_map/psum | solution.py:319
  (648 shorter events, 289.9 us)
Async XLA Ops:
  7.2 46.9 %all-gather.14.cloned.1.call-start = ((), (), s32[]{:S(2)}) async-start(), calls=%async_computation.6 | async-start | bytes 1327104 | tf_op jit(solution)/shard_map/all_gather | solution.py:202
  9.2 86.8 %all-gather.18.cloned.1.call-start = ((), (), s32[]{:S(2)}) async-start(), calls=%async_computation.8 | async-start | bytes 1327104 | tf_op jit(solution)/shard_map/all_gather | solution.py:202
  10.0 135.3 %all-gather.10.cloned.1.call-start = ((), (), s32[]{:S(2)}) async-start(), calls=%async_computation.2 | async-start | bytes 2211840 | tf_op jit(solution)/shard_map/all_gather | solution.py:212
  11.8 206.1 %all-gather.12.cloned.1.call-start = ((), (), s32[]{:S(2)}) async-start(), calls=%async_computation.5 | async-start | bytes 4644864 | tf_op jit(solution)/shard_map/all_gather | solution.py:201
  13.1 278.0 %all-gather.16.cloned.1.call-start = ((), (), s32[]{:S(2)}) async-start(), calls=%async_computation.7 | async-start | bytes 4644864 | tf_op jit(solution)/shard_map/all_gather | solution.py:201
  13.7 658.9 %all-reduce.67.cloned.1.call-start = ((), (), s32[]{:S(2)}) async-start(), calls=%async_computation.9 | async-start | bytes 7864320
  18.9 128.2 %copy-start.105 = (f32[384]{0:T(512)}, f32[384]{0:T(512)S(1)}, u32[]{:S(2)}) copy-start(f32[384]{0:T(512)S(1)} %get-tuple-element.162) | copy-start | bytes 4612
  33.5 220.2 %copy-start.13 = (f32[256,384]{1,0:T(8,128)}, f32[256,384]{1,0:T(8,128)S(1)}, u32[]{:S(2)}) copy-start(f32[256,384]{1,0:T(8,128)S(1)} %pad_maximum_fusion) | copy-start | bytes 1179652
  147.1 106.6 %copy-start = (f32[6,256,384]{2,1,0:T(8,128)}, f32[6,256,384]{2,1,0:T(8,128)S(1)}, u32[]{:S(2)}) copy-start(f32[6,256,384]{2,1,0:T(8,128)S(1)} %get-tuple-element.186) | copy-start | bytes 7077892
  147.1 72.8 %copy-start.77 = (f32[6,256]{1,0:T(8,128)}, f32[6,256]{1,0:T(8,128)S(1)}, u32[]{:S(2)}) copy-start(f32[6,256]{1,0:T(8,128)S(1)} %broadcast_multiply_fusion.5) | copy-start | bytes 18436
  156.4 134.7 %copy-start.75 = (bf16[6,384]{1,0:T(8,128)(2,1)}, bf16[6,384]{1,0:T(8,128)(2,1)S(1)}, u32[]{:S(2)}) copy-start(bf16[6,384]{1,0:T(8,128)(2,1)S(1)} %get-tuple-element.183) | copy-start | bytes 13828
  441.3 98.8 %copy-start.24 = (bf16[6,256,384]{2,1,0:T(8,128)(2,1)}, bf16[6,256,384]{2,1,0:T(8,128)(2,1)S(1)}, u32[]{:S(2)}) copy-start(bf16[6,256,384]{2,1,0:T(8,128)(2,1)S(1)} %multiply_convert_fusion.4) | copy-start | bytes 3538948
  523.9 247.0 %reduce-scatter.5.cloned.1.call-start = ((), (), s32[]{:S(2)}) async-start(), calls=%async_computation.4 | async-start | bytes 5308416 | tf_op jit(solution)/shard_map/reduce_scatter | solution.py:279
  536.8 513.6 %reduce-scatter.3.cloned.1.call-start = ((), (), s32[]{:S(2)}) async-start(), calls=%async_computation.3 | async-start | bytes 18579456 | tf_op jit(solution)/shard_map/reduce_scatter | solution.py:278
  563.6 557.4 %all-reduce.69.cloned.1.call-start = ((), (), s32[]{:S(2)}) async-start(), calls=%async_computation.10 | async-start | bytes 6291456 | tf_op jit(solution)/shard_map/psum | solution.py:282
  616.7 433.7 %copy-start.143 = (f32[1952]{0:T(1024)}, f32[1952]{0:T(1024)S(1)}, u32[]{:S(2)}) copy-start(f32[1952]{0:T(1024)S(1)} %get-tuple-element.109) | copy-start | bytes 23428
  618.8 431.6 %copy-start.94 = (f32[2,5376]{1,0:T(2,128)}, f32[2,5376]{1,0:T(2,128)S(1)}, u32[]{:S(2)}) copy-start(f32[2,5376]{1,0:T(2,128)S(1)} %get-tuple-element.111) | copy-start | bytes 129028
  618.9 431.6 %copy-start.93 = (f32[2,5376]{1,0:T(2,128)S(1)}, f32[2,5376]{1,0:T(2,128)}, u32[]{:S(2)}) copy-start(f32[2,5376]{1,0:T(2,128)} %param.24) | copy-start | bytes 129028
  1050.4 75.6 %copy-start.174 = (f32[2,48]{1,0:T(2,128)S(1)}, f32[2,48]{1,0:T(2,128)}, u32[]{:S(2)}) copy-start(f32[2,48]{1,0:T(2,128)} %param.26) | copy-start | bytes 1156
  1050.4 75.8 %copy-start.178 = (f32[48]{0:T(128)S(1)}, f32[48]{0:T(128)}, u32[]{:S(2)}) copy-start(f32[48]{0:T(128)} %param.30) | copy-start | bytes 580
  1050.4 76.4 %copy-start.171 = (f32[2,192]{1,0:T(2,128)S(1)}, f32[2,192]{1,0:T(2,128)}, u32[]{:S(2)}) copy-start(f32[2,192]{1,0:T(2,128)} %param.28) | copy-start | bytes 4612
  1050.4 114.1 %copy-start.124 = (f32[2457]{0:T(1024)S(1)}, f32[2457]{0:T(1024)}, u32[]{:S(2)}) copy-start(f32[2457]{0:T(1024)} %broadcast_multiply_fusion) | copy-start | bytes 29488
  1050.4 114.8 %copy-start.170 = (f32[2,384]{1,0:T(2,128)S(1)}, f32[2,384]{1,0:T(2,128)}, u32[]{:S(2)}) copy-start(f32[2,384]{1,0:T(2,128)} %param.29) | copy-start | bytes 9220
  1050.4 114.8 %copy-start.138 = (f32[2,5376]{1,0:T(2,128)S(1)}, f32[2,5376]{1,0:T(2,128)}, u32[]{:S(2)}) copy-start(f32[2,5376]{1,0:T(2,128)} %param.27) | copy-start | bytes 129028
  (185 other events, 1545.4 us)
Sparse Core Ops, SparseCore 0:
  10.2 43.8 all-gather.13
  56.2 39.7 all-gather.17
  98.8 46.4 all-gather.9
  147.4 70.5 all-gather.11
  220.6 70.4 all-gather.15
  524.0 148.5 all-reduce.66
  676.2 94.6 reduce-scatter.4
  774.9 275.3 reduce-scatter.2
  1053.4 67.5 all-reduce.68

commit v2 on v1

v2 whole, which is shorter than its diff:
```python
import functools
import math

import jax
import jax.numpy as jnp
from jax import lax
from jax.experimental import pallas as pl
from jax.experimental.pallas import tpu as pltpu
from jax.sharding import PartitionSpec as P

NCLS = 1001
FREQ = 256
CHANNELS = 4
PATCH = 2
GRID = 32
TSTEPS = 1000
eps_stat = 1e-30
decay = 0.5
rate = 0.01
clip_level = 1.0
D = 384
HEADS = 6
HEAD_DIM = 64
FF = 1536
TOK = 256
PATCH_IN = 16
eps_norm = 1e-06
F32 = jnp.float32
BF16 = jnp.bfloat16
GELU_A = 0.7978845608028654
GELU_B = 0.044715
NT = (((1,), (1,)), ((), ()))
TN = (((0,), (0,)), ((), ()))
FFC = 512
OWN = 48


def dot(a, b, dims=(((1,), (0,)), ((), ()))):
    return lax.dot_general(a, b, dims, preferred_element_type=F32)


def norm_rows(t):
    center = t - jnp.mean(t, axis=-1, keepdims=True)
    spread = jnp.mean(center * center, axis=-1, keepdims=True)
    scale = lax.rsqrt(spread + eps_norm)
    return center * scale, scale


def norm_back(dn, n, scale):
    mean_d = jnp.mean(dn, axis=-1, keepdims=True)
    mean_dn = jnp.mean(dn * n, axis=-1, keepdims=True)
    return scale * (dn - mean_d - n * mean_dn)


def rows_sum(v):
    return jnp.sum(v, axis=0, keepdims=True)


def soft_rows(s):
    e = jnp.exp(s - jnp.max(s, axis=-1, keepdims=True))
    return e / jnp.sum(e, axis=-1, keepdims=True)


def gelu_parts(x):
    t = jnp.tanh(GELU_A * (x + GELU_B * (x * x * x)))
    return t


QKV = 0
WO = 3 * D
WF1 = 4 * D
BQ, BV, BO, BF1, BF2 = 0, D, 2 * D, 3 * D, 3 * D + FF
BW = 4 * D + FF


def compute_kernel(
    images,
    group,
    blocked,
    patches_ref,
    target_ref,
    pos_ref,
    mods_ref,
    w_in_ref,
    w_out_ref,
    w_patch_ref,
    w_head_ref,
    bias_ref,
    bpatch_ref,
    bhead_ref,
    g_in_ref,
    g_out_ref,
    g_patch_ref,
    g_head_ref,
    g_bias_ref,
    g_bpatch_ref,
    g_bhead_ref,
    g_mods_ref,
    sse_ref,
    tok,
    mid,
    qkv,
    att,
    branch,
    outb,
    normed,
    act,
    dinner,
    dsmall,
    dqkv,
    stage,
    sems,
):
    steps = images // group
    crow = group * TOK
    lane = lax.broadcasted_iota(jnp.int32, (TOK, 128), 1)
    first_half = lane < HEAD_DIM

    def rows_of(i):
        return pl.ds(pl.multiple_of(i * TOK, TOK), TOK)

    def chunk_of(i):
        return pl.ds(pl.multiple_of(i * crow, crow), crow)

    def mod_row(b, k):
        return mods_ref[b, pl.ds(k, 1), :]

    g_bias_ref[...] = jnp.zeros_like(g_bias_ref)
    g_patch_ref[...] = jnp.zeros_like(g_patch_ref)
    g_head_ref[...] = jnp.zeros_like(g_head_ref)
    g_bpatch_ref[...] = jnp.zeros_like(g_bpatch_ref)
    g_bhead_ref[...] = jnp.zeros_like(g_bhead_ref)
    sse_ref[...] = jnp.zeros_like(sse_ref)
    depth = w_in_ref.shape[0]

    @pl.loop(0, images)
    def _(b):
        r = rows_of(b)
        tok[0, r, :] = dot(patches_ref[r, :], w_patch_ref[...], NT) + bpatch_ref[...] + pos_ref[...]

    def half(v, which):
        zero = jnp.zeros_like(v)
        return jnp.where(first_half, v, zero) if which == 0 else jnp.where(first_half, zero, v)

    def attention(layer, r):
        for pair in range(HEADS // 2):
            c = pair * 128
            q = qkv[layer, r, c : c + 128]
            k = qkv[layer, r, D + c : D + c + 128]
            v = qkv[layer, r, 2 * D + c : 2 * D + c + 128]
            got = []
            for which in range(2):
                s = dot(half(q, which), k, NT) * HEAD_DIM ** (-0.5)
                got.append(dot(soft_rows(s).astype(BF16), v))
            att[layer, r, c : c + 128] = jnp.where(first_half, got[0], got[1]).astype(BF16)

    def modulated(t, b, k):
        n, scale = norm_rows(t)
        return n, scale, (n * (1.0 + mod_row(b, k + 1)) + mod_row(b, k)).astype(BF16)

    for layer in range(depth):
        mo = layer * 6

        @pl.loop(0, steps)
        def _(i):
            cr = chunk_of(i)
            for j in range(group):
                b = i * group + j
                r = rows_of(b)
                normed[r, :] = modulated(tok[layer, r, :], b, mo)[2]
            hc = normed[cr, :]
            for part in range(3):
                p = dot(hc, w_in_ref[layer, :, QKV + part * D : QKV + (part + 1) * D])
                if part == 0:
                    p = p + bias_ref[layer : layer + 1, BQ : BQ + D]
                if part == 2:
                    p = p + bias_ref[layer : layer + 1, BV : BV + D]
                qkv[layer, cr, part * D : (part + 1) * D] = p.astype(BF16)
            for j in range(group):
                attention(layer, rows_of(i * group + j))
            br = dot(att[layer, cr, :], w_in_ref[layer, :, WO : WO + D]) + bias_ref[layer : layer + 1, BO : BO + D]
            branch[layer, cr, :] = br.astype(BF16)
            for j in range(group):
                b = i * group + j
                r = rows_of(b)
                t2 = tok[layer, r, :] + mod_row(b, mo + 2) * br[j * TOK : (j + 1) * TOK]
                mid[layer, r, :] = t2
                normed[r, :] = modulated(t2, b, mo + 3)[2]
            mc = normed[cr, :]
            out = jnp.zeros((crow, D), F32) + bias_ref[layer : layer + 1, BF2 : BF2 + D]
            for c in range(0, FF, FFC):
                x = dot(mc, w_in_ref[layer, :, WF1 + c : WF1 + c + FFC]) + bias_ref[layer : layer + 1, BF1 + c : BF1 + c + FFC]
                a = (x * (0.5 * (1.0 + gelu_parts(x)))).astype(BF16)
                out = out + dot(a, w_out_ref[layer, c : c + FFC, :])
            outb[layer, cr, :] = out.astype(BF16)
            for j in range(group):
                b = i * group + j
                r = rows_of(b)
                tok[layer + 1, r, :] = mid[layer, r, :] + mod_row(b, mo + 5) * out[j * TOK : (j + 1) * TOK]

    dtok = tok.at[depth]

    @pl.loop(0, images)
    def _(b):
        r = rows_of(b)
        k = 6 * depth
        n, scale, n3 = modulated(dtok[r, :], b, k)
        miss = dot(n3, w_head_ref[...], NT) + bhead_ref[...] - target_ref[r, :]
        sse_ref[...] += jnp.sum(rows_sum(miss * miss), axis=1, keepdims=True)
        dp = (2.0 * miss).astype(BF16)
        g_head_ref[...] += dot(dp, n3, TN)
        g_bhead_ref[...] += rows_sum(dp.astype(F32))
        dn3 = dot(dp, w_head_ref[...])
        g_mods_ref[b, pl.ds(k, 1), :] = rows_sum(dn3)
        g_mods_ref[b, pl.ds(k + 1, 1), :] = rows_sum(dn3 * n)
        dtok[r, :] = norm_back(dn3 * (1.0 + mod_row(b, k + 1)), n, scale)

    pending = {}

    def free(slot):
        for copy in pending.pop(slot, ()):
            copy.wait()

    def send_in(layer, first):
        slot = 0
        moves = []
        for q in range(4):
            source = stage.at[slot, :, q * D : (q + 1) * D]
            if blocked:
                target = (g_in_ref if first == QKV else g_out_ref).at[layer, q, :, 0:D]
            else:
                target = g_in_ref.at[layer, :, first + q * D : first + (q + 1) * D]
            moves.append(pltpu.make_async_copy(source, target, sems.at[slot, q]))
        for move in moves:
            move.start()
        pending[slot] = moves

    def send_down(layer):
        slot = 1
        moves = []
        for c in range(4):
            if not blocked:
                source = stage.at[slot, :, c * D : (c + 1) * D]
                target = g_out_ref.at[layer, c * D : (c + 1) * D, :]
                moves.append(pltpu.make_async_copy(source, target, sems.at[slot, c]))
                continue
            for owner in range(2):
                for q in range(4):
                    start = owner * (D // 2) + q * OWN
                    source = stage.at[slot, start : start + OWN, c * D : (c + 1) * D]
                    begin = (2 * c + owner) * OWN
                    target = g_out_ref.at[layer, q, begin : begin + OWN, D : 2 * D]
                    moves.append(pltpu.make_async_copy(source, target, sems.at[slot, len(moves)]))
        for move in moves:
            move.start()
        pending[slot] = moves

    for layer in reversed(range(depth)):
        mo = layer * 6
        lb = slice(layer, layer + 1)

        @pl.loop(0, steps)
        def _(i):
            cr = chunk_of(i)
            for j in range(group):
                b = i * group + j
                r = rows_of(b)
                normed[r, :] = modulated(mid[layer, r, :], b, mo + 3)[2]
                d = dtok[r, :]
                g_mods_ref[b, pl.ds(mo + 5, 1), :] = rows_sum(d * outb[layer, r, :].astype(F32))
                do = (d * mod_row(b, mo + 5)).astype(BF16)
                dsmall[r, :] = do
                g_bias_ref[lb, BF2 : BF2 + D] += rows_sum(do.astype(F32))
            mc = normed[cr, :]
            do = dsmall[cr, :]
            dm = jnp.zeros((crow, D), F32)
            for c in range(0, FF, FFC):
                x = dot(mc, w_in_ref[layer, :, WF1 + c : WF1 + c + FFC]) + bias_ref[lb, BF1 + c : BF1 + c + FFC]
                x2 = x * x
                t = jnp.tanh(GELU_A * (x + GELU_B * (x2 * x)))
                cdf = 0.5 * (1.0 + t)
                act[cr, c : c + FFC] = (x * cdf).astype(BF16)
                slope = cdf + (0.5 * GELU_A) * x * (1.0 - t * t) * (1.0 + (3.0 * GELU_B) * x2)
                di = (dot(do, w_out_ref[layer, c : c + FFC, :], NT) * slope).astype(BF16)
                dinner[cr, c : c + FFC] = di
                g_bias_ref[lb, BF1 + c : BF1 + c + FFC] += rows_sum(di.astype(F32))
                dm = dm + dot(di, w_in_ref[layer, :, WF1 + c : WF1 + c + FFC], NT)
            for j in range(group):
                b = i * group + j
                r = rows_of(b)
                n, scale = norm_rows(mid[layer, r, :])
                dmj = dm[j * TOK : (j + 1) * TOK]
                g_mods_ref[b, pl.ds(mo + 3, 1), :] = rows_sum(dmj)
                g_mods_ref[b, pl.ds(mo + 4, 1), :] = rows_sum(dmj * n)
                dtok[r, :] = dtok[r, :] + norm_back(dmj * (1.0 + mod_row(b, mo + 4)), n, scale)

        free(0)

        @pl.loop(0, FF // D)
        def _(c):
            cs = pl.ds(pl.multiple_of(c * D, D), D)
            stage[0, :, cs] = dot(normed[...], dinner[:, cs], TN)

        send_in(layer, WF1)
        free(1)

        @pl.loop(0, FF // D)
        def _(c):
            cs = pl.ds(pl.multiple_of(c * D, D), D)
            stage[1, :, cs] = dot(dsmall[...], act[:, cs], TN).T

        send_down(layer)

        @pl.loop(0, steps)
        def _(i):
            cr = chunk_of(i)
            for j in range(group):
                b = i * group + j
                r = rows_of(b)
                d = dtok[r, :]
                g_mods_ref[b, pl.ds(mo + 2, 1), :] = rows_sum(d * branch[layer, r, :].astype(F32))
                db = (d * mod_row(b, mo + 2)).astype(BF16)
                dsmall[r, :] = db
                g_bias_ref[lb, BO : BO + D] += rows_sum(db.astype(F32))
            branch[layer, cr, :] = dot(dsmall[cr, :], w_in_ref[layer, :, WO : WO + D], NT).astype(BF16)
            for j in range(group):
                r = rows_of(i * group + j)
                for pair in range(HEADS // 2):
                    c = pair * 128
                    q = qkv[layer, r, c : c + 128]
                    k = qkv[layer, r, D + c : D + c + 128]
                    v = qkv[layer, r, 2 * D + c : 2 * D + c + 128]
                    da = branch[layer, r, c : c + 128]
                    got = []
                    for which in range(2):
                        s = dot(half(q, which), k, NT) * HEAD_DIM ** (-0.5)
                        p = soft_rows(s)
                        dv = dot(p.astype(BF16), da, TN)
                        dpr = dot(half(da, which), v, NT)
                        ds = p * (dpr - jnp.sum(dpr * p, axis=-1, keepdims=True))
                        ds = ds.astype(BF16)
                        dq = dot(ds, k)
                        dk = dot(ds, q, TN)
                        got.append((dq, dk, dv))
                    dq = (jnp.where(first_half, got[0][0], got[1][0]) * HEAD_DIM ** (-0.5)).astype(BF16)
                    dk = (jnp.where(first_half, got[0][1], got[1][1]) * HEAD_DIM ** (-0.5)).astype(BF16)
                    dv = jnp.where(first_half, got[0][2], got[1][2]).astype(BF16)
                    dqkv[r, c : c + 128] = dq
                    dqkv[r, D + c : D + c + 128] = dk
                    dqkv[r, 2 * D + c : 2 * D + c + 128] = dv
                    g_bias_ref[lb, BQ + c : BQ + c + 128] += rows_sum(dq.astype(F32))
                    g_bias_ref[lb, BV + c : BV + c + 128] += rows_sum(dv.astype(F32))
            dh = dot(dqkv[cr, :], w_in_ref[layer, :, QKV : QKV + 3 * D], NT)
            for j in range(group):
                b = i * group + j
                r = rows_of(b)
                n, scale, h = modulated(tok[layer, r, :], b, mo)
                normed[r, :] = h
                dhj = dh[j * TOK : (j + 1) * TOK]
                g_mods_ref[b, pl.ds(mo, 1), :] = rows_sum(dhj)
                g_mods_ref[b, pl.ds(mo + 1, 1), :] = rows_sum(dhj * n)
                dtok[r, :] = dtok[r, :] + norm_back(dhj * (1.0 + mod_row(b, mo + 1)), n, scale)

        free(0)

        @pl.loop(0, 3)
        def _(c):
            cs = pl.ds(pl.multiple_of(c * D, D), D)
            stage[0, :, cs] = dot(normed[...], dqkv[:, cs], TN)

        stage[0, :, 3 * D : 4 * D] = dot(att[layer], dsmall[...], TN)
        send_in(layer, QKV)
        free(1)

    @pl.loop(0, images)
    def _(b):
        r = rows_of(b)
        d = dtok[r, :].astype(BF16)
        g_bpatch_ref[...] += rows_sum(d.astype(F32))
        g_patch_ref[...] += dot(patches_ref[r, :], d, TN)

    free(0)


def compute(patches, target, pos, mods, w_in, w_out, w_patch, w_head_t, bias, bpatch, bhead, group=3, blocked=False):
    depth = w_in.shape[0]
    rows = patches.shape[0]
    images = rows // TOK
    kinds = mods.shape[1]
    vm = pl.BlockSpec(memory_space=pltpu.VMEM)
    anyspace = pl.BlockSpec(memory_space=pl.ANY)
    shape = jax.ShapeDtypeStruct
    return pl.pallas_call(
        functools.partial(compute_kernel, images, group, blocked),
        out_shape=(
            shape((depth, 4, D, D) if blocked else (depth, D, 4 * D + FF), F32),
            shape((depth, 4, D, 2 * D) if blocked else (depth, FF, D), F32),
            shape((PATCH_IN, D), F32),
            shape((PATCH_IN, D), F32),
            shape((depth, BW), F32),
            shape((1, D), F32),
            shape((1, PATCH_IN), F32),
            shape((images, kinds, D), F32),
            shape((1, 1), F32),
        ),
        in_specs=[vm] * 11,
        out_specs=(anyspace, anyspace, vm, vm, vm, vm, vm, vm, vm),
        scratch_shapes=[
            pltpu.VMEM((depth + 1, rows, D), F32),
            pltpu.VMEM((depth, rows, D), F32),
            pltpu.VMEM((depth, rows, 3 * D), BF16),
            pltpu.VMEM((depth, rows, D), BF16),
            pltpu.VMEM((depth, rows, D), BF16),
            pltpu.VMEM((depth, rows, D), BF16),
            pltpu.VMEM((rows, D), BF16),
            pltpu.VMEM((rows, FF), BF16),
            pltpu.VMEM((rows, FF), BF16),
            pltpu.VMEM((rows, D), BF16),
            pltpu.VMEM((rows, 3 * D), BF16),
            pltpu.VMEM((2, D, FF), F32),
            pltpu.SemaphoreType.DMA((2, 32)),
        ],
        compiler_params=pltpu.CompilerParams(vmem_limit_bytes=60 * 1024 * 1024),
        name="step_compute",
    )(patches, target, pos, mods, w_in, w_out, w_patch, w_head_t, bias, bpatch, bhead)


def place():
    f = lax.axis_index("fsdp")
    r = lax.axis_index("rep")
    z = f // 2
    y = f - 2 * z
    x = r // 2
    c = r - 2 * x
    return z, y, x, c


def device(z, y, x, c):
    return {"fsdp": 2 * z + y, "rep": 2 * x + c}


def greet(peers):
    barrier = pltpu.get_barrier_semaphore()
    for peer in peers:
        pl.semaphore_signal(barrier, inc=1, device_id=peer, device_id_type=pl.DeviceIdType.MESH)
    pl.semaphore_wait(barrier, len(peers))


def remote(source, target, send, recv, peer):
    return pltpu.make_async_remote_copy(
        src_ref=source, dst_ref=target, send_sem=send, recv_sem=recv, device_id=peer, device_id_type=pl.DeviceIdType.MESH
    )


class Reducer:
    def __init__(self, source, bufs, out, sends, recvs, loads):
        self.source = source
        self.keep, self.got0, self.sx, self.gotx, self.sy, self.goty, self.sz, self.gotz, self.sw, self.gotw = bufs
        self.out = out
        self.sends, self.recvs, self.loads = sends, recvs, loads
        self.link = self.sx.dtype
        self.z, self.y, self.x, self.c = place()
        z, y, x, c = self.z, self.y, self.x, self.c
        self.to_c = device(z, y, x, 1 - c)
        self.to_x = device(z, y, 1 - x, c)
        self.to_y = device(z, 1 - y, x, c)
        self.z1 = z + 1 - 2 * lax.rem(z, 2)
        self.z2 = lax.rem(z + 2, 4)
        self.to_z1 = device(self.z1, y, x, c)
        self.to_z2 = device(self.z2, y, x, c)
        self.moves = {}

    def send(self, slot, source, target, peer):
        copy = remote(source, target, self.sends.at[slot], self.recvs.at[slot], peer)
        copy.start()
        self.moves[slot] = copy

    def step(self, k):
        z, y, x, c = self.z, self.y, self.x, self.c
        if k == 0:
            for half in range(2):
                load = pltpu.make_async_copy(self.source.at[2 * half + c], self.keep.at[half], self.loads.at[half])
                load.start()
                self.moves["load", half] = load
                self.send(half, self.source.at[2 * half + 1 - c], self.got0.at[half], self.to_c)
        if k == 1:
            for half in range(2):
                self.moves["load", half].wait()
                self.moves[half].wait()

            @pl.loop(0, 4)
            def _(i):
                for j in range(2):
                    self.sx[i, j] = (self.keep[1 - x, i, j] + self.got0[1 - x, i, j]).astype(self.link)

            self.send(2, self.sx, self.gotx, self.to_x)

            @pl.loop(0, 4)
            def _(i):
                for j in range(2):
                    self.keep[x, i, j] = self.keep[x, i, j] + self.got0[x, i, j]
        if k == 2:
            self.moves[2].wait()

            @pl.loop(0, 4)
            def _(i):
                self.sy[i] = (self.keep[x, i, 1 - y] + self.gotx[i, 1 - y].astype(F32)).astype(self.link)

            self.send(3, self.sy, self.goty, self.to_y)

            @pl.loop(0, 4)
            def _(i):
                self.keep[x, i, y] = self.keep[x, i, y] + self.gotx[i, y].astype(F32)
        if k == 3:
            self.moves[3].wait()
            for s in range(2):
                at = lax.rem(self.z1 + 2 * s, 4)
                self.sz[s] = (self.keep[x, at, y] + self.goty[at].astype(F32)).astype(self.link)
            self.send(4, self.sz, self.gotz, self.to_z1)
            for s in range(2):
                at = lax.rem(z + 2 * s, 4)
                self.keep[x, at, y] = self.keep[x, at, y] + self.goty[at].astype(F32)
        if k == 4:
            self.moves[4].wait()
            self.sw[...] = (self.keep[x, self.z2, y] + self.gotz[1].astype(F32)).astype(self.link)
            self.send(5, self.sw, self.gotw, self.to_z2)
        if k == 5:
            self.moves[5].wait()
            mine = 2 * x + c
            self.out[mine] = self.keep[x, z, y] + self.gotz[0].astype(F32) + self.gotw[...].astype(F32)
            self.send(6, self.out.at[mine], self.out.at[mine], self.to_x)
            self.send(7, self.out.at[mine], self.out.at[mine], self.to_c)
        if k == 6:
            self.moves[6].wait()
            other = 2 * (1 - x) + c
            self.send(8, self.out.at[other], self.out.at[other], self.to_c)
        if k == 7:
            self.moves[7].wait()
            self.moves[8].wait()

    def peers(self):
        return [self.to_c, self.to_x, self.to_y, self.to_z1, self.to_z2]


REDUCER_STEPS = 8


def reducer_scratch(width, own=OWN, link=BF16):
    return [
        pltpu.VMEM((2, 4, 2, own, width), F32),
        pltpu.VMEM((2, 4, 2, own, width), F32),
        pltpu.VMEM((4, 2, own, width), link),
        pltpu.VMEM((4, 2, own, width), link),
        pltpu.VMEM((4, own, width), link),
        pltpu.VMEM((4, own, width), link),
        pltpu.VMEM((2, own, width), link),
        pltpu.VMEM((2, own, width), link),
        pltpu.VMEM((own, width), link),
        pltpu.VMEM((own, width), link),
    ]


def reduce_kernel(depth, t_ref, m_ref, s_ref, out_t_ref, out_m_ref, out_s_ref, *scratch):
    sends, recvs, loads = scratch[-3:]
    pieces = []

    def piece(source, out):
        n = len(pieces)
        pieces.append(Reducer(source, scratch[10 * n : 10 * n + 10], out, sends.at[n], recvs.at[n], loads.at[n]))

    for layer in reversed(range(depth)):
        piece(m_ref.at[layer], out_m_ref.at[layer])
        piece(t_ref.at[layer], out_t_ref.at[layer])
    piece(s_ref, out_s_ref)
    greet(pieces[0].peers())
    for t in range(REDUCER_STEPS + len(pieces) - 1):
        for n, one in enumerate(pieces):
            if 0 <= t - n < REDUCER_STEPS:
                one.step(t - n)


def reduce_grads(g_t, g_m, small):
    depth = g_t.shape[0]
    shape = jax.ShapeDtypeStruct
    scratch = []
    for _ in range(depth):
        scratch += reducer_scratch(2 * D) + reducer_scratch(D)
    scratch += reducer_scratch(128, 8, F32)
    count = 2 * depth + 1
    scratch += [pltpu.SemaphoreType.DMA((count, 9)), pltpu.SemaphoreType.DMA((count, 9)), pltpu.SemaphoreType.DMA((count, 2))]
    anyspace = pl.BlockSpec(memory_space=pl.ANY)
    vm = pl.BlockSpec(memory_space=pltpu.VMEM)
    return pl.pallas_call(
        functools.partial(reduce_kernel, depth),
        out_shape=(shape((depth, 4, OWN, D), F32), shape((depth, 4, OWN, 2 * D), F32), shape((4, 8, 128), F32)),
        in_specs=[anyspace] * 3,
        out_specs=(vm, vm, vm),
        scratch_shapes=scratch,
        compiler_params=pltpu.CompilerParams(collective_id=1, has_side_effects=True, vmem_limit_bytes=60 * 1024 * 1024),
        name="step_reduce",
    )(g_t.reshape(depth, 4, 4, 2, OWN, D), g_m.reshape(depth, 4, 4, 2, OWN, 2 * D), small)


class Gatherer:
    def __init__(self, source, target, whole, sends, recvs, local):
        self.source, self.target, self.whole = source, target, whole
        self.sends, self.recvs, self.local = sends, recvs, local
        self.z, self.y, self.x, self.c = place()
        self.q = 2 * self.x + self.c
        self.moves = {}

    def send(self, slot, source, target, peer):
        copy = remote(source, target, self.sends.at[slot], self.recvs.at[slot], peer)
        copy.start()
        self.moves[slot] = copy

    def step(self, k):
        z, y, x, c, q = self.z, self.y, self.x, self.c, self.q
        f = 2 * z + y
        if k == 0:
            for d in range(1, 4):
                peer = lax.rem(z + d, 4)
                self.send(d - 1, self.source(q), self.target(f, q), device(peer, y, x, c))
            self.send(3, self.source(q), self.target(f, q), device(z, 1 - y, x, c))
            own = pltpu.make_async_copy(self.source(q), self.target(f, q), self.local)
            own.start()
            self.moves["own"] = own
        if k == 1:
            for d in range(1, 4):
                self.moves[d - 1].wait()
                at = 2 * lax.rem(z + 4 - d, 4) + y
                self.send(3 + d, self.target(at, q), self.target(at, q), device(z, 1 - y, x, c))
        if k == 2:
            self.moves["own"].wait()
            for slot in range(3, 7):
                self.moves[slot].wait()
            self.send(7, self.whole(q), self.whole(q), device(z, y, 1 - x, c))
            self.send(8, self.whole(q), self.whole(q), device(z, y, x, 1 - c))
        if k == 3:
            self.moves[7].wait()
            other = 2 * (1 - x) + c
            self.send(9, self.whole(other), self.whole(other), device(z, y, x, 1 - c))
        if k == 4:
            self.moves[8].wait()
            self.moves[9].wait()

    def peers(self):
        z, y, x, c = self.z, self.y, self.x, self.c
        return [device(lax.rem(z + d, 4), y, x, c) for d in range(1, 4)] + [
            device(z, 1 - y, x, c),
            device(z, y, 1 - x, c),
            device(z, y, x, 1 - c),
        ]


GATHER_STEPS = 5


def by_columns(source, target, sends, recvs, local):
    rows, width = source.shape
    part = width // 4

    def cols(q):
        return pl.ds(pl.multiple_of(q * part, 128), part)

    def rows_of(f):
        return pl.ds(pl.multiple_of(f * rows, 16), rows)

    return Gatherer(
        lambda q: source.at[:, cols(q)],
        lambda f, q: target.at[rows_of(f), cols(q)],
        lambda q: target.at[:, cols(q)],
        sends,
        recvs,
        local,
    )


def by_rows(source, target, sends, recvs, local):
    return Gatherer(
        lambda q: source.at[q],
        lambda f, q: target.at[f, q],
        lambda q: target.at[:, q],
        sends,
        recvs,
        local,
    )


def gather_kernel(kinds, *refs):
    n = len(kinds)
    sends, recvs, local = refs[-3:]
    pieces = []
    for i, kind in enumerate(kinds):
        make = by_columns if kind == "columns" else by_rows
        pieces.append(make(refs[i], refs[n + i], sends.at[i], recvs.at[i], local.at[i]))
    greet(pieces[0].peers())
    for t in range(GATHER_STEPS + n - 1):
        for i, piece in enumerate(pieces):
            if 0 <= t - i < GATHER_STEPS:
                piece.step(t - i)


def gather(items, ident, space=pltpu.VMEM):
    kinds = tuple(kind for kind, _ in items)
    n = len(items)
    outs = tuple(
        jax.ShapeDtypeStruct((8 * v.shape[0],) + v.shape[1:] if kind == "columns" else (8,) + v.shape, v.dtype)
        for kind, v in items
    )
    return pl.pallas_call(
        functools.partial(gather_kernel, kinds),
        out_shape=outs,
        in_specs=[pl.BlockSpec(memory_space=pl.ANY)] * n,
        out_specs=tuple(pl.BlockSpec(memory_space=space) for _ in items),
        scratch_shapes=[
            pltpu.SemaphoreType.DMA((n, 10)),
            pltpu.SemaphoreType.DMA((n, 10)),
            pltpu.SemaphoreType.DMA((n,)),
        ],
        compiler_params=pltpu.CompilerParams(collective_id=ident, has_side_effects=True, vmem_limit_bytes=60 * 1024 * 1024),
        name="step_gather",
    )(*[v for _, v in items])


def exchange_kernel(axes, count, x_ref, out_ref, sends, recvs, local):
    sizes = [lax.axis_size(a) for a in axes]
    me = lax.axis_index(axes[0])
    for a in axes[1:]:
        me = me * lax.axis_size(a) + lax.axis_index(a)

    def peer_of(k):
        other = lax.rem(me + k, count)
        if len(axes) == 1:
            return {axes[0]: other}
        return {axes[0]: other // sizes[1], axes[1]: lax.rem(other, sizes[1])}

    greet([peer_of(k) for k in range(1, count)])
    own = pltpu.make_async_copy(x_ref, out_ref.at[me], local)
    own.start()
    copies = []
    for k in range(1, count):
        copies.append(remote(x_ref, out_ref.at[me], sends.at[k - 1], recvs.at[k - 1], peer_of(k)))
        copies[-1].start()
    own.wait()
    for copy in copies:
        copy.wait()


def exchange(x, axes, count, ident):
    vm = pl.BlockSpec(memory_space=pltpu.VMEM)
    return pl.pallas_call(
        functools.partial(exchange_kernel, axes, count),
        out_shape=jax.ShapeDtypeStruct((count,) + x.shape, x.dtype),
        in_specs=[vm],
        out_specs=vm,
        scratch_shapes=[
            pltpu.SemaphoreType.DMA((count - 1,)),
            pltpu.SemaphoreType.DMA((count - 1,)),
            pltpu.SemaphoreType.DMA,
        ],
        compiler_params=pltpu.CompilerParams(collective_id=ident, has_side_effects=True),
        name="step_exchange",
    )(x)


def swap_kernel(count, x_ref, out_ref, got, sends, recvs, local):
    me = lax.axis_index("fsdp")
    peers = [{"fsdp": lax.rem(me + k, count)} for k in range(1, count)]
    greet(peers)
    own = pltpu.make_async_copy(x_ref.at[me], got.at[me], local)
    own.start()
    copies = []
    for k in range(1, count):
        copies.append(remote(x_ref.at[lax.rem(me + k, count)], got.at[me], sends.at[k - 1], recvs.at[k - 1], peers[k - 1]))
        copies[-1].start()
    own.wait()
    for copy in copies:
        copy.wait()
    total = got[0]
    for k in range(1, count):
        total = total + got[k]
    out_ref[...] = total


def swap_sum(x, ident):
    count = x.shape[0]
    vm = pl.BlockSpec(memory_space=pltpu.VMEM)
    return pl.pallas_call(
        functools.partial(swap_kernel, count),
        out_shape=jax.ShapeDtypeStruct(x.shape[1:], x.dtype),
        in_specs=[vm],
        out_specs=vm,
        scratch_shapes=[
            pltpu.VMEM(x.shape, x.dtype),
            pltpu.SemaphoreType.DMA((count - 1,)),
            pltpu.SemaphoreType.DMA((count - 1,)),
            pltpu.SemaphoreType.DMA,
        ],
        compiler_params=pltpu.CompilerParams(collective_id=ident, has_side_effects=True),
        name="step_swap",
    )(x)


def mix_weights(tsteps):
    betas = 0.0001 + (0.02 - 0.0001) * jnp.arange(TSTEPS, dtype=jnp.float32) / (TSTEPS - 1)
    alpha_bar = jnp.exp(jnp.cumsum(jnp.log(1.0 - betas)))
    picked = jnp.arange(TSTEPS)[None, :] == tsteps[:, None]
    return jnp.sum(jnp.where(picked, alpha_bar[None, :], 0.0), axis=1)


def patchify(latent_rows):
    images = latent_rows.shape[0]
    grid_side = GRID // PATCH
    shaped = latent_rows.reshape(images, CHANNELS, grid_side, PATCH, grid_side, PATCH)
    shaped = jnp.transpose(shaped, (0, 2, 4, 1, 3, 5))
    return shaped.reshape(images, grid_side * grid_side, CHANNELS * PATCH * PATCH)


def position_table():
    grid_side = GRID // PATCH
    quarter = D // 4
    omegas = 1.0 / 10000.0 ** (jnp.arange(quarter, dtype=jnp.float32) / quarter)
    places = jnp.arange(grid_side * grid_side)
    across = (places % grid_side).astype(jnp.float32)
    downward = (places // grid_side).astype(jnp.float32)

    def one_axis(coords):
        angles = coords[:, None] * omegas[None, :]
        return jnp.concatenate([jnp.sin(angles), jnp.cos(angles)], axis=1)

    return jnp.concatenate([one_axis(across), one_axis(downward)], axis=1)


def time_features(tsteps):
    half_freq = FREQ // 2
    frequencies = jnp.exp(-math.log(10000.0) * jnp.arange(half_freq, dtype=jnp.float32) / half_freq)
    angles = tsteps.astype(jnp.float32)[:, None] * frequencies[None, :]
    return jnp.concatenate([jnp.cos(angles), jnp.sin(angles)], axis=1)


def fetch(layer_in, layer_out, direct):
    own_in = layer_in[:, :, 6 * D :].astype(BF16)
    own_out = layer_out.astype(BF16)
    depth = layer_in.shape[0]
    if direct:
        items = []
        for layer in range(depth):
            items.append(("columns", own_in[layer]))
            items.append(("rows", own_out[layer].reshape(4, OWN, D)))
        got = gather(items, 2)
        return jnp.stack(got[0::2]), jnp.stack([v.reshape(FF, D) for v in got[1::2]])
    w_in = lax.all_gather(own_in, "fsdp", axis=1, tiled=True)
    w_out = lax.all_gather(own_out, "fsdp", axis=1, tiled=True)
    return w_in, w_out


def silu_slope(x):
    gate = jax.nn.sigmoid(x)
    return gate * (1.0 + x * (1.0 - gate))


def matmul(a, b, form):
    return jnp.einsum(form, a, b, preferred_element_type=F32)


def step_of(grad, rows_new, cols_new, rows_mean):
    second = rows_new[:, :, None] * cols_new[:, None, :] / rows_mean[:, None, None]
    return grad * lax.rsqrt(second)


def plain(weight, grad, moment):
    moment_new = decay * moment + (1.0 - decay) * (grad * grad + eps_stat)
    update = grad * lax.rsqrt(moment_new)
    root = jnp.sqrt(jnp.mean(update * update, axis=-1, keepdims=True))
    return (weight - rate * update / jnp.maximum(1.0, root / clip_level), moment_new)


def shards(
    latents,
    tsteps,
    labels,
    noise,
    layer_in,
    layer_out,
    edge_mat,
    layer_bias,
    top_bias,
    in_rows,
    in_cols,
    out_rows,
    out_cols,
    edge_rows,
    edge_cols,
    layer_bias_v,
    top_bias_v,
):
    images = latents.shape[0]
    depth, own, wide = layer_in.shape
    fsdp = lax.axis_size("fsdp")
    rep = lax.axis_size("rep")
    at_f = lax.axis_index("fsdp")
    at_r = lax.axis_index("rep")
    every = images * fsdp * rep
    direct = (fsdp, rep, own) == (8, 4, OWN)
    width = own * fsdp
    MOD = 6 * D
    start_freq = NCLS + PATCH_IN
    start_tail = start_freq + FREQ

    edge_low = edge_mat.astype(BF16)
    small = jnp.concatenate([edge_low[:, : start_tail + D], edge_low[:, start_tail + 3 * D :]], axis=1)
    if direct:
        small = jnp.pad(small, ((0, 0), (0, -small.shape[1] % 512)))
        full = gather([("columns", small)], 3)[0]
    else:
        full = lax.all_gather(small, "fsdp", axis=0, tiled=True)
    class_cols = full[:, :NCLS]
    patch_cols = full[:, NCLS:start_freq]
    freq_cols = full[:, start_freq:start_tail]
    time_second = full[:, start_tail : start_tail + D]
    head_cols = full[:, start_tail + D : start_tail + D + PATCH_IN]
    if direct:
        both = jnp.pad(jnp.stack([tsteps, labels]), ((0, 6), (0, 128 - images)))
        both = exchange(both, ("fsdp", "rep"), fsdp * rep, 4)
        all_tsteps = both[:, 0, :images].reshape(every)
        all_labels = both[:, 1, :images].reshape(every)
    else:
        all_tsteps = lax.all_gather(tsteps, ("fsdp", "rep"), axis=0, tiled=True)
        all_labels = lax.all_gather(labels, ("fsdp", "rep"), axis=0, tiled=True)
    features = time_features(all_tsteps).astype(BF16)
    time1 = matmul(features, freq_cols, "bf,df->bd") + top_bias[D : 2 * D]
    s1 = jax.nn.silu(time1).astype(BF16)
    picked = (all_labels[:, None] == jnp.arange(NCLS)[None, :]).astype(BF16)
    before = matmul(s1, time_second, "bd,de->be") + top_bias[2 * D : 3 * D] + matmul(picked, class_cols, "bc,dc->bd")
    cond = jax.nn.silu(before).astype(BF16)

    def own_part(values):
        return lax.dynamic_slice_in_dim(values, at_f * own, own, axis=1)

    low_in = layer_in.astype(BF16)
    w_mods = jnp.concatenate(
        [low_in[layer, :, :MOD] for layer in range(depth)] + [edge_low[:, start_tail + D : start_tail + 3 * D]], axis=1
    )
    cond_own = own_part(cond)
    group_own = lax.dynamic_index_in_dim(cond_own.reshape(fsdp, rep, images, own), at_r, axis=1, keepdims=False)
    part = matmul(group_own.reshape(fsdp * images, own), w_mods, "bd,de->be")
    bias_mods = jnp.concatenate([layer_bias[layer, :MOD] for layer in range(depth)] + [top_bias[3 * D : 5 * D]])
    kinds = 6 * depth + 2
    if direct:
        mods = swap_sum(jnp.pad(part.reshape(fsdp, images, kinds * D), ((0, 0), (0, 8 - images), (0, 0))), 5)[:images]
    else:
        mods = lax.psum_scatter(part, "fsdp", scatter_dimension=0, tiled=True)
    mods = (mods + bias_mods).reshape(images, kinds, D)

    alphas = mix_weights(tsteps)
    noisy = jnp.sqrt(alphas)[:, None, None] * latents + jnp.sqrt(1.0 - alphas)[:, None, None] * noise
    patches = patchify(noisy).astype(BF16).reshape(images * TOK, PATCH_IN)
    target = patchify(noise).reshape(images * TOK, PATCH_IN)

    w_in, w_out = fetch(layer_in, layer_out, direct)
    bias_rows = jnp.concatenate([layer_bias[:, MOD : MOD + D], layer_bias[:, MOD + D :]], axis=1)
    g_in, g_out, g_patch, g_head, g_bias, g_bpatch, g_bhead, g_mods, sse = compute(
        patches,
        target,
        position_table(),
        jnp.pad(mods, ((0, 0), (0, 16 - kinds), (0, 0))),
        w_in,
        w_out,
        patch_cols,
        head_cols.T,
        bias_rows,
        top_bias[None, :D],
        top_bias[None, 5 * D : 5 * D + PATCH_IN],
        blocked=direct,
    )

    d_mods = g_mods[:, :kinds].astype(BF16).reshape(images, kinds * D)
    if direct:
        d_mods = exchange(jnp.pad(d_mods.reshape(-1, 128), ((0, 4), (0, 0))), ("fsdp", "rep"), fsdp * rep, 6)
        d_mods = d_mods[:, : images * kinds * D // 128].reshape(every, kinds * D)
    else:
        d_mods = lax.all_gather(d_mods, ("fsdp", "rep"), axis=0, tiled=True)
    g_rows = matmul(cond_own, d_mods, "bd,be->de")
    g_bmods = jnp.sum(d_mods.astype(F32), axis=0)
    d_before = matmul(d_mods, w_mods, "be,de->bd") * silu_slope(own_part(before))
    g_class = jnp.einsum("bd,bc->dc", d_before, picked.astype(F32), precision=lax.Precision.HIGHEST)
    d_time2 = d_before.astype(BF16)
    if direct:
        d_time2 = exchange(jnp.pad(d_time2, ((0, 0), (0, 128 - own))), ("fsdp",), fsdp, 7)
        d_time2 = jnp.transpose(d_time2[:, :, :own], (1, 0, 2)).reshape(every, width)
    else:
        d_time2 = lax.all_gather(d_time2, "fsdp", axis=1, tiled=True)
    g_time2 = matmul(own_part(s1), d_time2, "bd,be->de")
    d_time1 = (matmul(d_time2, time_second, "be,de->bd") * silu_slope(time1)).astype(BF16)
    g_time1 = matmul(own_part(d_time1), features, "bd,bf->df")

    if direct:
        parts = (g_patch, g_head, g_bias, g_bpatch, g_bhead, sse)
        flat = jnp.concatenate([v.reshape(-1) for v in parts])
        flat = jnp.pad(flat, (0, 32 * 1024 - flat.shape[0])).reshape(4, 4, 2, 8, 128)
        out_t, out_m, out_s = reduce_grads(g_in, g_out, flat)

        def joined(v):
            return jnp.transpose(v, (0, 2, 1, 3)).reshape(depth, own, 4 * D)

        shard_in = jnp.concatenate([joined(out_t), joined(out_m[..., :D])], axis=2)
        shard_out = out_m[..., D:].reshape(depth, 4 * own, D)
        flat = jnp.transpose(exchange(out_s, ("fsdp",), fsdp, 8), (1, 0, 2, 3)).reshape(-1)
        sums = []
        at = 0
        for v in parts:
            sums.append(flat[at : at + v.size].reshape(v.shape))
            at += v.size
        g_patch, g_head, g_bias, g_bpatch, g_bhead, sse = sums
    else:
        shard_in = lax.psum(lax.psum_scatter(g_in, "fsdp", scatter_dimension=1, tiled=True), "rep")
        shard_out = lax.psum(lax.psum_scatter(g_out, "fsdp", scatter_dimension=1, tiled=True), "rep")
        g_patch, g_head, g_bias, g_bpatch, g_bhead, sse = lax.psum(
            (g_patch, g_head, g_bias, g_bpatch, g_bhead, sse), ("fsdp", "rep")
        )

    def over_fsdp(values, ident):
        if not direct:
            return lax.psum(values, "fsdp")
        flat = jnp.concatenate([v.reshape(-1) for v in values])
        flat = jnp.pad(flat, (0, -flat.shape[0] % 1024)).reshape(-1, 128)
        flat = jnp.sum(exchange(flat, ("fsdp",), fsdp, ident), axis=0).reshape(-1)
        sums = []
        at = 0
        for v in values:
            sums.append(flat[at : at + v.size].reshape(v.shape))
            at += v.size
        return sums

    tok_total = every * TOK
    scale_grad = 1.0 / (PATCH_IN * math.sqrt(tok_total))
    loss = sse[0, 0] / (tok_total * PATCH_IN)
    fin = depth * MOD
    grad_edge = jnp.concatenate(
        [
            g_class,
            own_part(g_patch).T,
            g_time1,
            g_time2,
            g_rows[:, fin:],
            own_part(g_head).T,
            jnp.zeros((own, PATCH_IN), F32),
        ],
        axis=1,
    )[None] * scale_grad
    grad_in = jnp.concatenate([jnp.stack([g_rows[:, layer * MOD : (layer + 1) * MOD] for layer in range(depth)]), shard_in], axis=2) * scale_grad
    grad_out = shard_out * scale_grad
    grad_lbias = jnp.concatenate([g_bmods[:fin].reshape(depth, MOD), g_bias], axis=1) * scale_grad
    grad_tbias = jnp.concatenate(
        [
            g_bpatch[0],
            jnp.sum(d_time1.astype(F32), axis=0),
            jnp.sum(d_time2.astype(F32), axis=0),
            g_bmods[fin:],
            g_bhead[0],
            jnp.zeros((PATCH_IN,), F32),
        ]
    ) * scale_grad

    full_rows_in = width
    full_rows_out = layer_out.shape[1] * fsdp
    full_rows_edge = edge_mat.shape[0] * fsdp
    square_in = grad_in * grad_in + eps_stat
    square_out = grad_out * grad_out + eps_stat
    square_edge = grad_edge * grad_edge + eps_stat
    rows_in_new = decay * in_rows + (1.0 - decay) * jnp.mean(square_in, axis=2)
    rows_out_new = decay * out_rows + (1.0 - decay) * jnp.mean(square_out, axis=2)
    rows_edge_new = decay * edge_rows[None] + (1.0 - decay) * jnp.mean(square_edge, axis=2)
    col_in, total_in, col_out, total_out, col_edge, total_edge = over_fsdp(
        (
            jnp.sum(square_in, axis=1),
            jnp.sum(rows_in_new, axis=1),
            jnp.sum(square_out, axis=1),
            jnp.sum(rows_out_new, axis=1),
            jnp.sum(square_edge, axis=1),
            jnp.sum(rows_edge_new, axis=1),
        ),
        9,
    )
    cols_in_new = decay * in_cols + (1.0 - decay) * col_in / full_rows_in
    cols_out_new = decay * out_cols + (1.0 - decay) * col_out / full_rows_out
    cols_edge_new = decay * edge_cols[None] + (1.0 - decay) * col_edge / full_rows_edge
    update_in = step_of(grad_in, rows_in_new, cols_in_new, total_in / full_rows_in)
    update_out = step_of(grad_out, rows_out_new, cols_out_new, total_out / full_rows_out)
    update_edge = step_of(grad_edge, rows_edge_new, cols_edge_new, total_edge / full_rows_edge)
    sum_in, sum_out, sum_edge = over_fsdp(
        (
            jnp.sum(update_in * update_in, axis=(1, 2)),
            jnp.sum(update_out * update_out, axis=(1, 2)),
            jnp.sum(update_edge * update_edge, axis=(1, 2)),
        ),
        10,
    )
    roots_in = jnp.sqrt(sum_in / (full_rows_in * grad_in.shape[2]))
    roots_out = jnp.sqrt(sum_out / (full_rows_out * grad_out.shape[2]))
    roots_edge = jnp.sqrt(sum_edge / (full_rows_edge * grad_edge.shape[2]))
    factor_in = jnp.maximum(1.0, roots_in / clip_level)[:, None, None]
    factor_out = jnp.maximum(1.0, roots_out / clip_level)[:, None, None]
    factor_edge = jnp.maximum(1.0, roots_edge / clip_level)[:, None, None]
    in_new = layer_in - rate * update_in / factor_in
    out_new = layer_out - rate * update_out / factor_out
    edge_new = (edge_mat[None] - rate * update_edge / factor_edge)[0]
    clip_roots = jnp.concatenate([roots_in, roots_out, roots_edge])
    lbias_new, lbias_v_new = plain(layer_bias, grad_lbias, layer_bias_v)
    tbias_new, tbias_v_new = plain(top_bias, grad_tbias, top_bias_v)
    return (
        loss,
        in_new,
        out_new,
        edge_new,
        lbias_new,
        tbias_new,
        rows_in_new,
        cols_in_new,
        rows_out_new,
        cols_out_new,
        rows_edge_new[0],
        cols_edge_new[0],
        lbias_v_new,
        tbias_v_new,
        clip_roots,
    )


def solution(mesh):
    placed = (
        P(("fsdp", "rep"), None, None),
        P(("fsdp", "rep")),
        P(("fsdp", "rep")),
        P(("fsdp", "rep"), None, None),
        P(None, "fsdp", None),
        P(None, "fsdp", None),
        P("fsdp", None),
        P(),
        P(),
        P(None, "fsdp"),
        P(),
        P(None, "fsdp"),
        P(),
        P("fsdp"),
        P(),
        P(),
        P(),
    )
    return jax.shard_map(
        shards,
        mesh=mesh,
        in_specs=placed,
        out_specs=(
            P(),
            P(None, "fsdp", None),
            P(None, "fsdp", None),
            P("fsdp", None),
            P(),
            P(),
            P(None, "fsdp"),
            P(),
            P(None, "fsdp"),
            P(),
            P("fsdp"),
            P(),
            P(),
            P(),
            P(),
        ),
        check_vma=False,
    )
```

time: 1210 us -> 601 us (0.50)
  waiting for transfers between devices: 690 us -> 0 us
  Pallas kernels: 0 us -> 448 us
  matrix products: 180 us -> 12.8 us
  blocking collectives: 95.8 us -> 0 us
  other arithmetic: 128 us -> 58 us
  local copies, waits for them, and re-layouts: 84.3 us -> 67 us
  between operations: 21.5 us -> 5.46 us
    pallas_call x0 -> x11, Pallas kernels: none -> 448 us  [the longest x1 145 us: compute(): pl.pallas_call(functools.partial(compute_kernel, images, group, blocked),...]
    reduce_scatter x2 -> x0, waiting for transfers between devices: 376 us -> none  [the longest x1 279 us: shards(): lax.psum_scatter(grad_in_full, 'fsdp', scatter_dimension=1, tiled=True)]
    all_gather x5 -> x0, waiting for transfers between devices: 190 us -> none  [the longest x2 78.5 us: fetch_weights(): lax.all_gather(own_in, 'fsdp', axis=0, tiled=True)]
    dot_general x53 -> x10, matrix products: 163 us -> 12.8 us  [the longest x9 12.3 us: matmul(): return jnp.einsum(form, a, b, preferred_element_type=F32)]
    psum x3 -> x0, blocking collectives: 95.8 us -> none  [the longest x1 40.4 us: shards(): lax.psum((grad_lbias, grad_tbias, loss_sum), ('fsdp', 'rep'))]
    psum x1 -> x0, waiting for transfers between devices: 69.8 us -> none  [shards(): lax.psum((shard_in, shard_out, shard_edge), 'rep')]
    unnamed x10 -> x0, waiting for transfers between devices: 55.1 us -> none
    convert_element_type x20 -> x5, other arithmetic: 50.4 us -> 1.42 us  [the longest x1 1.07 us: shards(): edge_low = edge_mat.astype(BF16)]
  transfers between devices with their start and end apart: 9 -> 0, of which waited for: 9 -> 0; matrix products, arithmetic and copies ran while one was open for 11% -> 0% of each run, Pallas kernels for 0% -> 0%
where the time goes in v2:
time: 601 us; the launch traced here: 591 us
  Pallas kernels  448 us (75%)
  local copies, waits for them, and re-layouts  67 us (11%)
  other arithmetic  58 us (10%)
  matrix products  12.8 us (2%)
    pallas_call x1, Pallas kernels, compute(): pl.pallas_call(functools.partial(compute_kernel, images, group, blocked),...  145 us
    pallas_call x6, Pallas kernels, exchange(): pl.pallas_call(functools.partial(exchange_kernel, axes, count), out_shape...  108 us
    pallas_call x2, Pallas kernels, gather(): pl.pallas_call(functools.partial(gather_kernel, kinds), out_shape=outs, i...  92.4 us
    pallas_call x1, Pallas kernels, reduce_grads(): pl.pallas_call(functools.partial(reduce_kernel, depth), out_shape=(shape(...  75.7 us
    pallas_call x1, Pallas kernels, swap_sum(): pl.pallas_call(functools.partial(swap_kernel, count), out_shape=jax.Shape...  27.5 us
    dot_general x9, matrix products, matmul(): return jnp.einsum(form, a, b, preferred_element_type=F32)  12.3 us

profile of v2, /device:TPU:0, one launch (start us, length us, event | category | flops | bytes accessed | tf_op | source)
XLA Modules:
  0.0 591.4 jit_solution(16163830185470440314)
XLA Ops:
  2.6 26.1 %step_gather.2 = bf16[384,2048]{1,0:T(8,128)(2,1)} custom-call(bf16[48,2048]{1,0:T(8,128)(2,1)} %fusion.22.refs_0_), custom_call_target="tpu_custom_call" | custom-call | tf_op jit(solution)/shard_map/step_gather/pallas_call | solution.py:711
  29.3 9.6 %step_exchange.6 = s32[32,8,128]{2,1,0:T(8,128)} custom-call(s32[8,128]{1,0:T(8,128)} %pad.40.x_ref), custom_call_target="tpu_custom_call" | custom-call | tf_op jit(solution)/shard_map/step_exchange/pallas_call | solution.py:752
  40.5 2.1 multiply_convert_fusion
  49.8 27.5 %step_swap.1 = f32[8,5376]{1,0:T(8,128)} custom-call(f32[8,8,5376]{2,1,0:T(8,128)} %pad.42.x_ref), custom_call_target="tpu_custom_call" | custom-call | tf_op jit(solution)/shard_map/step_swap/pallas_call | solution.py:789
  82.8 66.3 %step_gather.3 = (bf16[384,3072]{1,0:T(8,128)(2,1)}, bf16[8,4,48,384]{3,2,1,0:T(8,128)(2,1)}, bf16[384,3072]{1,0:T(8,128)(2,1)}, bf16[8,4,48,384]{3,2,1,0:T(8,128)(2,1)}) custom-call(bf16[48,3072]{1,0:T(8,128)(2,1)} %get-tuple-element.76.refs_0_, bf16[4,48,384]{2,1,0:T(8,128)(2,1)} %bitcast.127, bf16[48,3072]{1,0:T(8,128)(2,1)} %get-tuple-element.75.refs_2_, ...), custom_call_target="tpu_custom_call" | custom-call | tf_op jit(solution)/shard_map/step_gather/pallas_call | solution.py:711
  149.1 5.2 pad_maximum_fusion.w_in_ref
  159.9 2.2 copy.70
  164.7 2.2 copy.72
  169.6 144.7 %step_compute.1 = (f32[2,4,384,384]{3,2,1,0:T(8,128)}, f32[2,4,384,768]{3,2,1,0:T(8,128)}, f32[16,384]{1,0:T(8,128)}, f32[16,384]{1,0:T(8,128)}, f32[2,3072]{1,0...) custom-call(bf16[1536,16]{1,0:T(8,128)(2,1)} %copy.76.patches_ref, ...), custom_call_target="tpu_custom_call" | custom-call | tf_op jit(solution)/shard_map/step_compute/pallas_call | solution.py:393
  319.3 75.7 %step_reduce.1 = (f32[2,4,48,384]{3,2,1,0:T(8,128)}, f32[2,4,48,768]{3,2,1,0:T(8,128)}, f32[4,8,128]{2,1,0:T(8,128)}) custom-call(f32[2,4,4,2,48,384]{5,4,3,2,1,0:T(8,128)} %bitcast.115, f32[2,4,4,2,48,768]{5,4,3,2,1,0:T(8,128)} %bitcast.106, f32[4,4,2,8,128]{4,3,2,1,0:T(8,128)} %bitcast.128), custom_call_target="tpu_custom_call" | custom-call | tf_op jit(solution)/shard_map/step_reduce/pallas_call | solution.py:593
  395.0 2.1 fusion.10
  397.9 41.1 %step_exchange.8 = bf16[32,256,128]{2,1,0:T(8,128)(2,1)} custom-call(bf16[256,128]{1,0:T(8,128)(2,1)} %pad.45.x_ref), custom_call_target="tpu_custom_call" | custom-call | tf_op jit(solution)/shard_map/step_exchange/pallas_call | solution.py:752
  439.0 3.6 reshape.465
  449.0 20.3 %step_exchange.7 = f32[8,4,8,128]{3,2,1,0:T(8,128)} custom-call(f32[4,8,128]{2,1,0:T(8,128)} %get-tuple-element.43.x_ref), custom_call_target="tpu_custom_call" | custom-call | tf_op jit(solution)/shard_map/step_exchange/pallas_call | solution.py:752
  477.1 2.3 fusion.53
  480.1 13.0 %step_exchange.9 = bf16[8,192,128]{2,1,0:T(8,128)(2,1)} custom-call(bf16[192,128]{1,0:T(8,128)(2,1)} %pad.46.x_ref), custom_call_target="tpu_custom_call" | custom-call | tf_op jit(solution)/shard_map/step_exchange/pallas_call | solution.py:752
  496.0 2.1 convert_reduce_fusion.2
  511.7 2.1 concatenate.83
  515.3 13.7 %step_exchange.10 = f32[8,112,128]{2,1,0:T(8,128)} custom-call(f32[112,128]{1,0:T(8,128)} %pad_bitcast_fusion.x_ref), custom_call_target="tpu_custom_call" | custom-call | tf_op jit(solution)/shard_map/step_exchange/pallas_call | solution.py:752
  535.7 2.3 multiply_reduce_fusion
  539.6 2.1 slice_multiply_fusion
  548.2 10.4 %step_exchange.11 = f32[8,8,128]{2,1,0:T(8,128)} custom-call(f32[8,128]{1,0:T(8,128)} %fusion.33.x_ref), custom_call_target="tpu_custom_call" | custom-call | tf_op jit(solution)/shard_map/step_exchange/pallas_call | solution.py:752
  581.7 2.2 divide_subtract_fusion.1
  583.9 2.3 fusion.9
  (219 shorter events, 104.8 us)
Async XLA Ops:
  0.6 28.0 %copy-start.38 = (s32[6]{0:T(128)S(1)}, s32[6]{0:T(128)}, u32[]{:S(2)}) copy-start(s32[6]{0:T(128)} %param.18) | copy-start | bytes 76
  0.7 28.0 %copy-start.41 = (s32[6]{0:T(128)S(1)}, s32[6]{0:T(128)}, u32[]{:S(2)}) copy-start(s32[6]{0:T(128)} %param.19) | copy-start | bytes 76
  0.7 39.8 %copy-start.30 = (f32[1952]{0:T(1024)S(1)}, f32[1952]{0:T(1024)}, u32[]{:S(2)}) copy-start(f32[1952]{0:T(1024)} %param.25) | copy-start | bytes 23428
  40.4 6.2 %copy-start.21 = (bf16[192,128]{1,0:T(8,128)(2,1)}, bf16[192,128]{1,0:T(8,128)(2,1)S(1)}, u32[]{:S(2)}) copy-start(bf16[192,128]{1,0:T(8,128)(2,1)S(1)} %get-tuple-element.93) | copy-start | bytes 147460
  40.5 6.2 %copy-start.23 = (bf16[192,128]{1,0:T(8,128)(2,1)}, bf16[192,128]{1,0:T(8,128)(2,1)S(1)}, u32[]{:S(2)}) copy-start(bf16[192,128]{1,0:T(8,128)(2,1)S(1)} %get-tuple-element.94) | copy-start | bytes 147460
  40.5 6.9 %copy-start = (f32[2,48,5376]{2,1,0:T(8,128)S(1)}, f32[2,48,5376]{2,1,0:T(8,128)}, u32[]{:S(2)}) copy-start(f32[2,48,5376]{2,1,0:T(8,128)} %param.21) | copy-start | bytes 6193156
  48.6 28.7 %copy-start.25 = (f32[2,5376]{1,0:T(2,128)S(1)}, f32[2,5376]{1,0:T(2,128)}, u32[]{:S(2)}) copy-start(f32[2,5376]{1,0:T(2,128)} %param.24) | copy-start | bytes 129028
  77.3 4.7 copy-start.7
  149.1 5.2 copy-start.8
  149.1 5.2 copy-start.9
  154.3 4.9 copy-start.15
  154.3 4.9 copy-start.28
  444.1 33.0 %copy-start.11 = (bf16[48,2304]{1,0:T(8,128)(2,1)S(1)}, bf16[48,2304]{1,0:T(8,128)(2,1)}, u32[]{:S(2)}) copy-start(bf16[48,2304]{1,0:T(8,128)(2,1)} %copy-done.10) | copy-start | bytes 663556
  479.4 18.7 %copy-start.22 = (bf16[192,128]{1,0:T(8,128)(2,1)S(1)}, bf16[192,128]{1,0:T(8,128)(2,1)}, u32[]{:S(2)}) copy-start(bf16[192,128]{1,0:T(8,128)(2,1)} %copy-done.21) | copy-start | bytes 147460
  494.8 8.1 %copy-start.20 = (f32[16,48]{0,1:T(8,128)S(1)}, f32[16,48]{0,1:T(8,128)}, u32[]{:S(2)}) copy-start(f32[16,48]{0,1:T(8,128)} %copy.94) | copy-start | bytes 9220
  513.9 25.7 %copy-start.34 = (f32[2,192]{1,0:T(2,128)S(1)}, f32[2,192]{1,0:T(2,128)}, u32[]{:S(2)}) copy-start(f32[2,192]{1,0:T(2,128)} %get-tuple-element.63) | copy-start | bytes 4612
  539.5 44.4 %copy-start.33 = (f32[2,384]{1,0:T(2,128)}, f32[2,384]{1,0:T(2,128)S(1)}, u32[]{:S(2)}) copy-start(f32[2,384]{1,0:T(2,128)S(1)} %multiply_add_fusion.4) | copy-start | bytes 9220
  542.5 39.2 %copy-start.26 = (f32[2457]{0:T(1024)}, f32[2457]{0:T(1024)S(1)}, u32[]{:S(2)}) copy-start(f32[2457]{0:T(1024)S(1)} %fusion.32) | copy-start | bytes 29488
  579.7 6.6 %copy-start.1 = (f32[2,48,5376]{2,1,0:T(8,128)S(1)}, f32[2,48,5376]{2,1,0:T(8,128)}, u32[]{:S(2)}) copy-start(f32[2,48,5376]{2,1,0:T(8,128)} %param.21) | copy-start | bytes 6193156
  581.7 4.6 copy-start.5
  581.7 4.6 copy-start.17
  581.7 4.6 copy-start.35
  581.7 4.6 copy-start.37
  581.7 4.6 copy-start.39
  (18 other events, 36.1 us)

commit v3 on v2

--- a/solution.py
+++ b/solution.py
@@ -31,7 +31,7 @@
 GELU_B = 0.044715
 NT = (((1,), (1,)), ((), ()))
 TN = (((0,), (0,)), ((), ()))
-FFC = 512
+FFC = 768
 OWN = 48
 
 
@@ -71,6 +71,7 @@
 WF1 = 4 * D
 BQ, BV, BO, BF1, BF2 = 0, D, 2 * D, 3 * D, 3 * D + FF
 BW = 4 * D + FF
+S_HEAD, S_BIAS, S_BPATCH, S_BHEAD, S_SSE, S_ROWS = 16, 32, 48, 49, 50, 56
 
 
 def compute_kernel(
@@ -90,13 +91,8 @@
     bhead_ref,
     g_in_ref,
     g_out_ref,
-    g_patch_ref,
-    g_head_ref,
-    g_bias_ref,
-    g_bpatch_ref,
-    g_bhead_ref,
+    sums_ref,
     g_mods_ref,
-    sse_ref,
     tok,
     mid,
     qkv,
@@ -109,6 +105,7 @@
     dsmall,
     dqkv,
     stage,
+    mod_sums,
     sems,
 ):
     steps = images // group
@@ -123,14 +120,19 @@
         return pl.ds(pl.multiple_of(i * crow, crow), crow)
 
     def mod_row(b, k):
-        return mods_ref[b, pl.ds(k, 1), :]
-
-    g_bias_ref[...] = jnp.zeros_like(g_bias_ref)
-    g_patch_ref[...] = jnp.zeros_like(g_patch_ref)
-    g_head_ref[...] = jnp.zeros_like(g_head_ref)
-    g_bpatch_ref[...] = jnp.zeros_like(g_bpatch_ref)
-    g_bhead_ref[...] = jnp.zeros_like(g_bhead_ref)
-    sse_ref[...] = jnp.zeros_like(sse_ref)
+        return mods_ref[k, pl.ds(b, 1), :]
+
+    sums_ref[...] = jnp.zeros_like(sums_ref)
+    mod_sums[...] = jnp.zeros_like(mod_sums)
+
+    def add_bias(layer, first, value):
+        for at in range(0, value.shape[1], D):
+            row = S_BIAS + 8 * layer + (first + at) // D
+            sums_ref[row : row + 1, :] += value[:, at : at + D]
+
+    def put_mod(b, k, value):
+        mod_sums[k, pl.ds(b, 1), :] = value
+
     depth = w_in_ref.shape[0]
 
     @pl.loop(0, images)
@@ -169,13 +171,11 @@
                 r = rows_of(b)
                 normed[r, :] = modulated(tok[layer, r, :], b, mo)[2]
             hc = normed[cr, :]
-            for part in range(3):
-                p = dot(hc, w_in_ref[layer, :, QKV + part * D : QKV + (part + 1) * D])
-                if part == 0:
-                    p = p + bias_ref[layer : layer + 1, BQ : BQ + D]
-                if part == 2:
-                    p = p + bias_ref[layer : layer + 1, BV : BV + D]
-                qkv[layer, cr, part * D : (part + 1) * D] = p.astype(BF16)
+            p = dot(hc, w_in_ref[layer, :, QKV : QKV + 2 * D])
+            qkv[layer, cr, 0:D] = (p[:, 0:D] + bias_ref[layer : layer + 1, BQ : BQ + D]).astype(BF16)
+            qkv[layer, cr, D : 2 * D] = p[:, D : 2 * D].astype(BF16)
+            p = dot(hc, w_in_ref[layer, :, QKV + 2 * D : QKV + 3 * D])
+            qkv[layer, cr, 2 * D : 3 * D] = (p + bias_ref[layer : layer + 1, BV : BV + D]).astype(BF16)
             for j in range(group):
                 attention(layer, rows_of(i * group + j))
             br = dot(att[layer, cr, :], w_in_ref[layer, :, WO : WO + D]) + bias_ref[layer : layer + 1, BO : BO + D]
@@ -206,13 +206,13 @@
         k = 6 * depth
         n, scale, n3 = modulated(dtok[r, :], b, k)
         miss = dot(n3, w_head_ref[...], NT) + bhead_ref[...] - target_ref[r, :]
-        sse_ref[...] += jnp.sum(rows_sum(miss * miss), axis=1, keepdims=True)
+        sums_ref[S_SSE : S_SSE + 1, 0:PATCH_IN] += rows_sum(miss * miss)
         dp = (2.0 * miss).astype(BF16)
-        g_head_ref[...] += dot(dp, n3, TN)
-        g_bhead_ref[...] += rows_sum(dp.astype(F32))
+        sums_ref[S_HEAD : S_HEAD + PATCH_IN, :] += dot(dp, n3, TN)
+        sums_ref[S_BHEAD : S_BHEAD + 1, 0:PATCH_IN] += rows_sum(dp.astype(F32))
         dn3 = dot(dp, w_head_ref[...])
-        g_mods_ref[b, pl.ds(k, 1), :] = rows_sum(dn3)
-        g_mods_ref[b, pl.ds(k + 1, 1), :] = rows_sum(dn3 * n)
+        put_mod(b, k, rows_sum(dn3))
+        put_mod(b, k + 1, rows_sum(dn3 * n))
         dtok[r, :] = norm_back(dn3 * (1.0 + mod_row(b, k + 1)), n, scale)
 
     pending = {}
@@ -267,10 +267,10 @@
                 r = rows_of(b)
                 normed[r, :] = modulated(mid[layer, r, :], b, mo + 3)[2]
                 d = dtok[r, :]
-                g_mods_ref[b, pl.ds(mo + 5, 1), :] = rows_sum(d * outb[layer, r, :].astype(F32))
+                put_mod(b, mo + 5, rows_sum(d * outb[layer, r, :].astype(F32)))
                 do = (d * mod_row(b, mo + 5)).astype(BF16)
                 dsmall[r, :] = do
-                g_bias_ref[lb, BF2 : BF2 + D] += rows_sum(do.astype(F32))
+                add_bias(layer, BF2, rows_sum(do.astype(F32)))
             mc = normed[cr, :]
             do = dsmall[cr, :]
             dm = jnp.zeros((crow, D), F32)
@@ -283,15 +283,15 @@
                 slope = cdf + (0.5 * GELU_A) * x * (1.0 - t * t) * (1.0 + (3.0 * GELU_B) * x2)
                 di = (dot(do, w_out_ref[layer, c : c + FFC, :], NT) * slope).astype(BF16)
                 dinner[cr, c : c + FFC] = di
-                g_bias_ref[lb, BF1 + c : BF1 + c + FFC] += rows_sum(di.astype(F32))
+                add_bias(layer, BF1 + c, rows_sum(di.astype(F32)))
                 dm = dm + dot(di, w_in_ref[layer, :, WF1 + c : WF1 + c + FFC], NT)
             for j in range(group):
                 b = i * group + j
                 r = rows_of(b)
                 n, scale = norm_rows(mid[layer, r, :])
                 dmj = dm[j * TOK : (j + 1) * TOK]
-                g_mods_ref[b, pl.ds(mo + 3, 1), :] = rows_sum(dmj)
-                g_mods_ref[b, pl.ds(mo + 4, 1), :] = rows_sum(dmj * n)
+                put_mod(b, mo + 3, rows_sum(dmj))
+                put_mod(b, mo + 4, rows_sum(dmj * n))
                 dtok[r, :] = dtok[r, :] + norm_back(dmj * (1.0 + mod_row(b, mo + 4)), n, scale)
 
         free(0)
@@ -318,10 +318,10 @@
                 b = i * group + j
                 r = rows_of(b)
                 d = dtok[r, :]
-                g_mods_ref[b, pl.ds(mo + 2, 1), :] = rows_sum(d * branch[layer, r, :].astype(F32))
+                put_mod(b, mo + 2, rows_sum(d * branch[layer, r, :].astype(F32)))
                 db = (d * mod_row(b, mo + 2)).astype(BF16)
                 dsmall[r, :] = db
-                g_bias_ref[lb, BO : BO + D] += rows_sum(db.astype(F32))
+                add_bias(layer, BO, rows_sum(db.astype(F32)))
             branch[layer, cr, :] = dot(dsmall[cr, :], w_in_ref[layer, :, WO : WO + D], NT).astype(BF16)
             for j in range(group):
                 r = rows_of(i * group + j)
@@ -348,8 +348,9 @@
                     dqkv[r, c : c + 128] = dq
                     dqkv[r, D + c : D + c + 128] = dk
                     dqkv[r, 2 * D + c : 2 * D + c + 128] = dv
-                    g_bias_ref[lb, BQ + c : BQ + c + 128] += rows_sum(dq.astype(F32))
-                    g_bias_ref[lb, BV + c : BV + c + 128] += rows_sum(dv.astype(F32))
+                    row = S_BIAS + 8 * layer
+                    sums_ref[row : row + 1, c : c + 128] += rows_sum(dq.astype(F32))
+                    sums_ref[row + 1 : row + 2, c : c + 128] += rows_sum(dv.astype(F32))
             dh = dot(dqkv[cr, :], w_in_ref[layer, :, QKV : QKV + 3 * D], NT)
             for j in range(group):
                 b = i * group + j
@@ -357,8 +358,8 @@
                 n, scale, h = modulated(tok[layer, r, :], b, mo)
                 normed[r, :] = h
                 dhj = dh[j * TOK : (j + 1) * TOK]
-                g_mods_ref[b, pl.ds(mo, 1), :] = rows_sum(dhj)
-                g_mods_ref[b, pl.ds(mo + 1, 1), :] = rows_sum(dhj * n)
+                put_mod(b, mo, rows_sum(dhj))
+                put_mod(b, mo + 1, rows_sum(dhj * n))
                 dtok[r, :] = dtok[r, :] + norm_back(dhj * (1.0 + mod_row(b, mo + 1)), n, scale)
 
         free(0)
@@ -376,9 +377,10 @@
     def _(b):
         r = rows_of(b)
         d = dtok[r, :].astype(BF16)
-        g_bpatch_ref[...] += rows_sum(d.astype(F32))
-        g_patch_ref[...] += dot(patches_ref[r, :], d, TN)
-
+        sums_ref[S_BPATCH : S_BPATCH + 1, :] += rows_sum(d.astype(F32))
+        sums_ref[0:PATCH_IN, :] += dot(patches_ref[r, :], d, TN)
+
+    g_mods_ref[...] = mod_sums[...].astype(BF16)
     free(0)
 
 
@@ -386,7 +388,7 @@
     depth = w_in.shape[0]
     rows = patches.shape[0]
     images = rows // TOK
-    kinds = mods.shape[1]
+    kinds = mods.shape[0]
     vm = pl.BlockSpec(memory_space=pltpu.VMEM)
     anyspace = pl.BlockSpec(memory_space=pl.ANY)
     shape = jax.ShapeDtypeStruct
@@ -395,16 +397,11 @@
         out_shape=(
             shape((depth, 4, D, D) if blocked else (depth, D, 4 * D + FF), F32),
             shape((depth, 4, D, 2 * D) if blocked else (depth, FF, D), F32),
-            shape((PATCH_IN, D), F32),
-            shape((PATCH_IN, D), F32),
-            shape((depth, BW), F32),
-            shape((1, D), F32),
-            shape((1, PATCH_IN), F32),
-            shape((images, kinds, D), F32),
-            shape((1, 1), F32),
+            shape((S_ROWS, D), F32),
+            shape((kinds, 8, D), BF16),
         ),
         in_specs=[vm] * 11,
-        out_specs=(anyspace, anyspace, vm, vm, vm, vm, vm, vm, vm),
+        out_specs=(anyspace, anyspace, vm, vm),
         scratch_shapes=[
             pltpu.VMEM((depth + 1, rows, D), F32),
             pltpu.VMEM((depth, rows, D), F32),
@@ -418,6 +415,7 @@
             pltpu.VMEM((rows, D), BF16),
             pltpu.VMEM((rows, 3 * D), BF16),
             pltpu.VMEM((2, D, FF), F32),
+            pltpu.VMEM((mods.shape[0], 8, D), F32),
             pltpu.SemaphoreType.DMA((2, 32)),
         ],
         compiler_params=pltpu.CompilerParams(vmem_limit_bytes=60 * 1024 * 1024),
@@ -560,47 +558,6 @@
     ]
 
 
-def reduce_kernel(depth, t_ref, m_ref, s_ref, out_t_ref, out_m_ref, out_s_ref, *scratch):
-    sends, recvs, loads = scratch[-3:]
-    pieces = []
-
-    def piece(source, out):
-        n = len(pieces)
-        pieces.append(Reducer(source, scratch[10 * n : 10 * n + 10], out, sends.at[n], recvs.at[n], loads.at[n]))
-
-    for layer in reversed(range(depth)):
-        piece(m_ref.at[layer], out_m_ref.at[layer])
-        piece(t_ref.at[layer], out_t_ref.at[layer])
-    piece(s_ref, out_s_ref)
-    greet(pieces[0].peers())
-    for t in range(REDUCER_STEPS + len(pieces) - 1):
-        for n, one in enumerate(pieces):
-            if 0 <= t - n < REDUCER_STEPS:
-                one.step(t - n)
-
-
-def reduce_grads(g_t, g_m, small):
-    depth = g_t.shape[0]
-    shape = jax.ShapeDtypeStruct
-    scratch = []
-    for _ in range(depth):
-        scratch += reducer_scratch(2 * D) + reducer_scratch(D)
-    scratch += reducer_scratch(128, 8, F32)
-    count = 2 * depth + 1
-    scratch += [pltpu.SemaphoreType.DMA((count, 9)), pltpu.SemaphoreType.DMA((count, 9)), pltpu.SemaphoreType.DMA((count, 2))]
-    anyspace = pl.BlockSpec(memory_space=pl.ANY)
-    vm = pl.BlockSpec(memory_space=pltpu.VMEM)
-    return pl.pallas_call(
-        functools.partial(reduce_kernel, depth),
-        out_shape=(shape((depth, 4, OWN, D), F32), shape((depth, 4, OWN, 2 * D), F32), shape((4, 8, 128), F32)),
-        in_specs=[anyspace] * 3,
-        out_specs=(vm, vm, vm),
-        scratch_shapes=scratch,
-        compiler_params=pltpu.CompilerParams(collective_id=1, has_side_effects=True, vmem_limit_bytes=60 * 1024 * 1024),
-        name="step_reduce",
-    )(g_t.reshape(depth, 4, 4, 2, OWN, D), g_m.reshape(depth, 4, 4, 2, OWN, 2 * D), small)
-
-
 class Gatherer:
     def __init__(self, source, target, whole, sends, recvs, local):
         self.source, self.target, self.whole = source, target, whole
@@ -687,119 +644,514 @@
     )
 
 
-def gather_kernel(kinds, *refs):
-    n = len(kinds)
-    sends, recvs, local = refs[-3:]
-    pieces = []
-    for i, kind in enumerate(kinds):
-        make = by_columns if kind == "columns" else by_rows
-        pieces.append(make(refs[i], refs[n + i], sends.at[i], recvs.at[i], local.at[i]))
-    greet(pieces[0].peers())
-    for t in range(GATHER_STEPS + n - 1):
-        for i, piece in enumerate(pieces):
-            if 0 <= t - i < GATHER_STEPS:
-                piece.step(t - i)
-
-
-def gather(items, ident, space=pltpu.VMEM):
-    kinds = tuple(kind for kind, _ in items)
-    n = len(items)
-    outs = tuple(
-        jax.ShapeDtypeStruct((8 * v.shape[0],) + v.shape[1:] if kind == "columns" else (8,) + v.shape, v.dtype)
-        for kind, v in items
-    )
-    return pl.pallas_call(
-        functools.partial(gather_kernel, kinds),
-        out_shape=outs,
-        in_specs=[pl.BlockSpec(memory_space=pl.ANY)] * n,
-        out_specs=tuple(pl.BlockSpec(memory_space=space) for _ in items),
-        scratch_shapes=[
-            pltpu.SemaphoreType.DMA((n, 10)),
-            pltpu.SemaphoreType.DMA((n, 10)),
-            pltpu.SemaphoreType.DMA((n,)),
-        ],
-        compiler_params=pltpu.CompilerParams(collective_id=ident, has_side_effects=True, vmem_limit_bytes=60 * 1024 * 1024),
-        name="step_gather",
-    )(*[v for _, v in items])
-
-
-def exchange_kernel(axes, count, x_ref, out_ref, sends, recvs, local):
-    sizes = [lax.axis_size(a) for a in axes]
-    me = lax.axis_index(axes[0])
-    for a in axes[1:]:
-        me = me * lax.axis_size(a) + lax.axis_index(a)
-
-    def peer_of(k):
-        other = lax.rem(me + k, count)
-        if len(axes) == 1:
-            return {axes[0]: other}
-        return {axes[0]: other // sizes[1], axes[1]: lax.rem(other, sizes[1])}
-
-    greet([peer_of(k) for k in range(1, count)])
-    own = pltpu.make_async_copy(x_ref, out_ref.at[me], local)
-    own.start()
-    copies = []
-    for k in range(1, count):
-        copies.append(remote(x_ref, out_ref.at[me], sends.at[k - 1], recvs.at[k - 1], peer_of(k)))
-        copies[-1].start()
-    own.wait()
-    for copy in copies:
-        copy.wait()
-
-
-def exchange(x, axes, count, ident):
+def slab(source, target, sends, recvs, local):
+    return Gatherer(lambda q: source, lambda f, q: target.at[q, f], lambda q: target.at[q], sends, recvs, local)
+
+
+class Butterfly:
+    def __init__(self, total, got, sends, recvs, like):
+        self.total, self.got, self.sends, self.recvs = total, got, sends, recvs
+        self.order = [like.to_c, like.to_x, like.to_y, like.to_z1, like.to_z2]
+        self.move = None
+
+    def step(self, k):
+        if k > 0:
+            self.move.wait()
+            self.total[...] = self.total[...] + self.got[k - 1]
+        if k < 5:
+            self.move = remote(self.total, self.got.at[k], self.sends.at[k], self.recvs.at[k], self.order[k])
+            self.move.start()
+
+
+BUTTERFLY_STEPS = 6
+
+
+def run_steps(plans):
+    last = max(first + count for first, count, _ in plans)
+    for tick in range(last):
+        for first, count, piece in plans:
+            if 0 <= tick - first < count:
+                piece.step(tick - first)
+
+
+def reduce_kernel(depth, t_ref, m_ref, s_ref, d_ref, out_t_ref, out_m_ref, out_s_ref, out_d_ref, *scratch):
+    scratch = list(scratch)
+    sends, recvs, loads, g_sends, g_recvs, g_local, b_sends, b_recvs, got = scratch[-9:]
+    plans = []
+
+    def piece(source, out):
+        n = len(plans)
+        one = Reducer(source, scratch[10 * n : 10 * n + 10], out, sends.at[n], recvs.at[n], loads.at[n])
+        plans.append((n, REDUCER_STEPS, one))
+
+    for layer in reversed(range(depth)):
+        piece(m_ref.at[layer], out_m_ref.at[layer])
+        piece(t_ref.at[layer], out_t_ref.at[layer])
+    first = plans[0][2]
+    mods = slab(d_ref, out_d_ref, g_sends, g_recvs, g_local)
+    out_s_ref[...] = s_ref[...]
+    sums = Butterfly(out_s_ref, got, b_sends, b_recvs, first)
+    z, y, x, c = place()
+    z3 = 3 - z
+    greet(first.peers() + [device(z3, y, x, c)])
+    run_steps([(0, GATHER_STEPS, mods), (0, BUTTERFLY_STEPS, sums)] + plans)
+
+
+def reduce_grads(g_t, g_m, sums, mods):
+    depth = g_t.shape[0]
+    shape = jax.ShapeDtypeStruct
+    scratch = []
+    for _ in range(depth):
+        scratch += reducer_scratch(2 * D) + reducer_scratch(D)
+    count = 2 * depth
+    dma = pltpu.SemaphoreType.DMA
+    scratch += [dma((count, 9)), dma((count, 9)), dma((count, 2)), dma((10,)), dma((10,)), dma, dma((5,)), dma((5,))]
+    scratch += [pltpu.VMEM((5,) + sums.shape, F32)]
+    anyspace = pl.BlockSpec(memory_space=pl.ANY)
     vm = pl.BlockSpec(memory_space=pltpu.VMEM)
     return pl.pallas_call(
-        functools.partial(exchange_kernel, axes, count),
-        out_shape=jax.ShapeDtypeStruct((count,) + x.shape, x.dtype),
-        in_specs=[vm],
-        out_specs=vm,
-        scratch_shapes=[
-            pltpu.SemaphoreType.DMA((count - 1,)),
-            pltpu.SemaphoreType.DMA((count - 1,)),
-            pltpu.SemaphoreType.DMA,
-        ],
-        compiler_params=pltpu.CompilerParams(collective_id=ident, has_side_effects=True),
-        name="step_exchange",
-    )(x)
-
-
-def swap_kernel(count, x_ref, out_ref, got, sends, recvs, local):
-    me = lax.axis_index("fsdp")
-    peers = [{"fsdp": lax.rem(me + k, count)} for k in range(1, count)]
-    greet(peers)
-    own = pltpu.make_async_copy(x_ref.at[me], got.at[me], local)
-    own.start()
+        functools.partial(reduce_kernel, depth),
+        out_shape=(
+            shape((depth, 4, OWN, D), F32),
+            shape((depth, 4, OWN, 2 * D), F32),
+            shape(sums.shape, F32),
+            shape((4, 8) + mods.shape, mods.dtype),
+        ),
+        in_specs=[anyspace, anyspace, vm, vm],
+        out_specs=(vm, vm, vm, vm),
+        scratch_shapes=scratch,
+        compiler_params=pltpu.CompilerParams(collective_id=1, has_side_effects=True, vmem_limit_bytes=60 * 1024 * 1024),
+        name="step_reduce",
+    )(g_t.reshape(depth, 4, 4, 2, OWN, D), g_m.reshape(depth, 4, 4, 2, OWN, 2 * D), sums, mods)
+
+
+C_T1, C_T2, C_PATCH, C_HEAD, C_ALL = 1024, 1280, 1664, 1680, 2048
+SLOTS = 256
+
+
+def silu_slope(x):
+    gate = 1.0 / (1.0 + jnp.exp(-x))
+    return gate * (1.0 + x * (1.0 - gate))
+
+
+def silu(x):
+    return x / (1.0 + jnp.exp(-x))
+
+
+def prologue_kernel(
+    depth,
+    kinds,
+    small_ref,
+    feat_ref,
+    w_mods_ref,
+    top_ref,
+    bias_ref,
+    own_in_ref,
+    own_out_ref,
+    full_ref,
+    w_in_ref,
+    w_out_ref,
+    mods_ref,
+    time1_ref,
+    s1_ref,
+    before_ref,
+    cond_ref,
+    feats_ref,
+    part,
+    got,
+    cond_rows,
+    wide,
+    sends,
+    recvs,
+    local,
+    p_sends,
+    p_recvs,
+    p_local,
+):
+    z, y, x, c = place()
+    f = 2 * z + y
+    r = 2 * x + c
+    feats = slab(feat_ref, feats_ref, sends.at[0], recvs.at[0], local.at[0])
+    small = by_columns(small_ref, full_ref, sends.at[1], recvs.at[1], local.at[1])
+    plans = [(0, GATHER_STEPS, feats), (0, GATHER_STEPS, small)]
+    for layer in range(depth):
+        n = 2 + 2 * layer
+        plans.append(
+            (1 + 2 * layer, GATHER_STEPS, by_columns(own_in_ref.at[layer], w_in_ref.at[layer], sends.at[n], recvs.at[n], local.at[n]))
+        )
+        plans.append(
+            (
+                2 + 2 * layer,
+                GATHER_STEPS,
+                by_rows(own_out_ref.at[layer], w_out_ref.at[layer], sends.at[n + 1], recvs.at[n + 1], local.at[n + 1]),
+            )
+        )
+    others = [{"fsdp": lax.rem(f + k, 8)} for k in range(1, 8)]
+    greet(others + [device(z, y, 1 - x, c), device(z, y, x, 1 - c)])
+    last = max(first + count for first, count, _ in plans)
     copies = []
-    for k in range(1, count):
-        copies.append(remote(x_ref.at[lax.rem(me + k, count)], got.at[me], sends.at[k - 1], recvs.at[k - 1], peers[k - 1]))
-        copies[-1].start()
+    for tick in range(last):
+        for first, count, piece in plans:
+            if 0 <= tick - first < count:
+                piece.step(tick - first)
+        if tick != GATHER_STEPS - 1:
+            continue
+        rows = feats_ref[...].reshape(SLOTS, feats_ref.shape[-1])
+        feat = rows[:, :FREQ].astype(BF16)
+        label = rows[:, FREQ : FREQ + 1]
+        place_of = lax.broadcasted_iota(jnp.int32, (SLOTS, C_T1), 1).astype(F32)
+        picked = jnp.where(label == place_of, 1.0, 0.0).astype(BF16)
+        time1 = dot(feat, full_ref[:, C_T1:C_T2], NT) + top_ref[0:1, :]
+        s1 = silu(time1).astype(BF16)
+        before = dot(s1, full_ref[:, C_T2 : C_T2 + D]) + top_ref[1:2, :] + dot(picked, full_ref[:, :C_T1], NT)
+        cond = silu(before)
+        cond_rows[...] = cond
+        mine = pl.ds(pl.multiple_of(f * OWN, OWN), OWN)
+        time1_ref[...] = time1.T
+        wide[...] = s1.astype(F32).T
+        s1_ref[...] = wide[mine, :].astype(BF16)
+        wide[...] = before.T
+        before_ref[...] = wide[mine, :]
+        wide[...] = cond.T
+        cond_ref[...] = wide[mine, :].astype(BF16)
+        pick = lax.broadcasted_iota(jnp.int32, (D, OWN), 0) == f * OWN + lax.broadcasted_iota(jnp.int32, (D, OWN), 1)
+        group = cond_rows[pl.ds(pl.multiple_of(r * 64, 64), 64), :].astype(BF16)
+        group = dot(group, jnp.where(pick, 1.0, 0.0).astype(BF16)).astype(BF16)
+        for k in range(kinds):
+            part[:, k] = dot(group, w_mods_ref[:, k * D : (k + 1) * D]).reshape(8, 8, D)
+        for k in range(1, 8):
+            copies.append(remote(part.at[lax.rem(f + k, 8)], got.at[f], p_sends.at[k - 1], p_recvs.at[k - 1], others[k - 1]))
+            copies[-1].start()
+        own = pltpu.make_async_copy(part.at[f], got.at[f], p_local)
+        own.start()
     own.wait()
     for copy in copies:
         copy.wait()
     total = got[0]
-    for k in range(1, count):
+    for k in range(1, 8):
         total = total + got[k]
-    out_ref[...] = total
-
-
-def swap_sum(x, ident):
-    count = x.shape[0]
+    for k in range(kinds):
+        mods_ref[k] = total[k] + bias_ref[:, k * D : (k + 1) * D]
+    mods_ref[kinds:] = jnp.zeros_like(mods_ref[kinds:])
+
+
+def prologue(small, feat, w_mods, top, bias, own_in, own_out):
+    depth = own_in.shape[0]
+    kinds = w_mods.shape[1] // D
+    shape = jax.ShapeDtypeStruct
+    anyspace = pl.BlockSpec(memory_space=pl.ANY)
     vm = pl.BlockSpec(memory_space=pltpu.VMEM)
+    dma = pltpu.SemaphoreType.DMA
+    n = 2 + 2 * depth
     return pl.pallas_call(
-        functools.partial(swap_kernel, count),
-        out_shape=jax.ShapeDtypeStruct(x.shape[1:], x.dtype),
-        in_specs=[vm],
-        out_specs=vm,
+        functools.partial(prologue_kernel, depth, kinds),
+        out_shape=(
+            shape((D, C_ALL), BF16),
+            shape((depth, D, own_in.shape[2]), BF16),
+            shape((depth, 8, 4, OWN, D), BF16),
+            shape((16, 8, D), F32),
+            shape((D, SLOTS), F32),
+            shape((OWN, SLOTS), BF16),
+            shape((OWN, SLOTS), F32),
+            shape((OWN, SLOTS), BF16),
+            shape((4, 8) + feat.shape, F32),
+        ),
+        in_specs=[anyspace, vm, vm, vm, vm, anyspace, anyspace],
+        out_specs=(vm,) * 9,
         scratch_shapes=[
-            pltpu.VMEM(x.shape, x.dtype),
-            pltpu.SemaphoreType.DMA((count - 1,)),
-            pltpu.SemaphoreType.DMA((count - 1,)),
-            pltpu.SemaphoreType.DMA,
+            pltpu.VMEM((8, kinds, 8, D), F32),
+            pltpu.VMEM((8, kinds, 8, D), F32),
+            pltpu.VMEM((SLOTS, D), F32),
+            pltpu.VMEM((D, SLOTS), F32),
+            dma((n, 10)),
+            dma((n, 10)),
+            dma((n,)),
+            dma((7,)),
+            dma((7,)),
+            dma,
         ],
-        compiler_params=pltpu.CompilerParams(collective_id=ident, has_side_effects=True),
-        name="step_swap",
-    )(x)
+        compiler_params=pltpu.CompilerParams(collective_id=2, has_side_effects=True, vmem_limit_bytes=60 * 1024 * 1024),
+        name="step_prologue",
+    )(small, feat, w_mods, top, bias, own_in, own_out)
+
+
+E_PATCH, E_T1, E_T2, E_FIN, E_HEAD, E_ALL = 1024, 1152, 1408, 1792, 2560, 2688
+STAT = 1792
+
+
+def column_of(row):
+    n = row.shape[1]
+    same = lax.broadcasted_iota(jnp.int32, (n, n), 0) == lax.broadcasted_iota(jnp.int32, (n, n), 1)
+    return jnp.sum(jnp.where(same, row, 0.0), axis=1, keepdims=True)
+
+
+def row_of(column):
+    n = column.shape[0]
+    same = lax.broadcasted_iota(jnp.int32, (n, n), 0) == lax.broadcasted_iota(jnp.int32, (n, n), 1)
+    return jnp.sum(jnp.where(same, column, 0.0), axis=0, keepdims=True)
+
+
+def total_of(v):
+    return jnp.sum(rows_sum(v), axis=1, keepdims=True)
+
+
+def update_kernel(
+    sizes,
+    out_t_ref,
+    out_m_ref,
+    sums_ref,
+    d_mods_ref,
+    cond_ref,
+    before_ref,
+    time1_ref,
+    s1_ref,
+    feats_ref,
+    time2_ref,
+    w_mods_ref,
+    in_ref,
+    down_ref,
+    edge_ref,
+    lbias_ref,
+    tbias_ref,
+    in_rows_ref,
+    in_cols_ref,
+    down_rows_ref,
+    down_cols_ref,
+    edge_rows_ref,
+    edge_cols_ref,
+    lbias_v_ref,
+    tbias_v_ref,
+    in_new,
+    down_new,
+    edge_new,
+    lbias_new,
+    tbias_new,
+    in_rows_new,
+    in_cols_new,
+    down_rows_new,
+    down_cols_new,
+    edge_rows_new,
+    edge_cols_new,
+    lbias_v_new,
+    tbias_v_new,
+    tail_ref,
+    g_in,
+    g_down,
+    g_edge,
+    d_time2,
+    d_time1,
+    small_t,
+    stats,
+    squares,
+    sends,
+    recvs,
+):
+    classes, tokens = sizes
+    depth = in_ref.shape[0]
+    kinds = w_mods_ref.shape[1] // D
+    fin = 6 * depth
+    f = lax.axis_index("fsdp")
+    others = [{"fsdp": lax.rem(f + k, 8)} for k in range(1, 8)]
+    scale = 1.0 / (PATCH_IN * math.sqrt(tokens))
+    mine = pl.ds(pl.multiple_of(f * OWN, OWN), OWN)
+    greet(others)
+
+    def share(n, buffer):
+        copies = []
+        for k in range(1, 8):
+            copies.append(remote(buffer.at[f], buffer.at[f], sends.at[n, k - 1], recvs.at[n, k - 1], others[k - 1]))
+            copies[-1].start()
+        return copies
+
+    d_cond = jnp.zeros((OWN, SLOTS), F32)
+    ones = jnp.ones((8, SLOTS), BF16)
+    for k in range(kinds):
+        rows = d_mods_ref[:, :, k].astype(F32).reshape(SLOTS, D).astype(BF16)
+        g = dot(cond_ref[...], rows) * scale
+        b = dot(ones, rows)[0:1] * scale
+        if k < fin:
+            layer, at = k // 6, (k % 6) * D
+            g_in[layer, :, at : at + D] = g
+            lbias_new[layer : layer + 1, at : at + D] = b
+        else:
+            at = (k - fin) * D
+            g_edge[:, E_FIN + at : E_FIN + at + D] = g
+            tbias_new[:, 3 * D + at : 3 * D + at + D] = b
+        d_cond = d_cond + dot(w_mods_ref[:, k * D : (k + 1) * D], rows, NT)
+    d_before = d_cond * silu_slope(before_ref[...])
+    d_time2[f] = d_before.astype(BF16)
+    copies = share(0, d_time2)
+    rows = feats_ref[...].reshape(SLOTS, feats_ref.shape[-1])
+    feat = rows[:, :FREQ].astype(BF16)
+    label = rows[:, FREQ : FREQ + 1]
+    picked = jnp.where(label == lax.broadcasted_iota(jnp.int32, (SLOTS, E_PATCH), 1).astype(F32), 1.0, 0.0).astype(BF16)
+    top = d_before.astype(BF16)
+    left = d_before - top.astype(F32)
+    middle = left.astype(BF16)
+    low = (left - middle.astype(F32)).astype(BF16)
+    g_edge[:, 0:E_PATCH] = (dot(top, picked) + dot(middle, picked) + dot(low, picked)) * scale
+    small_t[:, 0 : 2 * PATCH_IN] = sums_ref[0 : 2 * PATCH_IN, :].T * scale
+    own_small = small_t[mine, :]
+    lane = lax.broadcasted_iota(jnp.int32, (OWN, 128), 1)
+    g_edge[:, E_PATCH:E_T1] = jnp.where(lane < PATCH_IN, own_small, 0.0)
+    g_edge[:, E_HEAD:E_ALL] = jnp.where(lane < PATCH_IN, pltpu.roll(own_small, 128 - PATCH_IN, 1), 0.0)
+    for layer in range(depth):
+        for q in range(4):
+            g_in[layer, :, 6 * D + q * D : 7 * D + q * D] = out_t_ref[layer, q] * scale
+            g_in[layer, :, 10 * D + q * D : 11 * D + q * D] = out_m_ref[layer, q, :, 0:D] * scale
+            g_down[layer, q * OWN : (q + 1) * OWN, :] = out_m_ref[layer, q, :, D : 2 * D] * scale
+    for copy in copies:
+        copy.wait()
+    d2 = d_time2[...].reshape(D, SLOTS)
+    g_edge[:, E_T2:E_FIN] = dot(s1_ref[...], d2, NT) * scale
+    d1 = (dot(time2_ref[...], d2) * silu_slope(time1_ref[...])).astype(BF16)
+    d_time1[...] = d1
+    g_edge[:, E_T1:E_T2] = dot(d_time1[mine, :], feat) * scale
+    tbias_new[:, D : 2 * D] = dot(ones, d1, NT)[0:1] * scale
+    tbias_new[:, 2 * D : 3 * D] = dot(ones, d2, NT)[0:1] * scale
+    tbias_new[:, 0:D] = sums_ref[S_BPATCH : S_BPATCH + 1, :] * scale
+    tail = tbias_new.shape[1]
+    tbias_new[:, 5 * D : tail] = jnp.zeros((1, tail - 5 * D), F32)
+    tbias_new[:, 5 * D : 5 * D + PATCH_IN] = sums_ref[S_BHEAD : S_BHEAD + 1, 0:PATCH_IN] * scale
+    for layer in range(depth):
+        for j in range(8):
+            row = S_BIAS + 8 * layer + j
+            lbias_new[layer : layer + 1, 6 * D + j * D : 7 * D + j * D] = sums_ref[row : row + 1, :] * scale
+
+    wide = in_ref.shape[2]
+    rows_in, rows_down = [], []
+    for layer in range(depth):
+        s = jnp.zeros((OWN, 1), F32)
+        for t in range(wide // STAT):
+            g = g_in[layer, :, t * STAT : (t + 1) * STAT]
+            g2 = g * g
+            s = s + jnp.sum(g2, axis=1, keepdims=True)
+            stats[f, wide // STAT * layer + t : wide // STAT * layer + t + 1, :] = rows_sum(g2)
+        new = decay * column_of(in_rows_ref[layer : layer + 1, :]) + (1.0 - decay) * (s / wide + eps_stat)
+        rows_in.append(new)
+        in_rows_new[layer : layer + 1, :] = row_of(new)
+        g = g_down[layer]
+        g2 = g * g
+        new = decay * column_of(down_rows_ref[layer : layer + 1, :]) + (1.0 - decay) * (
+            jnp.sum(g2, axis=1, keepdims=True) / D + eps_stat
+        )
+        rows_down.append(new)
+        down_rows_new[layer : layer + 1, :] = row_of(new)
+        stats[f, 7:8, E_ALL - STAT + layer * D : E_ALL - STAT + (layer + 1) * D] = rows_sum(g2)
+    g = g_edge[...]
+    g2 = g * g
+    rows_edge = decay * column_of(edge_rows_ref[...]) + (1.0 - decay) * (
+        jnp.sum(g2, axis=1, keepdims=True) / classes + eps_stat
+    )
+    edge_rows_new[...] = row_of(rows_edge)
+    g2 = rows_sum(g2)
+    stats[f, 6:7, :] = g2[:, 0:STAT]
+    stats[f, 7:8, 0 : E_ALL - STAT] = g2[:, STAT:E_ALL]
+    lane = lax.broadcasted_iota(jnp.int32, (1, 128), 1)
+    totals = jnp.zeros((1, 128), F32)
+    every = rows_in + rows_down + [rows_edge]
+    for n, v in enumerate(every):
+        totals = jnp.where(lane == n, rows_sum(v), totals)
+    spot = E_ALL - STAT + depth * D
+    stats[f, 7:8, spot : spot + 128] = totals
+    copies = share(1, stats)
+
+    def plain_rows(weight, new, old_v, new_v, columns):
+        g = new[...]
+        moment = decay * old_v[...] + (1.0 - decay) * (g * g + eps_stat)
+        u = g * lax.rsqrt(moment)
+        root = jnp.sqrt(jnp.sum(u * u, axis=1, keepdims=True) / columns)
+        new_v[...] = moment
+        new[...] = weight[...] - rate * u / jnp.maximum(1.0, root / clip_level)
+
+    plain_rows(lbias_ref, lbias_new, lbias_v_ref, lbias_v_new, wide)
+    plain_rows(tbias_ref, tbias_new, tbias_v_ref, tbias_v_new, 5 * D + 2 * PATCH_IN)
+    loss = jnp.sum(sums_ref[S_SSE : S_SSE + 1, 0:PATCH_IN], axis=1, keepdims=True) / (tokens * PATCH_IN)
+
+    for copy in copies:
+        copy.wait()
+    full = stats[0]
+    for k in range(1, 8):
+        full = full + stats[k]
+    height = 8.0 * OWN
+    tall = 4.0 * height
+
+    def factors(rows_col, total, count, cols):
+        return lax.rsqrt(rows_col / (total / count)), lax.rsqrt(cols)
+
+    squared = jnp.zeros((1, 128), F32)
+    used = []
+    for layer in range(depth):
+        total = full[7:8, spot + layer : spot + layer + 1]
+        s = jnp.zeros((1, 1), F32)
+        for t in range(wide // STAT):
+            at = slice(t * STAT, (t + 1) * STAT)
+            line = wide // STAT * layer + t
+            cols = decay * in_cols_ref[layer : layer + 1, at] + (1.0 - decay) * (full[line : line + 1, :] / height + eps_stat)
+            in_cols_new[layer : layer + 1, at] = cols
+            a, b = factors(rows_in[layer], total, height, cols)
+            u = g_in[layer, :, at] * a * b
+            g_in[layer, :, at] = u
+            s = s + total_of(u * u)
+        squared = jnp.where(lane == layer, s, squared)
+        at = E_ALL - STAT + layer * D
+        cols = decay * down_cols_ref[layer : layer + 1, :] + (1.0 - decay) * (full[7:8, at : at + D] / tall + eps_stat)
+        down_cols_new[layer : layer + 1, :] = cols
+        total = full[7:8, spot + depth + layer : spot + depth + layer + 1]
+        a, b = factors(rows_down[layer], total, tall, cols)
+        u = g_down[layer] * a * b
+        g_down[layer] = u
+        squared = jnp.where(lane == depth + layer, total_of(u * u), squared)
+    cols = jnp.concatenate([full[6:7, :], full[7:8, 0 : E_ALL - STAT]], axis=1)
+    cols = decay * edge_cols_ref[...] + (1.0 - decay) * (cols / height + eps_stat)
+    edge_cols_new[...] = cols
+    a, b = factors(rows_edge, full[7:8, spot + 2 * depth : spot + 2 * depth + 1], height, cols)
+    u = g_edge[...] * a * b
+    g_edge[...] = u
+    squared = jnp.where(lane == 2 * depth, total_of(u * u), squared)
+    squares[f] = jnp.broadcast_to(squared, (8, 128))
+    for copy in share(2, squares):
+        copy.wait()
+    full = squares[0]
+    for k in range(1, 8):
+        full = full + squares[k]
+    full = full[0:1, :]
+    counts = jnp.where(lane < depth, height * wide, jnp.where(lane < 2 * depth, tall * D, height * classes))
+    roots = jnp.sqrt(full / counts)
+    step = rate / jnp.maximum(1.0, roots / clip_level)
+    tail_ref[...] = jnp.where(lane == 2 * depth + 1, loss, roots)
+    for layer in range(depth):
+        in_new[layer] = in_ref[layer] - step[:, layer : layer + 1] * g_in[layer]
+        down_new[layer] = down_ref[layer] - step[:, depth + layer : depth + layer + 1] * g_down[layer]
+    edge_new[...] = edge_ref[...] - step[:, 2 * depth : 2 * depth + 1] * g_edge[...]
+
+
+def update(sizes, out_t, out_m, sums, d_mods, cond, before, time1, s1, feats, time2, w_mods, weights, stats):
+    shape = jax.ShapeDtypeStruct
+    vm = pl.BlockSpec(memory_space=pltpu.VMEM)
+    dma = pltpu.SemaphoreType.DMA
+    inputs = (out_t, out_m, sums, d_mods, cond, before, time1, s1, feats, time2, w_mods) + weights + stats
+    outs = tuple(shape(v.shape, F32) for v in weights + stats) + (shape((1, 128), F32),)
+    return pl.pallas_call(
+        functools.partial(update_kernel, sizes),
+        out_shape=outs,
+        in_specs=[vm] * len(inputs),
+        out_specs=(vm,) * len(outs),
+        scratch_shapes=[
+            pltpu.VMEM(weights[0].shape, F32),
+            pltpu.VMEM(weights[1].shape, F32),
+            pltpu.VMEM(weights[2].shape, F32),
+            pltpu.VMEM((8, OWN, SLOTS), BF16),
+            pltpu.VMEM((D, SLOTS), BF16),
+            pltpu.VMEM((D, 128), F32),
+            pltpu.VMEM((8, 8, STAT), F32),
+            pltpu.VMEM((8, 8, 128), F32),
+            dma((3, 7)),
+            dma((3, 7)),
+        ],
+        compiler_params=pltpu.CompilerParams(collective_id=3, has_side_effects=True, vmem_limit_bytes=60 * 1024 * 1024),
+        name="step_update",
+    )(*inputs)
 
 
 def mix_weights(tsteps):
@@ -839,25 +1191,12 @@
     return jnp.concatenate([jnp.cos(angles), jnp.sin(angles)], axis=1)
 
 
-def fetch(layer_in, layer_out, direct):
+def fetch(layer_in, layer_out):
     own_in = layer_in[:, :, 6 * D :].astype(BF16)
     own_out = layer_out.astype(BF16)
-    depth = layer_in.shape[0]
-    if direct:
-        items = []
-        for layer in range(depth):
-            items.append(("columns", own_in[layer]))
-            items.append(("rows", own_out[layer].reshape(4, OWN, D)))
-        got = gather(items, 2)
-        return jnp.stack(got[0::2]), jnp.stack([v.reshape(FF, D) for v in got[1::2]])
     w_in = lax.all_gather(own_in, "fsdp", axis=1, tiled=True)
     w_out = lax.all_gather(own_out, "fsdp", axis=1, tiled=True)
     return w_in, w_out
-
-
-def silu_slope(x):
-    gate = jax.nn.sigmoid(x)
-    return gate * (1.0 + x * (1.0 - gate))
 
 
 def matmul(a, b, form):
@@ -876,7 +1215,7 @@
     return (weight - rate * update / jnp.maximum(1.0, root / clip_level), moment_new)
 
 
-def shards(
+def library_step(
     latents,
     tsteps,
     labels,
@@ -902,7 +1241,6 @@
     at_f = lax.axis_index("fsdp")
     at_r = lax.axis_index("rep")
     every = images * fsdp * rep
-    direct = (fsdp, rep, own) == (8, 4, OWN)
     width = own * fsdp
     MOD = 6 * D
     start_freq = NCLS + PATCH_IN
@@ -910,24 +1248,16 @@
 
     edge_low = edge_mat.astype(BF16)
     small = jnp.concatenate([edge_low[:, : start_tail + D], edge_low[:, start_tail + 3 * D :]], axis=1)
-    if direct:
-        small = jnp.pad(small, ((0, 0), (0, -small.shape[1] % 512)))
-        full = gather([("columns", small)], 3)[0]
-    else:
-        full = lax.all_gather(small, "fsdp", axis=0, tiled=True)
+    full = lax.all_gather(small, "fsdp", axis=0, tiled=True)
     class_cols = full[:, :NCLS]
     patch_cols = full[:, NCLS:start_freq]
     freq_cols = full[:, start_freq:start_tail]
     time_second = full[:, start_tail : start_tail + D]
     head_cols = full[:, start_tail + D : start_tail + D + PATCH_IN]
-    if direct:
-        both = jnp.pad(jnp.stack([tsteps, labels]), ((0, 6), (0, 128 - images)))
-        both = exchange(both, ("fsdp", "rep"), fsdp * rep, 4)
-        all_tsteps = both[:, 0, :images].reshape(every)
-        all_labels = both[:, 1, :images].reshape(every)
-    else:
-        all_tsteps = lax.all_gather(tsteps, ("fsdp", "rep"), axis=0, tiled=True)
-        all_labels = lax.all_gather(labels, ("fsdp", "rep"), axis=0, tiled=True)
+    all_tsteps, all_labels = (
+        lax.all_gather(tsteps, ("fsdp", "rep"), axis=0, tiled=True),
+        lax.all_gather(labels, ("fsdp", "rep"), axis=0, tiled=True),
+    )
     features = time_features(all_tsteps).astype(BF16)
     time1 = matmul(features, freq_cols, "bf,df->bd") + top_bias[D : 2 * D]
     s1 = jax.nn.silu(time1).astype(BF16)
@@ -946,25 +1276,22 @@
     group_own = lax.dynamic_index_in_dim(cond_own.reshape(fsdp, rep, images, own), at_r, axis=1, keepdims=False)
     part = matmul(group_own.reshape(fsdp * images, own), w_mods, "bd,de->be")
     bias_mods = jnp.concatenate([layer_bias[layer, :MOD] for layer in range(depth)] + [top_bias[3 * D : 5 * D]])
+    mods = lax.psum_scatter(part, "fsdp", scatter_dimension=0, tiled=True) + bias_mods
     kinds = 6 * depth + 2
-    if direct:
-        mods = swap_sum(jnp.pad(part.reshape(fsdp, images, kinds * D), ((0, 0), (0, 8 - images), (0, 0))), 5)[:images]
-    else:
-        mods = lax.psum_scatter(part, "fsdp", scatter_dimension=0, tiled=True)
-    mods = (mods + bias_mods).reshape(images, kinds, D)
+    mods = mods.reshape(images, kinds, D)
 
     alphas = mix_weights(tsteps)
     noisy = jnp.sqrt(alphas)[:, None, None] * latents + jnp.sqrt(1.0 - alphas)[:, None, None] * noise
     patches = patchify(noisy).astype(BF16).reshape(images * TOK, PATCH_IN)
     target = patchify(noise).reshape(images * TOK, PATCH_IN)
 
-    w_in, w_out = fetch(layer_in, layer_out, direct)
+    w_in, w_out = fetch(layer_in, layer_out)
     bias_rows = jnp.concatenate([layer_bias[:, MOD : MOD + D], layer_bias[:, MOD + D :]], axis=1)
-    g_in, g_out, g_patch, g_head, g_bias, g_bpatch, g_bhead, g_mods, sse = compute(
+    g_in, g_out, sums, d_mods = compute(
         patches,
         target,
         position_table(),
-        jnp.pad(mods, ((0, 0), (0, 16 - kinds), (0, 0))),
+        jnp.transpose(jnp.pad(mods, ((0, 8 - images), (0, 16 - kinds), (0, 0))), (1, 0, 2)),
         w_in,
         w_out,
         patch_cols,
@@ -972,70 +1299,30 @@
         bias_rows,
         top_bias[None, :D],
         top_bias[None, 5 * D : 5 * D + PATCH_IN],
-        blocked=direct,
-    )
-
-    d_mods = g_mods[:, :kinds].astype(BF16).reshape(images, kinds * D)
-    if direct:
-        d_mods = exchange(jnp.pad(d_mods.reshape(-1, 128), ((0, 4), (0, 0))), ("fsdp", "rep"), fsdp * rep, 6)
-        d_mods = d_mods[:, : images * kinds * D // 128].reshape(every, kinds * D)
-    else:
-        d_mods = lax.all_gather(d_mods, ("fsdp", "rep"), axis=0, tiled=True)
+    )
+
+    d_mods = jnp.transpose(d_mods, (1, 0, 2))[:images, :kinds].reshape(images, kinds * D)
+    d_mods = lax.all_gather(d_mods, ("fsdp", "rep"), axis=0, tiled=True)
     g_rows = matmul(cond_own, d_mods, "bd,be->de")
     g_bmods = jnp.sum(d_mods.astype(F32), axis=0)
     d_before = matmul(d_mods, w_mods, "be,de->bd") * silu_slope(own_part(before))
     g_class = jnp.einsum("bd,bc->dc", d_before, picked.astype(F32), precision=lax.Precision.HIGHEST)
-    d_time2 = d_before.astype(BF16)
-    if direct:
-        d_time2 = exchange(jnp.pad(d_time2, ((0, 0), (0, 128 - own))), ("fsdp",), fsdp, 7)
-        d_time2 = jnp.transpose(d_time2[:, :, :own], (1, 0, 2)).reshape(every, width)
-    else:
-        d_time2 = lax.all_gather(d_time2, "fsdp", axis=1, tiled=True)
+    d_time2 = lax.all_gather(d_before.astype(BF16), "fsdp", axis=1, tiled=True)
     g_time2 = matmul(own_part(s1), d_time2, "bd,be->de")
     d_time1 = (matmul(d_time2, time_second, "be,de->bd") * silu_slope(time1)).astype(BF16)
     g_time1 = matmul(own_part(d_time1), features, "bd,bf->df")
 
-    if direct:
-        parts = (g_patch, g_head, g_bias, g_bpatch, g_bhead, sse)
-        flat = jnp.concatenate([v.reshape(-1) for v in parts])
-        flat = jnp.pad(flat, (0, 32 * 1024 - flat.shape[0])).reshape(4, 4, 2, 8, 128)
-        out_t, out_m, out_s = reduce_grads(g_in, g_out, flat)
-
-        def joined(v):
-            return jnp.transpose(v, (0, 2, 1, 3)).reshape(depth, own, 4 * D)
-
-        shard_in = jnp.concatenate([joined(out_t), joined(out_m[..., :D])], axis=2)
-        shard_out = out_m[..., D:].reshape(depth, 4 * own, D)
-        flat = jnp.transpose(exchange(out_s, ("fsdp",), fsdp, 8), (1, 0, 2, 3)).reshape(-1)
-        sums = []
-        at = 0
-        for v in parts:
-            sums.append(flat[at : at + v.size].reshape(v.shape))
-            at += v.size
-        g_patch, g_head, g_bias, g_bpatch, g_bhead, sse = sums
-    else:
-        shard_in = lax.psum(lax.psum_scatter(g_in, "fsdp", scatter_dimension=1, tiled=True), "rep")
-        shard_out = lax.psum(lax.psum_scatter(g_out, "fsdp", scatter_dimension=1, tiled=True), "rep")
-        g_patch, g_head, g_bias, g_bpatch, g_bhead, sse = lax.psum(
-            (g_patch, g_head, g_bias, g_bpatch, g_bhead, sse), ("fsdp", "rep")
-        )
-
-    def over_fsdp(values, ident):
-        if not direct:
-            return lax.psum(values, "fsdp")
-        flat = jnp.concatenate([v.reshape(-1) for v in values])
-        flat = jnp.pad(flat, (0, -flat.shape[0] % 1024)).reshape(-1, 128)
-        flat = jnp.sum(exchange(flat, ("fsdp",), fsdp, ident), axis=0).reshape(-1)
-        sums = []
-        at = 0
-        for v in values:
-            sums.append(flat[at : at + v.size].reshape(v.shape))
-            at += v.size
-        return sums
+    shard_in = lax.psum(lax.psum_scatter(g_in, "fsdp", scatter_dimension=1, tiled=True), "rep")
+    shard_out = lax.psum(lax.psum_scatter(g_out, "fsdp", scatter_dimension=1, tiled=True), "rep")
+    sums = lax.psum(sums, ("fsdp", "rep"))
+    g_patch, g_head = sums[:S_HEAD], sums[S_HEAD:S_BIAS]
+    g_bias = sums[S_BIAS:S_BPATCH].reshape(depth, BW)
+    g_bpatch, g_bhead = sums[S_BPATCH : S_BPATCH + 1], sums[S_BHEAD : S_BHEAD + 1, :PATCH_IN]
+    sse = jnp.sum(sums[S_SSE, :PATCH_IN])
 
     tok_total = every * TOK
     scale_grad = 1.0 / (PATCH_IN * math.sqrt(tok_total))
-    loss = sse[0, 0] / (tok_total * PATCH_IN)
+    loss = sse / (tok_total * PATCH_IN)
     fin = depth * MOD
     grad_edge = jnp.concatenate(
         [
@@ -1072,7 +1359,7 @@
     rows_in_new = decay * in_rows + (1.0 - decay) * jnp.mean(square_in, axis=2)
     rows_out_new = decay * out_rows + (1.0 - decay) * jnp.mean(square_out, axis=2)
     rows_edge_new = decay * edge_rows[None] + (1.0 - decay) * jnp.mean(square_edge, axis=2)
-    col_in, total_in, col_out, total_out, col_edge, total_edge = over_fsdp(
+    col_in, total_in, col_out, total_out, col_edge, total_edge = lax.psum(
         (
             jnp.sum(square_in, axis=1),
             jnp.sum(rows_in_new, axis=1),
@@ -1081,7 +1368,7 @@
             jnp.sum(square_edge, axis=1),
             jnp.sum(rows_edge_new, axis=1),
         ),
-        9,
+        "fsdp",
     )
     cols_in_new = decay * in_cols + (1.0 - decay) * col_in / full_rows_in
     cols_out_new = decay * out_cols + (1.0 - decay) * col_out / full_rows_out
@@ -1089,13 +1376,13 @@
     update_in = step_of(grad_in, rows_in_new, cols_in_new, total_in / full_rows_in)
     update_out = step_of(grad_out, rows_out_new, cols_out_new, total_out / full_rows_out)
     update_edge = step_of(grad_edge, rows_edge_new, cols_edge_new, total_edge / full_rows_edge)
-    sum_in, sum_out, sum_edge = over_fsdp(
+    sum_in, sum_out, sum_edge = lax.psum(
         (
             jnp.sum(update_in * update_in, axis=(1, 2)),
             jnp.sum(update_out * update_out, axis=(1, 2)),
             jnp.sum(update_edge * update_edge, axis=(1, 2)),
         ),
-        10,
+        "fsdp",
     )
     roots_in = jnp.sqrt(sum_in / (full_rows_in * grad_in.shape[2]))
     roots_out = jnp.sqrt(sum_out / (full_rows_out * grad_out.shape[2]))
@@ -1128,6 +1415,156 @@
     )
 
 
+def direct_step(
+    latents,
+    tsteps,
+    labels,
+    noise,
+    layer_in,
+    layer_out,
+    edge_mat,
+    layer_bias,
+    top_bias,
+    in_rows,
+    in_cols,
+    out_rows,
+    out_cols,
+    edge_rows,
+    edge_cols,
+    layer_bias_v,
+    top_bias_v,
+):
+    images = latents.shape[0]
+    depth = layer_in.shape[0]
+    MOD = 6 * D
+    tokens = images * 32 * TOK
+    classes = edge_mat.shape[1]
+    start_freq = NCLS + PATCH_IN
+    start_tail = start_freq + FREQ
+
+    def wide_to(v, width, fill=0.0):
+        return jnp.pad(v, ((0, 0), (0, width - v.shape[1])), constant_values=fill)
+
+    def aligned(v, fill):
+        return jnp.concatenate(
+            [
+                wide_to(v[:, :NCLS], E_PATCH, fill),
+                wide_to(v[:, NCLS:start_freq], E_T1 - E_PATCH, fill),
+                v[:, start_freq : start_tail + 3 * D],
+                wide_to(v[:, start_tail + 3 * D :], E_ALL - E_HEAD, fill),
+            ],
+            axis=1,
+        )
+
+    edge_a = aligned(edge_mat, 0.0)
+    edge_low = edge_a.astype(BF16)
+    small = jnp.concatenate(
+        [
+            edge_low[:, :E_PATCH],
+            edge_low[:, E_T1:E_FIN],
+            edge_low[:, E_PATCH : E_PATCH + PATCH_IN],
+            edge_low[:, E_HEAD : E_HEAD + PATCH_IN],
+            jnp.zeros((OWN, C_ALL - C_HEAD - PATCH_IN), BF16),
+        ],
+        axis=1,
+    )
+    w_mods = jnp.concatenate([layer_in[layer, :, :MOD].astype(BF16) for layer in range(depth)] + [edge_low[:, E_FIN:E_HEAD]], axis=1)
+    feat = jnp.concatenate(
+        [time_features(tsteps), jnp.broadcast_to(labels.astype(F32)[:, None], (images, 128))], axis=1
+    )
+    feat = jnp.pad(feat, ((0, 8 - images), (0, 0)))
+    bias_mods = jnp.concatenate([layer_bias[layer, :MOD] for layer in range(depth)] + [top_bias[3 * D : 5 * D]])[None]
+    full, w_in, w_out, mods, time1, s1, before, cond, feats = prologue(
+        small,
+        feat,
+        w_mods,
+        top_bias[D : 3 * D].reshape(2, D),
+        bias_mods,
+        layer_in[:, :, MOD:].astype(BF16),
+        layer_out.astype(BF16).reshape(depth, 4, OWN, D),
+    )
+
+    alphas = mix_weights(tsteps)
+    noisy = jnp.sqrt(alphas)[:, None, None] * latents + jnp.sqrt(1.0 - alphas)[:, None, None] * noise
+    patches = patchify(noisy).astype(BF16).reshape(images * TOK, PATCH_IN)
+    target = patchify(noise).reshape(images * TOK, PATCH_IN)
+    bias_rows = jnp.concatenate([layer_bias[:, MOD : MOD + D], layer_bias[:, MOD + D :]], axis=1)
+    g_t, g_m, sums, d_mods = compute(
+        patches,
+        target,
+        position_table(),
+        mods,
+        w_in,
+        w_out.reshape(depth, FF, D),
+        full[:, C_PATCH : C_PATCH + PATCH_IN],
+        full[:, C_HEAD : C_HEAD + PATCH_IN].T,
+        bias_rows,
+        top_bias[None, :D],
+        top_bias[None, 5 * D : 5 * D + PATCH_IN],
+        blocked=True,
+    )
+    out_t, out_m, sums, d_mods = reduce_grads(g_t, g_m, sums, d_mods)
+    weights = (layer_in, layer_out, edge_a, layer_bias, wide_to(top_bias[None], 16 * 128))
+    stats = (
+        in_rows,
+        in_cols,
+        out_rows,
+        out_cols,
+        edge_rows[None],
+        aligned(edge_cols[None], 1.0),
+        layer_bias_v,
+        wide_to(top_bias_v[None], 16 * 128, 1.0),
+    )
+    (
+        in_new,
+        out_new,
+        edge_new,
+        lbias_new,
+        tbias_new,
+        in_rows_new,
+        in_cols_new,
+        out_rows_new,
+        out_cols_new,
+        edge_rows_new,
+        edge_cols_new,
+        lbias_v_new,
+        tbias_v_new,
+        tail,
+    ) = update(
+        (classes, tokens), out_t, out_m, sums, d_mods, cond, before, time1, s1, feats, full[:, C_T2 : C_T2 + D], w_mods, weights, stats
+    )
+
+    def natural(v):
+        return jnp.concatenate(
+            [v[:, :NCLS], v[:, E_PATCH : E_PATCH + PATCH_IN], v[:, E_T1 : E_HEAD + 2 * PATCH_IN]], axis=1
+        )
+
+    count = top_bias.shape[0]
+    return (
+        tail[0, 2 * depth + 1],
+        in_new,
+        out_new,
+        natural(edge_new),
+        lbias_new,
+        tbias_new[0, :count],
+        in_rows_new,
+        in_cols_new,
+        out_rows_new,
+        out_cols_new,
+        edge_rows_new[0],
+        natural(edge_cols_new)[0],
+        lbias_v_new,
+        tbias_v_new[0, :count],
+        tail[0, : 2 * depth + 1],
+    )
+
+
+def shards(*arrays):
+    layer_in = arrays[4]
+    mesh = (lax.axis_size("fsdp"), lax.axis_size("rep"), layer_in.shape[0], layer_in.shape[1])
+    return (direct_step if mesh == (8, 4, 2, OWN) else library_step)(*arrays)
+
+
 def solution(mesh):
     placed = (
         P(("fsdp", "rep"), None, None),

time: 601 us -> 407 us (0.68); the launches traced: 591 us -> 404 us
  Pallas kernels: 448 us -> 345 us
  other arithmetic: 58 us -> 11.8 us
  local copies, waits for them, and re-layouts: 67 us -> 45.8 us
  matrix products: 12.8 us -> 0 us
    pallas_call x9 -> x2, Pallas kernels: 228 us -> 115 us  [the longest x1 78.3 us: prologue(): pl.pallas_call(functools.partial(prologue_kernel, depth, kinds), out_shap...]
    reduce_sum x14 -> x0, other arithmetic: 21.6 us -> none  [the longest x2 3.03 us: over_fsdp(): flat = jnp.sum(exchange(flat, ('fsdp',), fsdp, ident), axis=0).reshape(-1)]
    pallas_call x1, Pallas kernels: 75.7 us -> 90.6 us  [reduce_grads(): pl.pallas_call(functools.partial(reduce_kernel, depth), out_shape=(shape(...]
    dot_general x10 -> x0, matrix products: 12.8 us -> none  [the longest x9 12.3 us: matmul(): return jnp.einsum(form, a, b, preferred_element_type=F32)]
    reshape x15 -> x2, local copies, waits for them, and re-layouts: 12.3 us -> 0.59 us  [the longest x1 0.59 us: direct_step(): top_bias[D:3 * D].reshape(2, D)]
    sub x5 -> x0, other arithmetic: 9.22 us -> none  [the longest x2 2.8 us: plain(): weight - rate * update / jnp.maximum(1.0, root / clip_level)]
    another operation x7 -> x4, other arithmetic: 7.68 us -> 0.49 us  [the longest x1 5.19 us: fetch(): jnp.stack(got[0::2])]
    slice x20 -> x24, local copies, waits for them, and re-layouts: 13.1 us -> 16.2 us  [the longest x1 1.7 us: direct_step(): full[:, C_T2:C_T2 + D]]
where the time goes in v3:
time: 407 us; the launch traced here: 404 us
  Pallas kernels  345 us (85%)
  local copies, waits for them, and re-layouts  45.8 us (11%)
  other arithmetic  11.8 us (3%)
    pallas_call x1, Pallas kernels, compute(): pl.pallas_call(functools.partial(compute_kernel, images, group, blocked),...  139 us
    pallas_call x1, Pallas kernels, reduce_grads(): pl.pallas_call(functools.partial(reduce_kernel, depth), out_shape=(shape(...  90.6 us
    pallas_call x1, Pallas kernels, prologue(): pl.pallas_call(functools.partial(prologue_kernel, depth, kinds), out_shap...  78.3 us
    pallas_call x1, Pallas kernels, update(): pl.pallas_call(functools.partial(update_kernel, sizes), out_shape=outs, i...  36.8 us

profile of v3, /device:TPU:0, one launch (start us, length us, event | category | flops | bytes accessed | tf_op | source)
XLA Modules:
  0.0 403.8 jit_solution(13611246019792973173)
XLA Ops:
  2.0 1.2 slice_bitcast_fusion.4.bhead_ref
  6.8 1.3 pad.47.tbias_v_ref
  8.1 1.3 pad.43.tbias_ref
  13.0 1.3 concatenate.36.bias_ref
  17.5 1.0 add_convert_fusion
  18.6 0.9 slice_select_fusion
  19.5 1.1 slice.128
  23.7 1.0 multiply_sine_fusion.1
  24.7 1.0 pad_maximum_fusion.1.pos_ref
  26.2 2.5 copy.43
  32.6 2.2 copy.45
  35.2 1.2 copy.48.target_ref
  36.4 78.3 %step_prologue.1 = (bf16[384,2048]{1,0:T(8,128)(2,1)}, bf16[2,384,3072]{2,1,0:T(8,128)(2,1)}, bf16[2,8,4,48,384]{4,3,2,1,0:T(8,128)(2,1)}, f32[16,8,384]{2,1,0:T...) custom-call(bf16[48,2048]{1,0:T(8,128)(2,1)} %concatenate.32.small_r, ...), custom_call_target="tpu_custom_call" | custom-call | tf_op jit(solution)/shard_map/step_prologue/pallas_call | solution.py:846
  114.7 1.5 slice.142.w_patch_ref
  116.2 1.7 slice.146.time2_ref
  117.9 1.9 copy.46
  120.4 139.4 %step_compute.1 = (f32[2,4,384,384]{3,2,1,0:T(8,128)}, f32[2,4,384,768]{3,2,1,0:T(8,128)}, f32[56,384]{1,0:T(8,128)}, bf16[16,8,384]{2,1,0:T(8,128)(2,1)}) custom-call(bf16[1536,16]{1,0:T(8,128)(2,1)} %copy.47.patches_ref, f32[1536,16]{1,0:T(8,128)} %copy.48.target_ref, f32[256,384]{1,0:T(8,128)} %pad_maximum_fusion.1.pos_ref, ...), custom_call_target="tpu_custom_call" | custom-call | tf_op jit(solution)/shard_map/step_compute/pallas_call | solution.py:395
  259.8 90.6 %step_reduce.1 = (f32[2,4,48,384]{3,2,1,0:T(8,128)}, f32[2,4,48,768]{3,2,1,0:T(8,128)}, f32[56,384]{1,0:T(8,128)}, bf16[4,8,16,8,384]{4,3,2,1,0:T(8,128)(2,1)}) custom-call(f32[2,4,4,2,48,384]{5,4,3,2,1,0:T(8,128)} %bitcast.43, f32[2,4,4,2,48,768]{5,4,3,2,1,0:T(8,128)} %bitcast.41, f32[56,384]{1,0:T(8,128)} %get-tuple-element.52.s_ref, ...), custom_call_target="tpu_custom_call" | custom-call | tf_op jit(solution)/shard_map/step_reduce/pallas_call | solution.py:712
  350.4 36.8 %step_update.1 = (f32[2,48,5376]{2,1,0:T(8,128)}, f32[2,192,384]{2,1,0:T(8,128)}, f32[48,2688]{1,0:T(8,128)}, f32[2,5376]{1,0:T(2,128)}, f32[1,2048]{1,0:T(1,128...) custom-call(f32[2,4,48,384]{3,2,1,0:T(8,128)} %get-tuple-element.54., ...), custom_call_target="tpu_custom_call" | custom-call | tf_op jit(solution)/shard_map/step_update/pallas_call | solution.py:1135
  387.2 1.3 slice.151
  388.6 1.1 slice_bitcast_fusion.3
  393.2 0.9 slice.152
  394.2 1.0 slice.154
  396.2 1.3 copy.60
  (98 shorter events, 30.8 us)
Async XLA Ops:
  0.6 22.3 %copy-start.1 = (f32[2,192,384]{2,1,0:T(8,128)S(1)}, f32[2,192,384]{2,1,0:T(8,128)}, u32[]{:S(2)}) copy-start(f32[2,192,384]{2,1,0:T(8,128)} %down_ref.1) | copy-start | bytes 1769476
  24.7 5.4 %copy-start = (f32[2,48,5376]{2,1,0:T(8,128)S(1)}, f32[2,48,5376]{2,1,0:T(8,128)}, u32[]{:S(2)}) copy-start(f32[2,48,5376]{2,1,0:T(8,128)} %in_ref.1) | copy-start | bytes 6193156
  30.1 1.0 copy-start.5
  30.2 1.7 copy-start.4
  387.2 8.9 %copy-start.2 = (f32[2,48,5376]{2,1,0:T(8,128)S(1)}, f32[2,48,5376]{2,1,0:T(8,128)}, u32[]{:S(2)}) copy-start(f32[2,48,5376]{2,1,0:T(8,128)} %get-tuple-element.115) | copy-start | bytes 6193156
  396.1 1.4 copy-start.3
  396.1 2.2 copy-start.8
  396.1 2.8 copy-start.10
  396.1 3.4 copy-start.13
  396.1 4.0 copy-start.7
  396.1 4.6 %copy-start.12 = (f32[2,192]{1,0:T(2,128)S(1)}, f32[2,192]{1,0:T(2,128)}, u32[]{:S(2)}) copy-start(f32[2,192]{1,0:T(2,128)} %get-tuple-element.122) | copy-start | bytes 4612
  396.1 5.2 %copy-start.11 = (f32[2,384]{1,0:T(2,128)S(1)}, f32[2,384]{1,0:T(2,128)}, u32[]{:S(2)}) copy-start(f32[2,384]{1,0:T(2,128)} %get-tuple-element.123) | copy-start | bytes 9220
  396.1 5.7 %copy-start.14 = (f32[1,48]{1,0:T(1,128)S(1)}, f32[1,48]{1,0:T(1,128)}, u32[]{:S(2)}) copy-start(f32[1,48]{1,0:T(1,128)} %get-tuple-element.73) | copy-start | bytes 580
  396.1 6.2 %copy-start.6 = (f32[2,5376]{1,0:T(2,128)S(1)}, f32[2,5376]{1,0:T(2,128)}, u32[]{:S(2)}) copy-start(f32[2,5376]{1,0:T(2,128)} %get-tuple-element.126) | copy-start | bytes 129028
  396.2 6.8 %copy-start.9 = (f32[1,2048]{1,0:T(1,128)S(1)}, f32[1,2048]{1,0:T(1,128)}, u32[]{:S(2)}) copy-start(f32[1,2048]{1,0:T(1,128)} %get-tuple-element.76) | copy-start | bytes 24580

commit v4 on v3

--- a/solution.py
+++ b/solution.py
@@ -3,6 +3,7 @@
 
 import jax
 import jax.numpy as jnp
+import numpy as np
 from jax import lax
 from jax.experimental import pallas as pl
 from jax.experimental.pallas import tpu as pltpu
@@ -74,42 +75,55 @@
 S_HEAD, S_BIAS, S_BPATCH, S_BHEAD, S_SSE, S_ROWS = 16, 32, 48, 49, 50, 56
 
 
-def compute_kernel(
-    images,
-    group,
-    blocked,
-    patches_ref,
-    target_ref,
-    pos_ref,
-    mods_ref,
-    w_in_ref,
-    w_out_ref,
-    w_patch_ref,
-    w_head_ref,
-    bias_ref,
-    bpatch_ref,
-    bhead_ref,
-    g_in_ref,
-    g_out_ref,
-    sums_ref,
-    g_mods_ref,
-    tok,
-    mid,
-    qkv,
-    att,
-    branch,
-    outb,
-    normed,
-    act,
-    dinner,
-    dsmall,
-    dqkv,
-    stage,
-    mod_sums,
-    sems,
-):
+class BiasRows:
+    def __init__(self, ref):
+        self.ref = ref
+
+    def __getitem__(self, layer):
+        return self.ref[layer][:, 6 * D :]
+
+
+class BiasRows:
+    def __init__(self, ref):
+        self.ref = ref
+
+    def __getitem__(self, layer):
+        return self.ref[layer][:, 6 * D :]
+
+
+class BiasRows:
+    def __init__(self, ref):
+        self.ref = ref
+
+    def __getitem__(self, layer):
+        return self.ref[layer][:, 6 * D :]
+
+
+class BiasRows:
+    def __init__(self, ref):
+        self.ref = ref
+
+    def __getitem__(self, layer):
+        return self.ref[layer][:, 6 * D :]
+
+
+def compute_kernel(images, group, direct, *refs):
+    refs = list(refs)
+
+    def take(count):
+        got = refs[:count]
+        del refs[:count]
+        return got
+
+    patches_ref, target_ref, pos_ref, mods_ref, first_in_ref, first_out_ref, w_patch_ref, w_head_ref = take(8)
+    lbias_ref, tbias_ref = take(2)
+    own_in_ref, own_out_ref = take(2) if direct else (None,) * 2
+    g_in_ref, g_out_ref, sums_ref, g_mods_ref = take(4)
+    out_t_ref, out_m_ref, out_d_ref = take(3) if direct else (None,) * 3
+    w_in_ref, w_out_ref, tok, mid, qkv, att, branch, outb, normed, act, dinner, dsmall, stage, mod_sums, sems, w_sems = take(16)
     steps = images // group
     crow = group * TOK
+    depth = lbias_ref.shape[0]
     lane = lax.broadcasted_iota(jnp.int32, (TOK, 128), 1)
     first_half = lane < HEAD_DIM
 
@@ -119,26 +133,138 @@
     def chunk_of(i):
         return pl.ds(pl.multiple_of(i * crow, crow), crow)
 
+    def near(j):
+        return slice(j * TOK, (j + 1) * TOK)
+
+    def down_rows(layer, c):
+        rows = FF // w_out_ref.shape[1]
+        return w_out_ref[layer, c // rows : (c + FFC) // rows].reshape(FFC, D)
+
     def mod_row(b, k):
         return mods_ref[k, pl.ds(b, 1), :]
 
+    loads = []
+    for layer in range(1 if direct else depth):
+        source = first_in_ref, first_out_ref
+        if not direct:
+            source = first_in_ref.at[layer], first_out_ref.at[layer]
+        for n, (ours, theirs) in enumerate(zip((w_in_ref, w_out_ref), source)):
+            loads.append(pltpu.make_async_copy(theirs, ours.at[layer], w_sems.at[2 * layer + n]))
+            loads[-1].start()
+    bias_ref = BiasRows(lbias_ref)
+
     sums_ref[...] = jnp.zeros_like(sums_ref)
     mod_sums[...] = jnp.zeros_like(mod_sums)
 
     def add_bias(layer, first, value):
         for at in range(0, value.shape[1], D):
-            row = S_BIAS + 8 * layer + (first + at) // D
-            sums_ref[row : row + 1, :] += value[:, at : at + D]
+            row = (first + at) // D
+            sums_ref[S_BIAS // 8 + layer, row : row + 1, :] += value[:, at : at + D]
 
     def put_mod(b, k, value):
         mod_sums[k, pl.ds(b, 1), :] = value
 
-    depth = w_in_ref.shape[0]
+    if direct:
+        wide_m, wide_t = take(4), take(4)
+        plane = take(2 * depth)
+        s_got, r_sends, r_recvs, r_loads, g_sends, g_recvs, g_local, b_sends, b_recvs, w_sends, w_recvs, w_local = take(12)
+        partners = Partners().all()
+        greet(partners)
+        m_pieces, t_pieces = [], []
+        for layer in range(depth):
+            for kind, (pieces, source, out, wide) in enumerate(
+                ((m_pieces, g_out_ref, out_m_ref, wide_m), (t_pieces, g_in_ref, out_t_ref, wide_t))
+            ):
+                n = 2 * layer + kind
+                pieces.append(
+                    Reducer(source.at[layer], list(wide) + [plane[n]], out.at[layer], r_sends.at[n], r_recvs.at[n], r_loads.at[n])
+                )
+        w_pieces = []
+        for layer in range(1, depth):
+            own, ours = own_in_ref.at[layer], w_in_ref.at[layer]
+
+            def sems_of(n, first=3 * (layer - 1)):
+                return w_sends.at[first + n], w_recvs.at[first + n], w_local.at[first + n]
+
+            w_pieces.append(by_columns(own, ours, *sems_of(0), 0, 4 * D))
+            w_pieces.append(by_columns(own, ours, *sems_of(1), 4 * D, FF))
+            w_pieces.append(by_rows(own_out_ref.at[layer], w_out_ref.at[layer], *sems_of(2)))
+        s_piece = Butterfly(sums_ref, s_got, b_sends, b_recvs)
+        d_pieces = []
+        for n, (low, high) in enumerate(((0, 6 * (depth - 1)), (6 * (depth - 1), 6 * depth + 2))):
+            d_pieces.append(
+                Gatherer(
+                    lambda q, a=low, b=high: g_mods_ref.at[a:b],
+                    lambda f, q, a=low, b=high: out_d_ref.at[q, f, a:b],
+                    lambda q, a=low, b=high: out_d_ref.at[q, :, a:b],
+                    g_sends.at[n],
+                    g_recvs.at[n],
+                    g_local.at[n],
+                )
+            )
+
+    def send_mods(low, high):
+        g_mods_ref[low:high] = mod_sums[low:high].astype(BF16)
+
+    def in_moves(layer, first):
+        moves = []
+        for q in range(4):
+            source = stage.at[0, :, q * D : (q + 1) * D]
+            if direct:
+                target = (g_in_ref if first == QKV else g_out_ref).at[layer, q, :, 0:D]
+            else:
+                target = g_in_ref.at[layer, :, first + q * D : first + (q + 1) * D]
+            moves.append(pltpu.make_async_copy(source, target, sems.at[0, q]))
+        return moves
+
+    def down_moves(layer):
+        moves = []
+        for c in range(4):
+            if not direct:
+                source = stage.at[1, :, c * D : (c + 1) * D]
+                target = g_out_ref.at[layer, c * D : (c + 1) * D, :]
+                moves.append(pltpu.make_async_copy(source, target, sems.at[1, c]))
+                continue
+            for owner in range(2):
+                for q in range(4):
+                    start = owner * (D // 2) + q * OWN
+                    source = stage.at[1, start : start + OWN, c * D : (c + 1) * D]
+                    begin = (2 * c + owner) * OWN
+                    target = g_out_ref.at[layer, q, begin : begin + OWN, D : 2 * D]
+                    moves.append(pltpu.make_async_copy(source, target, sems.at[1, len(moves)]))
+        return moves
+
+    def start(moves):
+        for move in moves:
+            move.start()
+
+    def finish(moves):
+        for move in moves:
+            move.wait()
+
+    def clear(slot):
+        @pl.loop(0, FF // D)
+        def _(c):
+            stage[slot, :, pl.ds(pl.multiple_of(c * D, D), D)] = jnp.zeros((D, D), F32)
+
+    def at(li, i, *actions):
+        if not direct:
+            return
+
+        def place_at(turn_li, turn_i):
+            for want_li, want_i, todo in actions:
+
+                @pl.when(jnp.logical_and(turn_li == want_li, turn_i == want_i))
+                def _():
+                    for piece, k in todo:
+                        piece.step(k)
+
+        place_at(li, i)
 
     @pl.loop(0, images)
     def _(b):
         r = rows_of(b)
-        tok[0, r, :] = dot(patches_ref[r, :], w_patch_ref[...], NT) + bpatch_ref[...] + pos_ref[...]
+        tok[0, r, :] = dot(patches_ref[r, :], w_patch_ref[...], NT) + tbias_ref[:, 0:D] + pos_ref[...]
 
     def half(v, which):
         zero = jnp.zeros_like(v)
@@ -160,43 +286,65 @@
         n, scale = norm_rows(t)
         return n, scale, (n * (1.0 + mod_row(b, k + 1)) + mod_row(b, k)).astype(BF16)
 
-    for layer in range(depth):
+    for load in loads:
+        load.wait()
+    if direct:
+        w_a, w_f, w_o = w_pieces
+
+    @pl.loop(0, depth)
+    def _(layer):
         mo = layer * 6
 
         @pl.loop(0, steps)
         def _(i):
+            if direct:
+                at(
+                    layer,
+                    i,
+                    (0, 0, [(w_a, 0), (w_f, 0)]),
+                    (0, 1, [(w_a, 2), (w_f, 1), (w_o, 1)]),
+                    (1, 0, [(w_a, 4)]),
+                )
             cr = chunk_of(i)
+            bias = bias_ref[layer]
             for j in range(group):
                 b = i * group + j
-                r = rows_of(b)
-                normed[r, :] = modulated(tok[layer, r, :], b, mo)[2]
-            hc = normed[cr, :]
+                normed[near(j), :] = modulated(tok[layer, rows_of(b), :], b, mo)[2]
+            hc = normed[...]
             p = dot(hc, w_in_ref[layer, :, QKV : QKV + 2 * D])
-            qkv[layer, cr, 0:D] = (p[:, 0:D] + bias_ref[layer : layer + 1, BQ : BQ + D]).astype(BF16)
+            qkv[layer, cr, 0:D] = (p[:, 0:D] + bias[:, BQ : BQ + D]).astype(BF16)
             qkv[layer, cr, D : 2 * D] = p[:, D : 2 * D].astype(BF16)
             p = dot(hc, w_in_ref[layer, :, QKV + 2 * D : QKV + 3 * D])
-            qkv[layer, cr, 2 * D : 3 * D] = (p + bias_ref[layer : layer + 1, BV : BV + D]).astype(BF16)
+            qkv[layer, cr, 2 * D : 3 * D] = (p + bias[:, BV : BV + D]).astype(BF16)
             for j in range(group):
                 attention(layer, rows_of(i * group + j))
-            br = dot(att[layer, cr, :], w_in_ref[layer, :, WO : WO + D]) + bias_ref[layer : layer + 1, BO : BO + D]
+            if direct:
+                at(
+                    layer,
+                    i,
+                    (0, 0, [(w_a, 1), (w_o, 0)]),
+                    (0, 1, [(w_a, 3), (w_f, 2), (w_o, 2)]),
+                    (1, 0, [(w_f, 3), (w_o, 3), (w_f, 4), (w_o, 4)]),
+                )
+            br = dot(att[layer, cr, :], w_in_ref[layer, :, WO : WO + D]) + bias[:, BO : BO + D]
             branch[layer, cr, :] = br.astype(BF16)
             for j in range(group):
                 b = i * group + j
                 r = rows_of(b)
-                t2 = tok[layer, r, :] + mod_row(b, mo + 2) * br[j * TOK : (j + 1) * TOK]
+                t2 = tok[layer, r, :] + mod_row(b, mo + 2) * br[near(j)]
                 mid[layer, r, :] = t2
-                normed[r, :] = modulated(t2, b, mo + 3)[2]
-            mc = normed[cr, :]
-            out = jnp.zeros((crow, D), F32) + bias_ref[layer : layer + 1, BF2 : BF2 + D]
+                normed[near(j), :] = modulated(t2, b, mo + 3)[2]
+            mc = normed[...]
+            out = jnp.zeros((crow, D), F32) + bias[:, BF2 : BF2 + D]
             for c in range(0, FF, FFC):
-                x = dot(mc, w_in_ref[layer, :, WF1 + c : WF1 + c + FFC]) + bias_ref[layer : layer + 1, BF1 + c : BF1 + c + FFC]
+                x = dot(mc, w_in_ref[layer, :, WF1 + c : WF1 + c + FFC]) + bias[:, BF1 + c : BF1 + c + FFC]
                 a = (x * (0.5 * (1.0 + gelu_parts(x)))).astype(BF16)
-                out = out + dot(a, w_out_ref[layer, c : c + FFC, :])
+                out = out + dot(a, down_rows(layer, c))
             outb[layer, cr, :] = out.astype(BF16)
             for j in range(group):
                 b = i * group + j
                 r = rows_of(b)
-                tok[layer + 1, r, :] = mid[layer, r, :] + mod_row(b, mo + 5) * out[j * TOK : (j + 1) * TOK]
+                tok[layer + 1, r, :] = mid[layer, r, :] + mod_row(b, mo + 5) * out[near(j)]
 
     dtok = tok.at[depth]
 
@@ -205,114 +353,98 @@
         r = rows_of(b)
         k = 6 * depth
         n, scale, n3 = modulated(dtok[r, :], b, k)
-        miss = dot(n3, w_head_ref[...], NT) + bhead_ref[...] - target_ref[r, :]
-        sums_ref[S_SSE : S_SSE + 1, 0:PATCH_IN] += rows_sum(miss * miss)
+        miss = dot(n3, w_head_ref[...]) + tbias_ref[:, 5 * D : 5 * D + PATCH_IN] - target_ref[r, :]
+        sums_ref[S_SSE // 8, S_SSE % 8 : S_SSE % 8 + 1, 0:PATCH_IN] += rows_sum(miss * miss)
         dp = (2.0 * miss).astype(BF16)
-        sums_ref[S_HEAD : S_HEAD + PATCH_IN, :] += dot(dp, n3, TN)
-        sums_ref[S_BHEAD : S_BHEAD + 1, 0:PATCH_IN] += rows_sum(dp.astype(F32))
-        dn3 = dot(dp, w_head_ref[...])
+        sums_ref[S_HEAD // 8 : S_HEAD // 8 + 2] += dot(dp, n3, TN).reshape(2, 8, D)
+        sums_ref[S_BHEAD // 8, S_BHEAD % 8 : S_BHEAD % 8 + 1, 0:PATCH_IN] += rows_sum(dp.astype(F32))
+        dn3 = dot(dp, w_head_ref[...], NT)
         put_mod(b, k, rows_sum(dn3))
         put_mod(b, k + 1, rows_sum(dn3 * n))
         dtok[r, :] = norm_back(dn3 * (1.0 + mod_row(b, k + 1)), n, scale)
 
-    pending = {}
-
-    def free(slot):
-        for copy in pending.pop(slot, ()):
-            copy.wait()
-
-    def send_in(layer, first):
-        slot = 0
-        moves = []
-        for q in range(4):
-            source = stage.at[slot, :, q * D : (q + 1) * D]
-            if blocked:
-                target = (g_in_ref if first == QKV else g_out_ref).at[layer, q, :, 0:D]
-            else:
-                target = g_in_ref.at[layer, :, first + q * D : first + (q + 1) * D]
-            moves.append(pltpu.make_async_copy(source, target, sems.at[slot, q]))
-        for move in moves:
-            move.start()
-        pending[slot] = moves
-
-    def send_down(layer):
-        slot = 1
-        moves = []
-        for c in range(4):
-            if not blocked:
-                source = stage.at[slot, :, c * D : (c + 1) * D]
-                target = g_out_ref.at[layer, c * D : (c + 1) * D, :]
-                moves.append(pltpu.make_async_copy(source, target, sems.at[slot, c]))
-                continue
-            for owner in range(2):
-                for q in range(4):
-                    start = owner * (D // 2) + q * OWN
-                    source = stage.at[slot, start : start + OWN, c * D : (c + 1) * D]
-                    begin = (2 * c + owner) * OWN
-                    target = g_out_ref.at[layer, q, begin : begin + OWN, D : 2 * D]
-                    moves.append(pltpu.make_async_copy(source, target, sems.at[slot, len(moves)]))
-        for move in moves:
-            move.start()
-        pending[slot] = moves
-
-    for layer in reversed(range(depth)):
+    if direct:
+        t_last, m_last = t_pieces[depth - 1], m_pieces[depth - 1]
+        t_first, m_first = t_pieces[0], m_pieces[0]
+        d_first, d_last = d_pieces
+
+    @pl.loop(0, depth)
+    def _(li):
+        layer = depth - 1 - li
         mo = layer * 6
-        lb = slice(layer, layer + 1)
+        bias = bias_ref[layer]
+
+        @pl.when(li > 0)
+        def _():
+            finish(in_moves(layer + 1, QKV))
+            send_mods(6 * (depth - 1), 6 * depth + 2)
+
+        clear(0)
+        clear(1)
 
         @pl.loop(0, steps)
         def _(i):
+            if direct:
+                at(li, i, (1, 0, [(m_last, 2), (t_last, 0), (d_last, 0)]), (1, 1, [(t_last, 1)]))
             cr = chunk_of(i)
             for j in range(group):
                 b = i * group + j
                 r = rows_of(b)
-                normed[r, :] = modulated(mid[layer, r, :], b, mo + 3)[2]
+                normed[near(j), :] = modulated(mid[layer, r, :], b, mo + 3)[2]
                 d = dtok[r, :]
                 put_mod(b, mo + 5, rows_sum(d * outb[layer, r, :].astype(F32)))
                 do = (d * mod_row(b, mo + 5)).astype(BF16)
-                dsmall[r, :] = do
+                dsmall[near(j), :] = do
                 add_bias(layer, BF2, rows_sum(do.astype(F32)))
-            mc = normed[cr, :]
-            do = dsmall[cr, :]
+            mc = normed[...]
+            do = dsmall[...]
             dm = jnp.zeros((crow, D), F32)
             for c in range(0, FF, FFC):
-                x = dot(mc, w_in_ref[layer, :, WF1 + c : WF1 + c + FFC]) + bias_ref[lb, BF1 + c : BF1 + c + FFC]
+                x = dot(mc, w_in_ref[layer, :, WF1 + c : WF1 + c + FFC]) + bias[:, BF1 + c : BF1 + c + FFC]
                 x2 = x * x
                 t = jnp.tanh(GELU_A * (x + GELU_B * (x2 * x)))
                 cdf = 0.5 * (1.0 + t)
-                act[cr, c : c + FFC] = (x * cdf).astype(BF16)
+                act[:, c : c + FFC] = (x * cdf).astype(BF16)
                 slope = cdf + (0.5 * GELU_A) * x * (1.0 - t * t) * (1.0 + (3.0 * GELU_B) * x2)
-                di = (dot(do, w_out_ref[layer, c : c + FFC, :], NT) * slope).astype(BF16)
-                dinner[cr, c : c + FFC] = di
+                di = (dot(do, down_rows(layer, c), NT) * slope).astype(BF16)
+                dinner[:, c : c + FFC] = di
                 add_bias(layer, BF1 + c, rows_sum(di.astype(F32)))
                 dm = dm + dot(di, w_in_ref[layer, :, WF1 + c : WF1 + c + FFC], NT)
             for j in range(group):
                 b = i * group + j
                 r = rows_of(b)
                 n, scale = norm_rows(mid[layer, r, :])
-                dmj = dm[j * TOK : (j + 1) * TOK]
+                dmj = dm[near(j)]
                 put_mod(b, mo + 3, rows_sum(dmj))
                 put_mod(b, mo + 4, rows_sum(dmj * n))
                 dtok[r, :] = dtok[r, :] + norm_back(dmj * (1.0 + mod_row(b, mo + 4)), n, scale)
 
-        free(0)
+            if direct:
+                at(li, i, (1, 0, [(d_last, 1)]), (1, 1, [(m_last, 3), (d_last, 2)]))
+
+            @pl.loop(0, FF // FFC)
+            def _(c):
+                cs = pl.ds(pl.multiple_of(c * FFC, FFC), FFC)
+                stage[0, :, cs] += dot(normed[...], dinner[:, cs], TN)
+
+            @pl.loop(0, FF // D)
+            def _(c):
+                cs = pl.ds(pl.multiple_of(c * D, D), D)
+                stage[1, :, cs] += dot(dsmall[...], act[:, cs], TN)
+
+        start(in_moves(layer, WF1))
 
         @pl.loop(0, FF // D)
         def _(c):
             cs = pl.ds(pl.multiple_of(c * D, D), D)
-            stage[0, :, cs] = dot(normed[...], dinner[:, cs], TN)
-
-        send_in(layer, WF1)
-        free(1)
-
-        @pl.loop(0, FF // D)
-        def _(c):
-            cs = pl.ds(pl.multiple_of(c * D, D), D)
-            stage[1, :, cs] = dot(dsmall[...], act[:, cs], TN).T
-
-        send_down(layer)
+            stage[1, :, cs] = stage[1, :, cs].T
+
+        start(down_moves(layer))
 
         @pl.loop(0, steps)
         def _(i):
+            if direct:
+                at(li, i, (1, 0, [(t_last, 2)]))
             cr = chunk_of(i)
             for j in range(group):
                 b = i * group + j
@@ -320,9 +452,18 @@
                 d = dtok[r, :]
                 put_mod(b, mo + 2, rows_sum(d * branch[layer, r, :].astype(F32)))
                 db = (d * mod_row(b, mo + 2)).astype(BF16)
-                dsmall[r, :] = db
+                dsmall[near(j), :] = db
                 add_bias(layer, BO, rows_sum(db.astype(F32)))
-            branch[layer, cr, :] = dot(dsmall[cr, :], w_in_ref[layer, :, WO : WO + D], NT).astype(BF16)
+            branch[layer, cr, :] = dot(dsmall[...], w_in_ref[layer, :, WO : WO + D], NT).astype(BF16)
+
+            @pl.when(i == 0)
+            def _():
+                finish(in_moves(layer, WF1))
+                finish(down_moves(layer))
+                clear(0)
+
+            if direct:
+                at(li, i, (0, 0, [(m_last, 0)]), (1, 0, [(m_last, 4)]), (1, 1, [(m_first, 1), (t_last, 4)]))
             for j in range(group):
                 r = rows_of(i * group + j)
                 for pair in range(HEADS // 2):
@@ -345,82 +486,149 @@
                     dq = (jnp.where(first_half, got[0][0], got[1][0]) * HEAD_DIM ** (-0.5)).astype(BF16)
                     dk = (jnp.where(first_half, got[0][1], got[1][1]) * HEAD_DIM ** (-0.5)).astype(BF16)
                     dv = jnp.where(first_half, got[0][2], got[1][2]).astype(BF16)
-                    dqkv[r, c : c + 128] = dq
-                    dqkv[r, D + c : D + c + 128] = dk
-                    dqkv[r, 2 * D + c : 2 * D + c + 128] = dv
-                    row = S_BIAS + 8 * layer
-                    sums_ref[row : row + 1, c : c + 128] += rows_sum(dq.astype(F32))
-                    sums_ref[row + 1 : row + 2, c : c + 128] += rows_sum(dv.astype(F32))
-            dh = dot(dqkv[cr, :], w_in_ref[layer, :, QKV : QKV + 3 * D], NT)
+                    qkv[layer, r, c : c + 128] = dq
+                    qkv[layer, r, D + c : D + c + 128] = dk
+                    qkv[layer, r, 2 * D + c : 2 * D + c + 128] = dv
+                    sums_ref[S_BIAS // 8 + layer, 0:1, c : c + 128] += rows_sum(dq.astype(F32))
+                    sums_ref[S_BIAS // 8 + layer, 1:2, c : c + 128] += rows_sum(dv.astype(F32))
+            if direct:
+                at(
+                    li,
+                    i,
+                    (0, 0, [(m_last, 1)]),
+                    (1, 0, [(m_last, 5), (m_first, 0), (t_last, 3), (d_last, 3)]),
+                    (1, 1, [(t_last, 5), (d_last, 4)]),
+                )
+            dh = dot(qkv[layer, cr, :], w_in_ref[layer, :, QKV : QKV + 3 * D], NT)
             for j in range(group):
                 b = i * group + j
                 r = rows_of(b)
                 n, scale, h = modulated(tok[layer, r, :], b, mo)
-                normed[r, :] = h
-                dhj = dh[j * TOK : (j + 1) * TOK]
+                normed[near(j), :] = h
+                dhj = dh[near(j)]
                 put_mod(b, mo, rows_sum(dhj))
                 put_mod(b, mo + 1, rows_sum(dhj * n))
                 dtok[r, :] = dtok[r, :] + norm_back(dhj * (1.0 + mod_row(b, mo + 1)), n, scale)
 
-        free(0)
-
-        @pl.loop(0, 3)
-        def _(c):
-            cs = pl.ds(pl.multiple_of(c * D, D), D)
-            stage[0, :, cs] = dot(normed[...], dqkv[:, cs], TN)
-
-        stage[0, :, 3 * D : 4 * D] = dot(att[layer], dsmall[...], TN)
-        send_in(layer, QKV)
-        free(1)
+            @pl.loop(0, 3)
+            def _(c):
+                cs = pl.ds(pl.multiple_of(c * D, D), D)
+                stage[0, :, cs] += dot(normed[...], qkv[layer, cr, cs], TN)
+
+            stage[0, :, 3 * D : 4 * D] += dot(att[layer, cr, :], dsmall[...], TN)
+
+        start(in_moves(layer, QKV))
+
+    if direct:
+        send_mods(0, 6 * (depth - 1))
+        d_first.step(0)
+        m_first.step(2)
+    else:
+        g_mods_ref[...] = mod_sums[...].astype(BF16)
 
     @pl.loop(0, images)
     def _(b):
         r = rows_of(b)
         d = dtok[r, :].astype(BF16)
-        sums_ref[S_BPATCH : S_BPATCH + 1, :] += rows_sum(d.astype(F32))
-        sums_ref[0:PATCH_IN, :] += dot(patches_ref[r, :], d, TN)
-
-    g_mods_ref[...] = mod_sums[...].astype(BF16)
-    free(0)
-
-
-def compute(patches, target, pos, mods, w_in, w_out, w_patch, w_head_t, bias, bpatch, bhead, group=3, blocked=False):
-    depth = w_in.shape[0]
+        sums_ref[S_BPATCH // 8, S_BPATCH % 8 : S_BPATCH % 8 + 1, :] += rows_sum(d.astype(F32))
+        sums_ref[0:2] += dot(patches_ref[r, :], d, TN).reshape(2, 8, D)
+
+    finish(in_moves(0, QKV))
+    if direct:
+        for piece, k in (
+            (t_first, 0),
+            (s_piece, 0),
+            (d_first, 1),
+            (t_first, 1),
+            (s_piece, 1),
+            (d_first, 2),
+            (s_piece, 2),
+            (t_first, 2),
+            (m_first, 3),
+            (d_first, 3),
+            (s_piece, 3),
+            (s_piece, 4),
+            (t_first, 3),
+            (d_first, 4),
+            (s_piece, 5),
+            (m_first, 4),
+            (t_first, 4),
+            (m_first, 5),
+            (t_first, 5),
+        ):
+            piece.step(k)
+
+
+def run_steps(plans):
+    last = max(first + count for first, count, _ in plans)
+    for tick in range(last):
+        for first, count, piece in plans:
+            if 0 <= tick - first < count:
+                piece.step(tick - first)
+
+
+def compute(patches, target, pos, mods, w_in, w_out, w_patch, w_head, lbias, tbias, own=(), group=3):
+    direct = len(own) > 0
+    depth = lbias.shape[0]
     rows = patches.shape[0]
     images = rows // TOK
+    crow = group * TOK
     kinds = mods.shape[0]
     vm = pl.BlockSpec(memory_space=pltpu.VMEM)
     anyspace = pl.BlockSpec(memory_space=pl.ANY)
     shape = jax.ShapeDtypeStruct
+    dma = pltpu.SemaphoreType.DMA
+    out_shape = [
+        shape((depth, 4, D, D) if direct else (depth, D, 4 * D + FF), F32),
+        shape((depth, 4, D, 2 * D) if direct else (depth, FF, D), F32),
+        shape((S_ROWS // 8, 8, D), F32),
+        shape((kinds, 8, D), BF16),
+    ]
+    out_specs = [anyspace, anyspace, vm, vm]
+    scratch = [
+        pltpu.VMEM((depth, D, 4 * D + FF), BF16),
+        pltpu.VMEM((depth,) + (w_out.shape if direct else w_out.shape[1:]), BF16),
+        pltpu.VMEM((depth + 1, rows, D), F32),
+        pltpu.VMEM((depth, rows, D), F32),
+        pltpu.VMEM((depth, rows, 3 * D), BF16),
+        pltpu.VMEM((depth, rows, D), BF16),
+        pltpu.VMEM((depth, rows, D), BF16),
+        pltpu.VMEM((depth, rows, D), BF16),
+        pltpu.VMEM((crow, D), BF16),
+        pltpu.VMEM((crow, FF), BF16),
+        pltpu.VMEM((crow, FF), BF16),
+        pltpu.VMEM((crow, D), BF16),
+        pltpu.VMEM((2, D, FF), F32),
+        pltpu.VMEM((kinds, 8, D), F32),
+        dma((2, 32)),
+        dma((2 * depth,)),
+    ]
+    params = dict(vmem_limit_bytes=67_043_328)
+    if direct:
+        out_shape += [
+            shape((depth, 4, OWN, D), F32),
+            shape((depth, 4, OWN, 2 * D), F32),
+            shape((4, 8, kinds, 8, D), BF16),
+        ]
+        out_specs += [vm, vm, anyspace]
+        scratch += wide_scratch(2 * D) + wide_scratch(D)
+        for _ in range(depth):
+            scratch += [pltpu.VMEM((8, OWN, 2 * D), BF16), pltpu.VMEM((8, OWN, D), BF16)]
+        count = 2 * depth
+        gathers = 3 * (depth - 1)
+        scratch += [pltpu.VMEM((5, S_ROWS // 8, 8, D), F32), dma((count, 13)), dma((count, 13)), dma((count, 2))]
+        scratch += [dma((2, 10)), dma((2, 10)), dma((2,)), dma((5,)), dma((5,))]
+        scratch += [dma((gathers, 10)), dma((gathers, 10)), dma((gathers,))]
+        params.update(collective_id=1, has_side_effects=True)
     return pl.pallas_call(
-        functools.partial(compute_kernel, images, group, blocked),
-        out_shape=(
-            shape((depth, 4, D, D) if blocked else (depth, D, 4 * D + FF), F32),
-            shape((depth, 4, D, 2 * D) if blocked else (depth, FF, D), F32),
-            shape((S_ROWS, D), F32),
-            shape((kinds, 8, D), BF16),
-        ),
-        in_specs=[vm] * 11,
-        out_specs=(anyspace, anyspace, vm, vm),
-        scratch_shapes=[
-            pltpu.VMEM((depth + 1, rows, D), F32),
-            pltpu.VMEM((depth, rows, D), F32),
-            pltpu.VMEM((depth, rows, 3 * D), BF16),
-            pltpu.VMEM((depth, rows, D), BF16),
-            pltpu.VMEM((depth, rows, D), BF16),
-            pltpu.VMEM((depth, rows, D), BF16),
-            pltpu.VMEM((rows, D), BF16),
-            pltpu.VMEM((rows, FF), BF16),
-            pltpu.VMEM((rows, FF), BF16),
-            pltpu.VMEM((rows, D), BF16),
-            pltpu.VMEM((rows, 3 * D), BF16),
-            pltpu.VMEM((2, D, FF), F32),
-            pltpu.VMEM((mods.shape[0], 8, D), F32),
-            pltpu.SemaphoreType.DMA((2, 32)),
-        ],
-        compiler_params=pltpu.CompilerParams(vmem_limit_bytes=60 * 1024 * 1024),
+        functools.partial(compute_kernel, images, group, direct),
+        out_shape=tuple(out_shape),
+        in_specs=[vm] * 4 + [anyspace] * 2 + [vm] * 4 + [anyspace] * len(own),
+        out_specs=tuple(out_specs),
+        scratch_shapes=scratch,
+        compiler_params=pltpu.CompilerParams(**params),
         name="step_compute",
-    )(patches, target, pos, mods, w_in, w_out, w_patch, w_head_t, bias, bpatch, bhead)
+    )(patches, target, pos, mods, w_in, w_out, w_patch, w_head, lbias[:, None, :], tbias, *own)
 
 
 def place():
@@ -453,108 +661,109 @@
 class Reducer:
     def __init__(self, source, bufs, out, sends, recvs, loads):
         self.source = source
-        self.keep, self.got0, self.sx, self.gotx, self.sy, self.goty, self.sz, self.gotz, self.sw, self.gotw = bufs
+        self.keep, self.got0, self.low, self.gotx, self.gotp = bufs
         self.out = out
         self.sends, self.recvs, self.loads = sends, recvs, loads
-        self.link = self.sx.dtype
-        self.z, self.y, self.x, self.c = place()
-        z, y, x, c = self.z, self.y, self.x, self.c
-        self.to_c = device(z, y, x, 1 - c)
-        self.to_x = device(z, y, 1 - x, c)
-        self.to_y = device(z, 1 - y, x, c)
-        self.z1 = z + 1 - 2 * lax.rem(z, 2)
-        self.z2 = lax.rem(z + 2, 4)
-        self.to_z1 = device(self.z1, y, x, c)
-        self.to_z2 = device(self.z2, y, x, c)
-        self.moves = {}
-
-    def send(self, slot, source, target, peer):
-        copy = remote(source, target, self.sends.at[slot], self.recvs.at[slot], peer)
-        copy.start()
-        self.moves[slot] = copy
+
+    def flat(self, ref, half):
+        return ref.at[half].reshape(D, ref.shape[-1])
+
+    def load(self, half):
+        c = place()[3]
+        return pltpu.make_async_copy(self.source.at[2 * half + c], self.flat(self.keep, half), self.loads.at[half])
+
+    def move(self, slot):
+        z, y, x, c = place()
+        mine = 2 * x + c
+        partners = Partners()
+        if slot < 2:
+            source, target, peer = self.source.at[2 * slot + 1 - c], self.flat(self.got0, slot), partners.c
+        elif slot == 2:
+            source, target, peer = self.low, self.gotx, partners.x
+        elif slot < 10:
+            f = lax.axis_index("fsdp")
+            to = lax.rem(f + slot - 2, 8)
+            source, target, peer = self.low.at[to], self.gotp.at[f], {"fsdp": to}
+        else:
+            peer = partners.x if slot == 10 else partners.c
+            source = target = self.out.at[2 * (1 - x) + c if slot == 12 else mine]
+        return remote(source, target, self.sends.at[slot], self.recvs.at[slot], peer)
 
     def step(self, k):
-        z, y, x, c = self.z, self.y, self.x, self.c
+        z, y, x, c = place()
+        f = 2 * z + y
         if k == 0:
             for half in range(2):
-                load = pltpu.make_async_copy(self.source.at[2 * half + c], self.keep.at[half], self.loads.at[half])
-                load.start()
-                self.moves["load", half] = load
-                self.send(half, self.source.at[2 * half + 1 - c], self.got0.at[half], self.to_c)
+                self.load(half).start()
+                self.move(half).start()
         if k == 1:
             for half in range(2):
-                self.moves["load", half].wait()
-                self.moves[half].wait()
-
-            @pl.loop(0, 4)
+                self.load(half).wait()
+                self.move(half).wait()
+
+            @pl.loop(0, 8)
             def _(i):
-                for j in range(2):
-                    self.sx[i, j] = (self.keep[1 - x, i, j] + self.got0[1 - x, i, j]).astype(self.link)
-
-            self.send(2, self.sx, self.gotx, self.to_x)
-
-            @pl.loop(0, 4)
+                self.low[i] = (self.keep[1 - x, i] + self.got0[1 - x, i]).astype(BF16)
+
+            self.move(2).start()
+
+            @pl.loop(0, 8)
             def _(i):
-                for j in range(2):
-                    self.keep[x, i, j] = self.keep[x, i, j] + self.got0[x, i, j]
+                self.keep[x, i] = self.keep[x, i] + self.got0[x, i]
         if k == 2:
-            self.moves[2].wait()
-
-            @pl.loop(0, 4)
+            self.move(2).wait()
+
+            @pl.loop(0, 8)
             def _(i):
-                self.sy[i] = (self.keep[x, i, 1 - y] + self.gotx[i, 1 - y].astype(F32)).astype(self.link)
-
-            self.send(3, self.sy, self.goty, self.to_y)
-
-            @pl.loop(0, 4)
-            def _(i):
-                self.keep[x, i, y] = self.keep[x, i, y] + self.gotx[i, y].astype(F32)
+                self.low[i] = (self.keep[x, i] + self.gotx[i].astype(F32)).astype(BF16)
+
+            for slot in range(3, 10):
+                self.move(slot).start()
+            self.keep[x, f] = self.keep[x, f] + self.gotx[f].astype(F32)
         if k == 3:
-            self.moves[3].wait()
-            for s in range(2):
-                at = lax.rem(self.z1 + 2 * s, 4)
-                self.sz[s] = (self.keep[x, at, y] + self.goty[at].astype(F32)).astype(self.link)
-            self.send(4, self.sz, self.gotz, self.to_z1)
-            for s in range(2):
-                at = lax.rem(z + 2 * s, 4)
-                self.keep[x, at, y] = self.keep[x, at, y] + self.goty[at].astype(F32)
+            for slot in range(3, 10):
+                self.move(slot).wait()
+            total = self.keep[x, f]
+            for d in range(1, 8):
+                total = total + self.gotp[lax.rem(f + d, 8)].astype(F32)
+            self.out[2 * x + c] = total
+            for slot in range(10, 12):
+                self.move(slot).start()
         if k == 4:
-            self.moves[4].wait()
-            self.sw[...] = (self.keep[x, self.z2, y] + self.gotz[1].astype(F32)).astype(self.link)
-            self.send(5, self.sw, self.gotw, self.to_z2)
+            self.move(10).wait()
+            self.move(12).start()
         if k == 5:
-            self.moves[5].wait()
-            mine = 2 * x + c
-            self.out[mine] = self.keep[x, z, y] + self.gotz[0].astype(F32) + self.gotw[...].astype(F32)
-            self.send(6, self.out.at[mine], self.out.at[mine], self.to_x)
-            self.send(7, self.out.at[mine], self.out.at[mine], self.to_c)
-        if k == 6:
-            self.moves[6].wait()
-            other = 2 * (1 - x) + c
-            self.send(8, self.out.at[other], self.out.at[other], self.to_c)
-        if k == 7:
-            self.moves[7].wait()
-            self.moves[8].wait()
-
-    def peers(self):
-        return [self.to_c, self.to_x, self.to_y, self.to_z1, self.to_z2]
-
-
-REDUCER_STEPS = 8
-
-
-def reducer_scratch(width, own=OWN, link=BF16):
+            self.move(11).wait()
+            self.move(12).wait()
+
+
+class Partners:
+    def __init__(self):
+        z, y, x, c = place()
+        self.c = device(z, y, x, 1 - c)
+        self.x = device(z, y, 1 - x, c)
+        self.y = device(z, 1 - y, x, c)
+        self.z1 = device(z + 1 - 2 * lax.rem(z, 2), y, x, c)
+        self.z2 = device(lax.rem(z + 2, 4), y, x, c)
+
+    def pairs(self):
+        return [self.c, self.x, self.y, self.z1, self.z2]
+
+    def all(self):
+        z, y, x, c = place()
+        f = 2 * z + y
+        return [self.c, self.x, device(z, y, 1 - x, 1 - c)] + [{"fsdp": lax.rem(f + k, 8)} for k in range(1, 8)]
+
+
+REDUCER_STEPS = 6
+
+
+def wide_scratch(width):
     return [
-        pltpu.VMEM((2, 4, 2, own, width), F32),
-        pltpu.VMEM((2, 4, 2, own, width), F32),
-        pltpu.VMEM((4, 2, own, width), link),
-        pltpu.VMEM((4, 2, own, width), link),
-        pltpu.VMEM((4, own, width), link),
-        pltpu.VMEM((4, own, width), link),
-        pltpu.VMEM((2, own, width), link),
-        pltpu.VMEM((2, own, width), link),
-        pltpu.VMEM((own, width), link),
-        pltpu.VMEM((own, width), link),
+        pltpu.VMEM((2, 8, OWN, width), F32),
+        pltpu.VMEM((2, 8, OWN, width), F32),
+        pltpu.VMEM((8, OWN, width), BF16),
+        pltpu.VMEM((8, OWN, width), BF16),
     ]
 
 
@@ -562,63 +771,61 @@
     def __init__(self, source, target, whole, sends, recvs, local):
         self.source, self.target, self.whole = source, target, whole
         self.sends, self.recvs, self.local = sends, recvs, local
-        self.z, self.y, self.x, self.c = place()
-        self.q = 2 * self.x + self.c
-        self.moves = {}
-
-    def send(self, slot, source, target, peer):
-        copy = remote(source, target, self.sends.at[slot], self.recvs.at[slot], peer)
-        copy.start()
-        self.moves[slot] = copy
+
+    def own(self):
+        z, y, x, c = place()
+        return pltpu.make_async_copy(self.source(2 * x + c), self.target(2 * z + y, 2 * x + c), self.local)
+
+    def move(self, slot):
+        z, y, x, c = place()
+        q = 2 * x + c
+        if slot < 3:
+            source, target, peer = self.source(q), self.target(2 * z + y, q), device(lax.rem(z + 1 + slot, 4), y, x, c)
+        elif slot == 3:
+            source, target, peer = self.source(q), self.target(2 * z + y, q), device(z, 1 - y, x, c)
+        elif slot < 7:
+            at = 2 * lax.rem(z + 7 - slot, 4) + y
+            source = target = self.target(at, q)
+            peer = device(z, 1 - y, x, c)
+        else:
+            part = 2 * (1 - x) + c if slot == 9 else q
+            source = target = self.whole(part)
+            peer = device(z, y, 1 - x, c) if slot == 7 else device(z, y, x, 1 - c)
+        return remote(source, target, self.sends.at[slot], self.recvs.at[slot], peer)
 
     def step(self, k):
-        z, y, x, c, q = self.z, self.y, self.x, self.c, self.q
-        f = 2 * z + y
         if k == 0:
-            for d in range(1, 4):
-                peer = lax.rem(z + d, 4)
-                self.send(d - 1, self.source(q), self.target(f, q), device(peer, y, x, c))
-            self.send(3, self.source(q), self.target(f, q), device(z, 1 - y, x, c))
-            own = pltpu.make_async_copy(self.source(q), self.target(f, q), self.local)
-            own.start()
-            self.moves["own"] = own
+            for slot in range(4):
+                self.move(slot).start()
+            self.own().start()
         if k == 1:
-            for d in range(1, 4):
-                self.moves[d - 1].wait()
-                at = 2 * lax.rem(z + 4 - d, 4) + y
-                self.send(3 + d, self.target(at, q), self.target(at, q), device(z, 1 - y, x, c))
+            for slot in range(3):
+                self.move(slot).wait()
+                self.move(slot + 4).start()
         if k == 2:
-            self.moves["own"].wait()
+            self.own().wait()
             for slot in range(3, 7):
-                self.moves[slot].wait()
-            self.send(7, self.whole(q), self.whole(q), device(z, y, 1 - x, c))
-            self.send(8, self.whole(q), self.whole(q), device(z, y, x, 1 - c))
+                self.move(slot).wait()
+            self.move(7).start()
+            self.move(8).start()
         if k == 3:
-            self.moves[7].wait()
-            other = 2 * (1 - x) + c
-            self.send(9, self.whole(other), self.whole(other), device(z, y, x, 1 - c))
+            self.move(7).wait()
+            self.move(9).start()
         if k == 4:
-            self.moves[8].wait()
-            self.moves[9].wait()
-
-    def peers(self):
-        z, y, x, c = self.z, self.y, self.x, self.c
-        return [device(lax.rem(z + d, 4), y, x, c) for d in range(1, 4)] + [
-            device(z, 1 - y, x, c),
-            device(z, y, 1 - x, c),
-            device(z, y, x, 1 - c),
-        ]
+            self.move(8).wait()
+            self.move(9).wait()
 
 
 GATHER_STEPS = 5
 
 
-def by_columns(source, target, sends, recvs, local):
-    rows, width = source.shape
+def by_columns(source, target, sends, recvs, local, first=0, width=None):
+    rows = source.shape[0]
+    width = width or source.shape[1]
     part = width // 4
 
     def cols(q):
-        return pl.ds(pl.multiple_of(q * part, 128), part)
+        return pl.ds(pl.multiple_of(first + q * part, 128), part)
 
     def rows_of(f):
         return pl.ds(pl.multiple_of(f * rows, 16), rows)
@@ -649,83 +856,25 @@
 
 
 class Butterfly:
-    def __init__(self, total, got, sends, recvs, like):
+    def __init__(self, total, got, sends, recvs):
         self.total, self.got, self.sends, self.recvs = total, got, sends, recvs
-        self.order = [like.to_c, like.to_x, like.to_y, like.to_z1, like.to_z2]
-        self.move = None
+
+    def move(self, k):
+        partner = Partners().pairs()[k]
+        return remote(self.total, self.got.at[k], self.sends.at[k], self.recvs.at[k], partner)
 
     def step(self, k):
         if k > 0:
-            self.move.wait()
+            self.move(k - 1).wait()
             self.total[...] = self.total[...] + self.got[k - 1]
         if k < 5:
-            self.move = remote(self.total, self.got.at[k], self.sends.at[k], self.recvs.at[k], self.order[k])
-            self.move.start()
+            self.move(k).start()
 
 
 BUTTERFLY_STEPS = 6
 
 
-def run_steps(plans):
-    last = max(first + count for first, count, _ in plans)
-    for tick in range(last):
-        for first, count, piece in plans:
-            if 0 <= tick - first < count:
-                piece.step(tick - first)
-
-
-def reduce_kernel(depth, t_ref, m_ref, s_ref, d_ref, out_t_ref, out_m_ref, out_s_ref, out_d_ref, *scratch):
-    scratch = list(scratch)
-    sends, recvs, loads, g_sends, g_recvs, g_local, b_sends, b_recvs, got = scratch[-9:]
-    plans = []
-
-    def piece(source, out):
-        n = len(plans)
-        one = Reducer(source, scratch[10 * n : 10 * n + 10], out, sends.at[n], recvs.at[n], loads.at[n])
-        plans.append((n, REDUCER_STEPS, one))
-
-    for layer in reversed(range(depth)):
-        piece(m_ref.at[layer], out_m_ref.at[layer])
-        piece(t_ref.at[layer], out_t_ref.at[layer])
-    first = plans[0][2]
-    mods = slab(d_ref, out_d_ref, g_sends, g_recvs, g_local)
-    out_s_ref[...] = s_ref[...]
-    sums = Butterfly(out_s_ref, got, b_sends, b_recvs, first)
-    z, y, x, c = place()
-    z3 = 3 - z
-    greet(first.peers() + [device(z3, y, x, c)])
-    run_steps([(0, GATHER_STEPS, mods), (0, BUTTERFLY_STEPS, sums)] + plans)
-
-
-def reduce_grads(g_t, g_m, sums, mods):
-    depth = g_t.shape[0]
-    shape = jax.ShapeDtypeStruct
-    scratch = []
-    for _ in range(depth):
-        scratch += reducer_scratch(2 * D) + reducer_scratch(D)
-    count = 2 * depth
-    dma = pltpu.SemaphoreType.DMA
-    scratch += [dma((count, 9)), dma((count, 9)), dma((count, 2)), dma((10,)), dma((10,)), dma, dma((5,)), dma((5,))]
-    scratch += [pltpu.VMEM((5,) + sums.shape, F32)]
-    anyspace = pl.BlockSpec(memory_space=pl.ANY)
-    vm = pl.BlockSpec(memory_space=pltpu.VMEM)
-    return pl.pallas_call(
-        functools.partial(reduce_kernel, depth),
-        out_shape=(
-            shape((depth, 4, OWN, D), F32),
-            shape((depth, 4, OWN, 2 * D), F32),
-            shape(sums.shape, F32),
-            shape((4, 8) + mods.shape, mods.dtype),
-        ),
-        in_specs=[anyspace, anyspace, vm, vm],
-        out_specs=(vm, vm, vm, vm),
-        scratch_shapes=scratch,
-        compiler_params=pltpu.CompilerParams(collective_id=1, has_side_effects=True, vmem_limit_bytes=60 * 1024 * 1024),
-        name="step_reduce",
-    )(g_t.reshape(depth, 4, 4, 2, OWN, D), g_m.reshape(depth, 4, 4, 2, OWN, 2 * D), sums, mods)
-
-
-C_T1, C_T2, C_PATCH, C_HEAD, C_ALL = 1024, 1280, 1664, 1680, 2048
+C_T1, C_T2, C_PATCH, C_HEAD, C_ALL = 1024, 1280, 1664, 1792, 2048
 SLOTS = 256
 
 
@@ -739,16 +888,18 @@
 
 
 def prologue_kernel(
-    depth,
     kinds,
+    images,
     small_ref,
     feat_ref,
     w_mods_ref,
-    top_ref,
-    bias_ref,
+    lbias_ref,
+    tbias_ref,
     own_in_ref,
     own_out_ref,
-    full_ref,
+    w_patch_ref,
+    w_head_ref,
+    time2_ref,
     w_in_ref,
     w_out_ref,
     mods_ref,
@@ -757,6 +908,7 @@
     before_ref,
     cond_ref,
     feats_ref,
+    full,
     part,
     got,
     cond_rows,
@@ -771,23 +923,25 @@
     z, y, x, c = place()
     f = 2 * z + y
     r = 2 * x + c
-    feats = slab(feat_ref, feats_ref, sends.at[0], recvs.at[0], local.at[0])
-    small = by_columns(small_ref, full_ref, sends.at[1], recvs.at[1], local.at[1])
-    plans = [(0, GATHER_STEPS, feats), (0, GATHER_STEPS, small)]
-    for layer in range(depth):
-        n = 2 + 2 * layer
-        plans.append(
-            (1 + 2 * layer, GATHER_STEPS, by_columns(own_in_ref.at[layer], w_in_ref.at[layer], sends.at[n], recvs.at[n], local.at[n]))
-        )
-        plans.append(
-            (
-                2 + 2 * layer,
-                GATHER_STEPS,
-                by_rows(own_out_ref.at[layer], w_out_ref.at[layer], sends.at[n + 1], recvs.at[n + 1], local.at[n + 1]),
-            )
-        )
-    others = [{"fsdp": lax.rem(f + k, 8)} for k in range(1, 8)]
-    greet(others + [device(z, y, 1 - x, c), device(z, y, x, 1 - c)])
+
+    def sems(n):
+        return sends.at[n], recvs.at[n], local.at[n]
+
+    feats = slab(feat_ref, feats_ref, *sems(0))
+    small = by_columns(small_ref, full, *sems(1))
+    own_in, own_out = own_in_ref.at[0], own_out_ref.at[0]
+    attention = by_columns(own_in, w_in_ref, *sems(2), 0, 4 * D)
+    inner = by_columns(own_in, w_in_ref, *sems(3), 4 * D, FF)
+    outer = by_rows(own_out, w_out_ref, *sems(4))
+    plans = [
+        (0, GATHER_STEPS, feats),
+        (0, GATHER_STEPS, small),
+        (2, GATHER_STEPS, attention),
+        (3, GATHER_STEPS, inner),
+        (4, GATHER_STEPS, outer),
+    ]
+    partners = Partners()
+    greet(partners.all())
     last = max(first + count for first, count, _ in plans)
     copies = []
     for tick in range(last):
@@ -801,11 +955,24 @@
         label = rows[:, FREQ : FREQ + 1]
         place_of = lax.broadcasted_iota(jnp.int32, (SLOTS, C_T1), 1).astype(F32)
         picked = jnp.where(label == place_of, 1.0, 0.0).astype(BF16)
-        time1 = dot(feat, full_ref[:, C_T1:C_T2], NT) + top_ref[0:1, :]
+        time1 = dot(feat, full[:, C_T1:C_T2], NT) + tbias_ref[:, D : 2 * D]
         s1 = silu(time1).astype(BF16)
-        before = dot(s1, full_ref[:, C_T2 : C_T2 + D]) + top_ref[1:2, :] + dot(picked, full_ref[:, :C_T1], NT)
+        before = dot(s1, full[:, C_T2 : C_T2 + D]) + tbias_ref[:, 2 * D : 3 * D] + dot(picked, full[:, :C_T1], NT)
         cond = silu(before)
         cond_rows[...] = cond
+        pick = lax.broadcasted_iota(jnp.int32, (D, OWN), 0) == f * OWN + lax.broadcasted_iota(jnp.int32, (D, OWN), 1)
+        group = cond_rows[pl.ds(pl.multiple_of(r * 64, 64), 64), :].astype(BF16)
+        group = dot(group, jnp.where(pick, 1.0, 0.0).astype(BF16)).astype(BF16)
+        for k in range(kinds):
+            mods = dot(group, w_mods_ref[:, k * D : (k + 1) * D])
+            for n in range(8):
+                part[n, k * images : (k + 1) * images, :] = mods[8 * n : 8 * n + images]
+        for k in range(1, 8):
+            to = lax.rem(f + k, 8)
+            copies.append(remote(part.at[to], got.at[f], p_sends.at[k - 1], p_recvs.at[k - 1], {"fsdp": to}))
+            copies[-1].start()
+        own = pltpu.make_async_copy(part.at[f], got.at[f], p_local)
+        own.start()
         mine = pl.ds(pl.multiple_of(f * OWN, OWN), OWN)
         time1_ref[...] = time1.T
         wide[...] = s1.astype(F32).T
@@ -814,41 +981,42 @@
         before_ref[...] = wide[mine, :]
         wide[...] = cond.T
         cond_ref[...] = wide[mine, :].astype(BF16)
-        pick = lax.broadcasted_iota(jnp.int32, (D, OWN), 0) == f * OWN + lax.broadcasted_iota(jnp.int32, (D, OWN), 1)
-        group = cond_rows[pl.ds(pl.multiple_of(r * 64, 64), 64), :].astype(BF16)
-        group = dot(group, jnp.where(pick, 1.0, 0.0).astype(BF16)).astype(BF16)
-        for k in range(kinds):
-            part[:, k] = dot(group, w_mods_ref[:, k * D : (k + 1) * D]).reshape(8, 8, D)
-        for k in range(1, 8):
-            copies.append(remote(part.at[lax.rem(f + k, 8)], got.at[f], p_sends.at[k - 1], p_recvs.at[k - 1], others[k - 1]))
-            copies[-1].start()
-        own = pltpu.make_async_copy(part.at[f], got.at[f], p_local)
-        own.start()
+        w_patch_ref[...] = full[:, C_PATCH : C_PATCH + PATCH_IN]
+        w_head_ref[...] = full[:, C_HEAD : C_HEAD + PATCH_IN]
+        time2_ref[...] = full[:, C_T2 : C_T2 + D]
+        mods_ref[...] = jnp.zeros_like(mods_ref)
     own.wait()
     for copy in copies:
         copy.wait()
-    total = got[0]
-    for k in range(1, 8):
-        total = total + got[k]
+    depth = (kinds - 2) // 6
     for k in range(kinds):
-        mods_ref[k] = total[k] + bias_ref[:, k * D : (k + 1) * D]
-    mods_ref[kinds:] = jnp.zeros_like(mods_ref[kinds:])
-
-
-def prologue(small, feat, w_mods, top, bias, own_in, own_out):
-    depth = own_in.shape[0]
+        at = slice(k * images, (k + 1) * images)
+        total = got[0, at]
+        for n in range(1, 8):
+            total = total + got[n, at]
+        if k < 6 * depth:
+            bias = lbias_ref[k // 6 : k // 6 + 1, k % 6 * D : k % 6 * D + D]
+        else:
+            first = 3 * D + (k - 6 * depth) * D
+            bias = tbias_ref[:, first : first + D]
+        mods_ref[k, 0:images] = total + bias
+
+
+def prologue(small, feat, w_mods, lbias, tbias, own_in, own_out, images):
     kinds = w_mods.shape[1] // D
     shape = jax.ShapeDtypeStruct
     anyspace = pl.BlockSpec(memory_space=pl.ANY)
     vm = pl.BlockSpec(memory_space=pltpu.VMEM)
     dma = pltpu.SemaphoreType.DMA
-    n = 2 + 2 * depth
+    rows = -(-kinds * images // 8) * 8
     return pl.pallas_call(
-        functools.partial(prologue_kernel, depth, kinds),
+        functools.partial(prologue_kernel, kinds, images),
         out_shape=(
-            shape((D, C_ALL), BF16),
-            shape((depth, D, own_in.shape[2]), BF16),
-            shape((depth, 8, 4, OWN, D), BF16),
+            shape((D, PATCH_IN), BF16),
+            shape((D, PATCH_IN), BF16),
+            shape((D, D), BF16),
+            shape((D, own_in.shape[2]), BF16),
+            shape((8, 4, OWN, D), BF16),
             shape((16, 8, D), F32),
             shape((D, SLOTS), F32),
             shape((OWN, SLOTS), BF16),
@@ -857,22 +1025,23 @@
             shape((4, 8) + feat.shape, F32),
         ),
         in_specs=[anyspace, vm, vm, vm, vm, anyspace, anyspace],
-        out_specs=(vm,) * 9,
+        out_specs=(vm, vm, vm, anyspace, anyspace) + (vm,) * 6,
         scratch_shapes=[
-            pltpu.VMEM((8, kinds, 8, D), F32),
-            pltpu.VMEM((8, kinds, 8, D), F32),
+            pltpu.VMEM((D, C_ALL), BF16),
+            pltpu.VMEM((8, rows, D), F32),
+            pltpu.VMEM((8, rows, D), F32),
             pltpu.VMEM((SLOTS, D), F32),
             pltpu.VMEM((D, SLOTS), F32),
-            dma((n, 10)),
-            dma((n, 10)),
-            dma((n,)),
+            dma((5, 10)),
+            dma((5, 10)),
+            dma((5,)),
             dma((7,)),
             dma((7,)),
             dma,
         ],
         compiler_params=pltpu.CompilerParams(collective_id=2, has_side_effects=True, vmem_limit_bytes=60 * 1024 * 1024),
         name="step_prologue",
-    )(small, feat, w_mods, top, bias, own_in, own_out)
+    )(small, feat, w_mods, lbias, tbias, own_in, own_out)
 
 
 E_PATCH, E_T1, E_T2, E_FIN, E_HEAD, E_ALL = 1024, 1152, 1408, 1792, 2560, 2688
@@ -1010,9 +1179,8 @@
     tbias_new[:, D : 2 * D] = dot(ones, d1, NT)[0:1] * scale
     tbias_new[:, 2 * D : 3 * D] = dot(ones, d2, NT)[0:1] * scale
     tbias_new[:, 0:D] = sums_ref[S_BPATCH : S_BPATCH + 1, :] * scale
-    tail = tbias_new.shape[1]
-    tbias_new[:, 5 * D : tail] = jnp.zeros((1, tail - 5 * D), F32)
-    tbias_new[:, 5 * D : 5 * D + PATCH_IN] = sums_ref[S_BHEAD : S_BHEAD + 1, 0:PATCH_IN] * scale
+    lane = lax.broadcasted_iota(jnp.int32, (1, 2 * PATCH_IN), 1)
+    tbias_new[:, 5 * D :] = jnp.where(lane < PATCH_IN, sums_ref[S_BHEAD : S_BHEAD + 1, 0 : 2 * PATCH_IN], 0.0) * scale
     for layer in range(depth):
         for j in range(8):
             row = S_BIAS + 8 * layer + j
@@ -1170,18 +1338,16 @@
 
 
 def position_table():
-    grid_side = GRID // PATCH
+    side = GRID // PATCH
     quarter = D // 4
-    omegas = 1.0 / 10000.0 ** (jnp.arange(quarter, dtype=jnp.float32) / quarter)
-    places = jnp.arange(grid_side * grid_side)
-    across = (places % grid_side).astype(jnp.float32)
-    downward = (places // grid_side).astype(jnp.float32)
+    omegas = 1.0 / 10000.0 ** (np.arange(quarter) / quarter)
+    places = np.arange(side * side)
 
     def one_axis(coords):
         angles = coords[:, None] * omegas[None, :]
-        return jnp.concatenate([jnp.sin(angles), jnp.cos(angles)], axis=1)
-
-    return jnp.concatenate([one_axis(across), one_axis(downward)], axis=1)
+        return np.concatenate([np.sin(angles), np.cos(angles)], axis=1)
+
+    return np.concatenate([one_axis(places % side), one_axis(places // side)], axis=1).astype(np.float32)
 
 
 def time_features(tsteps):
@@ -1286,19 +1452,17 @@
     target = patchify(noise).reshape(images * TOK, PATCH_IN)
 
     w_in, w_out = fetch(layer_in, layer_out)
-    bias_rows = jnp.concatenate([layer_bias[:, MOD : MOD + D], layer_bias[:, MOD + D :]], axis=1)
     g_in, g_out, sums, d_mods = compute(
         patches,
         target,
-        position_table(),
+        jnp.asarray(position_table()),
         jnp.transpose(jnp.pad(mods, ((0, 8 - images), (0, 16 - kinds), (0, 0))), (1, 0, 2)),
         w_in,
-        w_out,
+        w_out.reshape(depth, FF // FFC, FFC, D),
         patch_cols,
-        head_cols.T,
-        bias_rows,
-        top_bias[None, :D],
-        top_bias[None, 5 * D : 5 * D + PATCH_IN],
+        head_cols,
+        layer_bias,
+        top_bias[None],
     )
 
     d_mods = jnp.transpose(d_mods, (1, 0, 2))[:images, :kinds].reshape(images, kinds * D)
@@ -1314,7 +1478,7 @@
 
     shard_in = lax.psum(lax.psum_scatter(g_in, "fsdp", scatter_dimension=1, tiled=True), "rep")
     shard_out = lax.psum(lax.psum_scatter(g_out, "fsdp", scatter_dimension=1, tiled=True), "rep")
-    sums = lax.psum(sums, ("fsdp", "rep"))
+    sums = lax.psum(sums, ("fsdp", "rep")).reshape(S_ROWS, D)
     g_patch, g_head = sums[:S_HEAD], sums[S_HEAD:S_BIAS]
     g_bias = sums[S_BIAS:S_BPATCH].reshape(depth, BW)
     g_bpatch, g_bhead = sums[S_BPATCH : S_BPATCH + 1], sums[S_BHEAD : S_BHEAD + 1, :PATCH_IN]
@@ -1462,9 +1626,9 @@
         [
             edge_low[:, :E_PATCH],
             edge_low[:, E_T1:E_FIN],
-            edge_low[:, E_PATCH : E_PATCH + PATCH_IN],
-            edge_low[:, E_HEAD : E_HEAD + PATCH_IN],
-            jnp.zeros((OWN, C_ALL - C_HEAD - PATCH_IN), BF16),
+            edge_low[:, E_PATCH:E_T1],
+            edge_low[:, E_HEAD:E_ALL],
+            jnp.zeros((OWN, C_ALL - C_HEAD - (E_ALL - E_HEAD)), BF16),
         ],
         axis=1,
     )
@@ -1473,38 +1637,20 @@
         [time_features(tsteps), jnp.broadcast_to(labels.astype(F32)[:, None], (images, 128))], axis=1
     )
     feat = jnp.pad(feat, ((0, 8 - images), (0, 0)))
-    bias_mods = jnp.concatenate([layer_bias[layer, :MOD] for layer in range(depth)] + [top_bias[3 * D : 5 * D]])[None]
-    full, w_in, w_out, mods, time1, s1, before, cond, feats = prologue(
-        small,
-        feat,
-        w_mods,
-        top_bias[D : 3 * D].reshape(2, D),
-        bias_mods,
-        layer_in[:, :, MOD:].astype(BF16),
-        layer_out.astype(BF16).reshape(depth, 4, OWN, D),
+    tbias = top_bias[None]
+    own = (layer_in[:, :, MOD:].astype(BF16), layer_out.astype(BF16).reshape(depth, 4, OWN, D))
+    w_patch, w_head, time2, w_in, w_out, mods, time1, s1, before, cond, feats = prologue(
+        small, feat, w_mods, layer_bias, tbias, *own, images
     )
 
     alphas = mix_weights(tsteps)
     noisy = jnp.sqrt(alphas)[:, None, None] * latents + jnp.sqrt(1.0 - alphas)[:, None, None] * noise
     patches = patchify(noisy).astype(BF16).reshape(images * TOK, PATCH_IN)
     target = patchify(noise).reshape(images * TOK, PATCH_IN)
-    bias_rows = jnp.concatenate([layer_bias[:, MOD : MOD + D], layer_bias[:, MOD + D :]], axis=1)
-    g_t, g_m, sums, d_mods = compute(
-        patches,
-        target,
-        position_table(),
-        mods,
-        w_in,
-        w_out.reshape(depth, FF, D),
-        full[:, C_PATCH : C_PATCH + PATCH_IN],
-        full[:, C_HEAD : C_HEAD + PATCH_IN].T,
-        bias_rows,
-        top_bias[None, :D],
-        top_bias[None, 5 * D : 5 * D + PATCH_IN],
-        blocked=True,
-    )
-    out_t, out_m, sums, d_mods = reduce_grads(g_t, g_m, sums, d_mods)
-    weights = (layer_in, layer_out, edge_a, layer_bias, wide_to(top_bias[None], 16 * 128))
+    _, _, sums, _, out_t, out_m, d_mods = compute(
+        patches, target, jnp.asarray(position_table()), mods, w_in, w_out, w_patch, w_head, layer_bias, tbias, own
+    )
+    weights = (layer_in, layer_out, edge_a, layer_bias, tbias)
     stats = (
         in_rows,
         in_cols,
@@ -1513,7 +1659,7 @@
         edge_rows[None],
         aligned(edge_cols[None], 1.0),
         layer_bias_v,
-        wide_to(top_bias_v[None], 16 * 128, 1.0),
+        top_bias_v[None],
     )
     (
         in_new,
@@ -1531,7 +1677,7 @@
         tbias_v_new,
         tail,
     ) = update(
-        (classes, tokens), out_t, out_m, sums, d_mods, cond, before, time1, s1, feats, full[:, C_T2 : C_T2 + D], w_mods, weights, stats
+        (classes, tokens), out_t, out_m, sums.reshape(S_ROWS, D), d_mods, cond, before, time1, s1, feats, time2, w_mods, weights, stats
     )
 
     def natural(v):
@@ -1539,14 +1685,13 @@
             [v[:, :NCLS], v[:, E_PATCH : E_PATCH + PATCH_IN], v[:, E_T1 : E_HEAD + 2 * PATCH_IN]], axis=1
         )
 
-    count = top_bias.shape[0]
     return (
         tail[0, 2 * depth + 1],
         in_new,
         out_new,
         natural(edge_new),
         lbias_new,
-        tbias_new[0, :count],
+        tbias_new[0],
         in_rows_new,
         in_cols_new,
         out_rows_new,
@@ -1554,7 +1699,7 @@
         edge_rows_new[0],
         natural(edge_cols_new)[0],
         lbias_v_new,
-        tbias_v_new[0, :count],
+        tbias_v_new[0],
         tail[0, : 2 * depth + 1],
     )
 

time: 407 us -> 355 us (0.87)
  Pallas kernels: 345 us -> 313 us
  local copies, waits for them, and re-layouts: 45.8 us -> 28.7 us
  other arithmetic: 11.8 us -> 6.91 us
    pallas_call x3 -> x2, Pallas kernels: 308 us -> 279 us  [the longest x1 222 us: compute(): pl.pallas_call(functools.partial(compute_kernel, images, group, direct),...]
    slice x9 -> x1, local copies, waits for them, and re-layouts: 5.65 us -> 0.07 us  [the longest x1 1.7 us: direct_step(): full[:, C_T2:C_T2 + D]]
    unnamed x42 -> x56, local copies, waits for them, and re-layouts: 8.12 us -> 8.19 us
where the time goes in v4:
time: 355 us; the launch traced here: 350 us
  Pallas kernels  313 us (88%)
  local copies, waits for them, and re-layouts  28.7 us (8%)
  other arithmetic  6.91 us (2%)
    pallas_call x1, Pallas kernels, compute(): pl.pallas_call(functools.partial(compute_kernel, images, group, direct),...  222 us
    pallas_call x1, Pallas kernels, prologue(): pl.pallas_call(functools.partial(prologue_kernel, kinds, images), out_sha...  57.7 us
    pallas_call x1, Pallas kernels, update(): pl.pallas_call(functools.partial(update_kernel, sizes), out_shape=outs, i...  33.7 us
    unnamed x56, local copies, waits for them, and re-layouts  8.19 us

profile of v4, /device:TPU:0, one launch (start us, length us, event | category | flops | bytes accessed | tf_op | source)
XLA Modules:
  0.0 349.8 jit_solution(18390445707401016356)
XLA Ops:
  0.7 1.2 slice.92
  1.9 1.0 slice_select_fusion
  2.9 0.8 slice.91
  3.7 0.9 slice.93
  4.5 0.9 fusion.5
  5.7 0.8 pad_maximum_fusion.w_mods_ref
  6.5 0.9 slice.122.own_in_ref.refs_10_
  8.2 0.8 convert_element_type.45
  9.0 57.7 %step_prologue.1 = (bf16[384,16]{1,0:T(8,128)(2,1)}, bf16[384,16]{1,0:T(8,128)(2,1)}, bf16[384,384]{1,0:T(8,128)(2,1)}, bf16[384,3072]{1,0:T(8,128)(2,1)}, bf16[...) custom-call(bf16[48,2048]{1,0:T(8,128)(2,1)} %copy-done.4, ...), custom_call_target="tpu_custom_call" | custom-call | tf_op jit(solution)/shard_map/step_prologue/pallas_call | solution.py:1012
  68.2 2.2 copy.42
  70.9 0.9 copy.45.refs_0_
  72.5 2.2 copy.44
  75.1 1.2 copy.46.refs_1_
  76.9 221.5 %step_compute.1 = (f32[2,4,384,384]{3,2,1,0:T(8,128)}, f32[2,4,384,768]{3,2,1,0:T(8,128)}, f32[7,8,384]{2,1,0:T(8,128)}, bf16[16,8,384]{2,1,0:T(8,128)(2,1)}, f3...) custom-call(bf16[1536,16]{1,0:T(8,128)(2,1)} %copy.45.refs_0_, ...), custom_call_target="tpu_custom_call" | custom-call | tf_op jit(solution)/shard_map/step_compute/pallas_call | solution.py:623
  298.4 0.7 broadcast_in_dim.50
  299.2 0.7 slice_select_fusion.1
  300.7 33.7 %step_update.1 = (f32[2,48,5376]{2,1,0:T(8,128)}, f32[2,192,384]{2,1,0:T(8,128)}, f32[48,2688]{1,0:T(8,128)}, f32[2,5376]{1,0:T(2,128)}, f32[1,1952]{1,0:T(1,128...) custom-call(f32[2,4,48,384]{3,2,1,0:T(8,128)} %get-tuple-element.49., ...), custom_call_target="tpu_custom_call" | custom-call | tf_op jit(solution)/shard_map/step_update/pallas_call | solution.py:1303
  334.4 0.8 slice.112
  337.3 1.0 slice.109
  338.3 0.9 slice.107
  339.3 0.7 slice.108
  340.0 0.9 concatenate.26
  342.1 1.3 copy.62
  343.4 0.8 copy.63
  (89 shorter events, 13.9 us)
Async XLA Ops:
  0.6 4.9 %copy-start = (f32[2,48,5376]{2,1,0:T(8,128)S(1)}, f32[2,48,5376]{2,1,0:T(8,128)}, u32[]{:S(2)}) copy-start(f32[2,48,5376]{2,1,0:T(8,128)} %in_ref.1) | copy-start | bytes 6193156
  5.5 1.1 copy-start.4
  5.6 1.8 copy-start.16
  5.6 1.9 copy-start.17
  5.6 2.6 copy-start.1
  6.5 61.0 %copy-start.5 = (f32[6,4,1024]{2,1,0:T(4,128)S(1)}, f32[6,4,1024]{2,1,0:T(4,128)}, u32[]{:S(2)}) copy-start(f32[6,4,1024]{2,1,0:T(4,128)} %param.21) | copy-start | bytes 294916
  6.5 61.0 %copy-start.7 = (f32[6,4,1024]{2,1,0:T(4,128)S(1)}, f32[6,4,1024]{2,1,0:T(4,128)}, u32[]{:S(2)}) copy-start(f32[6,4,1024]{2,1,0:T(4,128)} %param.18) | copy-start | bytes 294916
  72.5 3.8 %copy-start.6 = (f32[2,5376]{1,0:T(2,128)S(1)}, f32[2,5376]{1,0:T(2,128)}, u32[]{:S(2)}) copy-start(f32[2,5376]{1,0:T(2,128)} %lbias_ref.3) | copy-start | bytes 129028
  334.4 6.5 %copy-start.19 = (f32[1,128]{1,0:T(1,128)S(1)}, f32[1,128]{1,0:T(1,128)}, u32[]{:S(2)}) copy-start(f32[1,128]{1,0:T(1,128)} %get-tuple-element.59) | copy-start | bytes 1540
  334.4 7.6 %copy-start.2 = (f32[2,48,5376]{2,1,0:T(8,128)S(1)}, f32[2,48,5376]{2,1,0:T(8,128)}, u32[]{:S(2)}) copy-start(f32[2,48,5376]{2,1,0:T(8,128)} %get-tuple-element.97) | copy-start | bytes 6193156
  340.9 2.5 copy-start.3
  342.0 2.2 copy-start.10
  342.0 2.8 copy-start.12
  342.0 3.4 copy-start.15
  342.0 4.0 %copy-start.9 = (f32[2,5376]{1,0:T(2,128)S(1)}, f32[2,5376]{1,0:T(2,128)}, u32[]{:S(2)}) copy-start(f32[2,5376]{1,0:T(2,128)} %get-tuple-element.103) | copy-start | bytes 129028
  342.0 4.6 %copy-start.14 = (f32[2,192]{1,0:T(2,128)S(1)}, f32[2,192]{1,0:T(2,128)}, u32[]{:S(2)}) copy-start(f32[2,192]{1,0:T(2,128)} %get-tuple-element.104) | copy-start | bytes 4612
  342.1 5.2 %copy-start.13 = (f32[2,384]{1,0:T(2,128)S(1)}, f32[2,384]{1,0:T(2,128)}, u32[]{:S(2)}) copy-start(f32[2,384]{1,0:T(2,128)} %get-tuple-element.105) | copy-start | bytes 9220
  342.1 5.7 %copy-start.18 = (f32[1,48]{1,0:T(1,128)S(1)}, f32[1,48]{1,0:T(1,128)}, u32[]{:S(2)}) copy-start(f32[1,48]{1,0:T(1,128)} %get-tuple-element.69) | copy-start | bytes 580
  342.1 6.2 %copy-start.8 = (f32[2,5376]{1,0:T(2,128)S(1)}, f32[2,5376]{1,0:T(2,128)}, u32[]{:S(2)}) copy-start(f32[2,5376]{1,0:T(2,128)} %get-tuple-element.108) | copy-start | bytes 129028
  342.1 6.8 %copy-start.11 = (f32[1,1952]{1,0:T(1,128)S(1)}, f32[1,1952]{1,0:T(1,128)}, u32[]{:S(2)}) copy-start(f32[1,1952]{1,0:T(1,128)} %get-tuple-element.72) | copy-start | bytes 23428

commit v5 on v4

--- a/solution.py
+++ b/solution.py
@@ -34,6 +34,7 @@
 TN = (((0,), (0,)), ((), ()))
 FFC = 768
 OWN = 48
+ROWS = 32
 
 
 def dot(a, b, dims=(((1,), (0,)), ((), ()))):
@@ -57,14 +58,26 @@
     return jnp.sum(v, axis=0, keepdims=True)
 
 
+def column_of(row):
+    n = row.shape[1]
+    same = lax.broadcasted_iota(jnp.int32, (n, n), 0) == lax.broadcasted_iota(jnp.int32, (n, n), 1)
+    return jnp.sum(jnp.where(same, row, 0.0), axis=1, keepdims=True)
+
+
+def row_of(column):
+    n = column.shape[0]
+    same = lax.broadcasted_iota(jnp.int32, (n, n), 0) == lax.broadcasted_iota(jnp.int32, (n, n), 1)
+    return jnp.sum(jnp.where(same, column, 0.0), axis=0, keepdims=True)
+
+
 def soft_rows(s):
     e = jnp.exp(s - jnp.max(s, axis=-1, keepdims=True))
-    return e / jnp.sum(e, axis=-1, keepdims=True)
+    return e * (1.0 / jnp.sum(e, axis=-1, keepdims=True))
 
 
 def gelu_parts(x):
-    t = jnp.tanh(GELU_A * (x + GELU_B * (x * x * x)))
-    return t
+    x2 = x * x
+    return x2, jnp.tanh(x * (GELU_A + (GELU_A * GELU_B) * x2))
 
 
 QKV = 0
@@ -83,30 +96,6 @@
         return self.ref[layer][:, 6 * D :]
 
 
-class BiasRows:
-    def __init__(self, ref):
-        self.ref = ref
-
-    def __getitem__(self, layer):
-        return self.ref[layer][:, 6 * D :]
-
-
-class BiasRows:
-    def __init__(self, ref):
-        self.ref = ref
-
-    def __getitem__(self, layer):
-        return self.ref[layer][:, 6 * D :]
-
-
-class BiasRows:
-    def __init__(self, ref):
-        self.ref = ref
-
-    def __getitem__(self, layer):
-        return self.ref[layer][:, 6 * D :]
-
-
 def compute_kernel(images, group, direct, *refs):
     refs = list(refs)
 
@@ -120,7 +109,7 @@
     own_in_ref, own_out_ref = take(2) if direct else (None,) * 2
     g_in_ref, g_out_ref, sums_ref, g_mods_ref = take(4)
     out_t_ref, out_m_ref, out_d_ref = take(3) if direct else (None,) * 3
-    w_in_ref, w_out_ref, tok, mid, qkv, att, branch, outb, normed, act, dinner, dsmall, stage, mod_sums, sems, w_sems = take(16)
+    w_in_ref, w_out_ref, tok, mid, qkv, att, branch, outb, normed, act, dinner, dsmall, dqkv, stage, mod_sums, scores, d_probs, probs, d_scores, sems, w_sems = take(21)
     steps = images // group
     crow = group * TOK
     depth = lbias_ref.shape[0]
@@ -264,22 +253,29 @@
     @pl.loop(0, images)
     def _(b):
         r = rows_of(b)
-        tok[0, r, :] = dot(patches_ref[r, :], w_patch_ref[...], NT) + tbias_ref[:, 0:D] + pos_ref[...]
-
-    def half(v, which):
+        tok[0, r, :] = dot(patches_ref[:, r], w_patch_ref[...], (((0,), (1,)), ((), ()))) + tbias_ref[:, 0:D] + pos_ref[...]
+
+    def half(v, which, factor=None):
+        v = v if factor is None else v * jnp.asarray(factor, v.dtype)
         zero = jnp.zeros_like(v)
         return jnp.where(first_half, v, zero) if which == 0 else jnp.where(first_half, zero, v)
 
-    def attention(layer, r):
+    def attention(layer, r, turn):
         for pair in range(HEADS // 2):
             c = pair * 128
             q = qkv[layer, r, c : c + 128]
             k = qkv[layer, r, D + c : D + c + 128]
             v = qkv[layer, r, 2 * D + c : 2 * D + c + 128]
+            slot = turn % 2
+            turn += 1
+            for which in range(2):
+                scores[slot, which] = dot(half(q, which, HEAD_DIM ** (-0.5)), k, NT)
             got = []
             for which in range(2):
-                s = dot(half(q, which), k, NT) * HEAD_DIM ** (-0.5)
-                got.append(dot(soft_rows(s).astype(BF16), v))
+                for at_row in range(0, TOK, ROWS):
+                    block = slice(at_row, at_row + ROWS)
+                    probs[slot, which, block, :] = soft_rows(scores[slot, which, block, :]).astype(BF16)
+                got.append(dot(probs[slot, which], v))
             att[layer, r, c : c + 128] = jnp.where(first_half, got[0], got[1]).astype(BF16)
 
     def modulated(t, b, k):
@@ -317,7 +313,7 @@
             p = dot(hc, w_in_ref[layer, :, QKV + 2 * D : QKV + 3 * D])
             qkv[layer, cr, 2 * D : 3 * D] = (p + bias[:, BV : BV + D]).astype(BF16)
             for j in range(group):
-                attention(layer, rows_of(i * group + j))
+                attention(layer, rows_of(i * group + j), 3 * j)
             if direct:
                 at(
                     layer,
@@ -338,7 +334,8 @@
             out = jnp.zeros((crow, D), F32) + bias[:, BF2 : BF2 + D]
             for c in range(0, FF, FFC):
                 x = dot(mc, w_in_ref[layer, :, WF1 + c : WF1 + c + FFC]) + bias[:, BF1 + c : BF1 + c + FFC]
-                a = (x * (0.5 * (1.0 + gelu_parts(x)))).astype(BF16)
+                side = 0.5 * x
+                a = (side + side * gelu_parts(x)[1]).astype(BF16)
                 out = out + dot(a, down_rows(layer, c))
             outb[layer, cr, :] = out.astype(BF16)
             for j in range(group):
@@ -347,18 +344,21 @@
                 tok[layer + 1, r, :] = mid[layer, r, :] + mod_row(b, mo + 5) * out[near(j)]
 
     dtok = tok.at[depth]
+    head_bias = column_of(tbias_ref[:, 5 * D : 5 * D + PATCH_IN])
 
     @pl.loop(0, images)
     def _(b):
         r = rows_of(b)
         k = 6 * depth
         n, scale, n3 = modulated(dtok[r, :], b, k)
-        miss = dot(n3, w_head_ref[...]) + tbias_ref[:, 5 * D : 5 * D + PATCH_IN] - target_ref[r, :]
-        sums_ref[S_SSE // 8, S_SSE % 8 : S_SSE % 8 + 1, 0:PATCH_IN] += rows_sum(miss * miss)
+        miss = dot(w_head_ref[...], n3, (((0,), (1,)), ((), ()))) + head_bias - target_ref[:, r]
+        sums_ref[S_SSE // 8, S_SSE % 8 : S_SSE % 8 + 1, 0:TOK] += rows_sum(miss * miss)
         dp = (2.0 * miss).astype(BF16)
-        sums_ref[S_HEAD // 8 : S_HEAD // 8 + 2] += dot(dp, n3, TN).reshape(2, 8, D)
-        sums_ref[S_BHEAD // 8, S_BHEAD % 8 : S_BHEAD % 8 + 1, 0:PATCH_IN] += rows_sum(dp.astype(F32))
-        dn3 = dot(dp, w_head_ref[...], NT)
+        sums_ref[S_HEAD // 8 : S_HEAD // 8 + 2] += dot(dp, n3).reshape(2, 8, D)
+        sums_ref[S_BHEAD // 8, S_BHEAD % 8 : S_BHEAD % 8 + 1, 0:PATCH_IN] += row_of(
+            jnp.sum(dp.astype(F32), axis=1, keepdims=True)
+        )
+        dn3 = dot(dp, w_head_ref[...], (((0,), (1,)), ((), ())))
         put_mod(b, k, rows_sum(dn3))
         put_mod(b, k + 1, rows_sum(dn3 * n))
         dtok[r, :] = norm_back(dn3 * (1.0 + mod_row(b, k + 1)), n, scale)
@@ -401,11 +401,10 @@
             dm = jnp.zeros((crow, D), F32)
             for c in range(0, FF, FFC):
                 x = dot(mc, w_in_ref[layer, :, WF1 + c : WF1 + c + FFC]) + bias[:, BF1 + c : BF1 + c + FFC]
-                x2 = x * x
-                t = jnp.tanh(GELU_A * (x + GELU_B * (x2 * x)))
-                cdf = 0.5 * (1.0 + t)
-                act[:, c : c + FFC] = (x * cdf).astype(BF16)
-                slope = cdf + (0.5 * GELU_A) * x * (1.0 - t * t) * (1.0 + (3.0 * GELU_B) * x2)
+                x2, t = gelu_parts(x)
+                side = 0.5 * x
+                act[:, c : c + FFC] = (side + side * t).astype(BF16)
+                slope = (0.5 + 0.5 * t) + side * (1.0 - t * t) * (GELU_A + (3.0 * GELU_A * GELU_B) * x2)
                 di = (dot(do, down_rows(layer, c), NT) * slope).astype(BF16)
                 dinner[:, c : c + FFC] = di
                 add_bias(layer, BF1 + c, rows_sum(di.astype(F32)))
@@ -464,33 +463,46 @@
 
             if direct:
                 at(li, i, (0, 0, [(m_last, 0)]), (1, 0, [(m_last, 4)]), (1, 1, [(m_first, 1), (t_last, 4)]))
-            for j in range(group):
+
+            @pl.loop(0, group)
+            def _(j):
                 r = rows_of(i * group + j)
+                here = rows_of(j)
+                q_sums, v_sums = [], []
                 for pair in range(HEADS // 2):
                     c = pair * 128
                     q = qkv[layer, r, c : c + 128]
                     k = qkv[layer, r, D + c : D + c + 128]
                     v = qkv[layer, r, 2 * D + c : 2 * D + c + 128]
                     da = branch[layer, r, c : c + 128]
+                    slot = pair % 2
+                    for which in range(2):
+                        scores[slot, which] = dot(half(q, which, HEAD_DIM ** (-0.5)), k, NT)
+                        d_probs[slot, which] = dot(half(da, which), v, NT)
                     got = []
                     for which in range(2):
-                        s = dot(half(q, which), k, NT) * HEAD_DIM ** (-0.5)
-                        p = soft_rows(s)
-                        dv = dot(p.astype(BF16), da, TN)
-                        dpr = dot(half(da, which), v, NT)
-                        ds = p * (dpr - jnp.sum(dpr * p, axis=-1, keepdims=True))
-                        ds = ds.astype(BF16)
-                        dq = dot(ds, k)
-                        dk = dot(ds, q, TN)
+                        for at_row in range(0, TOK, ROWS):
+                            block = slice(at_row, at_row + ROWS)
+                            p = soft_rows(scores[slot, which, block, :])
+                            probs[slot, which, block, :] = p.astype(BF16)
+                            dpr = d_probs[slot, which, block, :]
+                            ds = p * (dpr - jnp.sum(dpr * p, axis=-1, keepdims=True))
+                            d_scores[slot, which, block, :] = ds.astype(BF16)
+                        dv = dot(probs[slot, which], da, TN)
+                        dq = dot(d_scores[slot, which], k)
+                        dk = dot(d_scores[slot, which], q, TN)
                         got.append((dq, dk, dv))
                     dq = (jnp.where(first_half, got[0][0], got[1][0]) * HEAD_DIM ** (-0.5)).astype(BF16)
                     dk = (jnp.where(first_half, got[0][1], got[1][1]) * HEAD_DIM ** (-0.5)).astype(BF16)
                     dv = jnp.where(first_half, got[0][2], got[1][2]).astype(BF16)
-                    qkv[layer, r, c : c + 128] = dq
-                    qkv[layer, r, D + c : D + c + 128] = dk
-                    qkv[layer, r, 2 * D + c : 2 * D + c + 128] = dv
-                    sums_ref[S_BIAS // 8 + layer, 0:1, c : c + 128] += rows_sum(dq.astype(F32))
-                    sums_ref[S_BIAS // 8 + layer, 1:2, c : c + 128] += rows_sum(dv.astype(F32))
+                    dqkv[here, c : c + 128] = dq
+                    dqkv[here, D + c : D + c + 128] = dk
+                    dqkv[here, 2 * D + c : 2 * D + c + 128] = dv
+                    q_sums.append(rows_sum(dq.astype(F32)))
+                    v_sums.append(rows_sum(dv.astype(F32)))
+                sums_ref[S_BIAS // 8 + layer, 0:1, :] += jnp.concatenate(q_sums, axis=1)
+                sums_ref[S_BIAS // 8 + layer, 1:2, :] += jnp.concatenate(v_sums, axis=1)
+
             if direct:
                 at(
                     li,
@@ -499,7 +511,7 @@
                     (1, 0, [(m_last, 5), (m_first, 0), (t_last, 3), (d_last, 3)]),
                     (1, 1, [(t_last, 5), (d_last, 4)]),
                 )
-            dh = dot(qkv[layer, cr, :], w_in_ref[layer, :, QKV : QKV + 3 * D], NT)
+            dh = dot(dqkv[...], w_in_ref[layer, :, QKV : QKV + 3 * D], NT)
             for j in range(group):
                 b = i * group + j
                 r = rows_of(b)
@@ -513,7 +525,7 @@
             @pl.loop(0, 3)
             def _(c):
                 cs = pl.ds(pl.multiple_of(c * D, D), D)
-                stage[0, :, cs] += dot(normed[...], qkv[layer, cr, cs], TN)
+                stage[0, :, cs] += dot(normed[...], dqkv[:, cs], TN)
 
             stage[0, :, 3 * D : 4 * D] += dot(att[layer, cr, :], dsmall[...], TN)
 
@@ -531,7 +543,7 @@
         r = rows_of(b)
         d = dtok[r, :].astype(BF16)
         sums_ref[S_BPATCH // 8, S_BPATCH % 8 : S_BPATCH % 8 + 1, :] += rows_sum(d.astype(F32))
-        sums_ref[0:2] += dot(patches_ref[r, :], d, TN).reshape(2, 8, D)
+        sums_ref[0:2] += dot(patches_ref[:, r], d).reshape(2, 8, D)
 
     finish(in_moves(0, QKV))
     if direct:
@@ -541,13 +553,13 @@
             (d_first, 1),
             (t_first, 1),
             (s_piece, 1),
-            (d_first, 2),
             (s_piece, 2),
             (t_first, 2),
+            (d_first, 2),
+            (s_piece, 3),
             (m_first, 3),
+            (s_piece, 4),
             (d_first, 3),
-            (s_piece, 3),
-            (s_piece, 4),
             (t_first, 3),
             (d_first, 4),
             (s_piece, 5),
@@ -570,7 +582,7 @@
 def compute(patches, target, pos, mods, w_in, w_out, w_patch, w_head, lbias, tbias, own=(), group=3):
     direct = len(own) > 0
     depth = lbias.shape[0]
-    rows = patches.shape[0]
+    rows = patches.shape[1]
     images = rows // TOK
     crow = group * TOK
     kinds = mods.shape[0]
@@ -598,8 +610,13 @@
         pltpu.VMEM((crow, FF), BF16),
         pltpu.VMEM((crow, FF), BF16),
         pltpu.VMEM((crow, D), BF16),
+        pltpu.VMEM((crow, 3 * D), BF16),
         pltpu.VMEM((2, D, FF), F32),
         pltpu.VMEM((kinds, 8, D), F32),
+        pltpu.VMEM((2, 2, TOK, TOK), F32),
+        pltpu.VMEM((2, 2, TOK, TOK), F32),
+        pltpu.VMEM((2, 2, TOK, TOK), BF16),
+        pltpu.VMEM((2, 2, TOK, TOK), BF16),
         dma((2, 32)),
         dma((2 * depth,)),
     ]
@@ -610,13 +627,13 @@
             shape((depth, 4, OWN, 2 * D), F32),
             shape((4, 8, kinds, 8, D), BF16),
         ]
-        out_specs += [vm, vm, anyspace]
+        out_specs += [anyspace, anyspace, anyspace]
         scratch += wide_scratch(2 * D) + wide_scratch(D)
         for _ in range(depth):
             scratch += [pltpu.VMEM((8, OWN, 2 * D), BF16), pltpu.VMEM((8, OWN, D), BF16)]
         count = 2 * depth
         gathers = 3 * (depth - 1)
-        scratch += [pltpu.VMEM((5, S_ROWS // 8, 8, D), F32), dma((count, 13)), dma((count, 13)), dma((count, 2))]
+        scratch += [pltpu.VMEM((5, S_ROWS // 8, 8, D), F32), dma((count, 13)), dma((count, 13)), dma((count, 3))]
         scratch += [dma((2, 10)), dma((2, 10)), dma((2,)), dma((5,)), dma((5,))]
         scratch += [dma((gathers, 10)), dma((gathers, 10)), dma((gathers,))]
         params.update(collective_id=1, has_side_effects=True)
@@ -671,6 +688,10 @@
     def load(self, half):
         c = place()[3]
         return pltpu.make_async_copy(self.source.at[2 * half + c], self.flat(self.keep, half), self.loads.at[half])
+
+    def store(self):
+        z, y, x, c = place()
+        return pltpu.make_async_copy(self.keep.at[x, 2 * z + y], self.out.at[2 * x + c], self.loads.at[2])
 
     def move(self, slot):
         z, y, x, c = place()
@@ -686,7 +707,8 @@
             source, target, peer = self.low.at[to], self.gotp.at[f], {"fsdp": to}
         else:
             peer = partners.x if slot == 10 else partners.c
-            source = target = self.out.at[2 * (1 - x) + c if slot == 12 else mine]
+            target = self.out.at[2 * (1 - x) + c if slot == 12 else mine]
+            source = target if slot == 12 else self.keep.at[x, 2 * z + y]
         return remote(source, target, self.sends.at[slot], self.recvs.at[slot], peer)
 
     def step(self, k):
@@ -726,13 +748,15 @@
             total = self.keep[x, f]
             for d in range(1, 8):
                 total = total + self.gotp[lax.rem(f + d, 8)].astype(F32)
-            self.out[2 * x + c] = total
+            self.keep[x, f] = total
+            self.store().start()
             for slot in range(10, 12):
                 self.move(slot).start()
         if k == 4:
             self.move(10).wait()
             self.move(12).start()
         if k == 5:
+            self.store().wait()
             self.move(11).wait()
             self.move(12).wait()
 
@@ -1048,18 +1072,6 @@
 STAT = 1792
 
 
-def column_of(row):
-    n = row.shape[1]
-    same = lax.broadcasted_iota(jnp.int32, (n, n), 0) == lax.broadcasted_iota(jnp.int32, (n, n), 1)
-    return jnp.sum(jnp.where(same, row, 0.0), axis=1, keepdims=True)
-
-
-def row_of(column):
-    n = column.shape[0]
-    same = lax.broadcasted_iota(jnp.int32, (n, n), 0) == lax.broadcasted_iota(jnp.int32, (n, n), 1)
-    return jnp.sum(jnp.where(same, column, 0.0), axis=0, keepdims=True)
-
-
 def total_of(v):
     return jnp.sum(rows_sum(v), axis=1, keepdims=True)
 
@@ -1234,7 +1246,7 @@
 
     plain_rows(lbias_ref, lbias_new, lbias_v_ref, lbias_v_new, wide)
     plain_rows(tbias_ref, tbias_new, tbias_v_ref, tbias_v_new, 5 * D + 2 * PATCH_IN)
-    loss = jnp.sum(sums_ref[S_SSE : S_SSE + 1, 0:PATCH_IN], axis=1, keepdims=True) / (tokens * PATCH_IN)
+    loss = jnp.sum(sums_ref[S_SSE : S_SSE + 1, 0:TOK], axis=1, keepdims=True) / (tokens * PATCH_IN)
 
     for copy in copies:
         copy.wait()
@@ -1329,25 +1341,22 @@
     return jnp.sum(jnp.where(picked, alpha_bar[None, :], 0.0), axis=1)
 
 
-def patchify(latent_rows):
+def patch_rows(latent_rows):
     images = latent_rows.shape[0]
-    grid_side = GRID // PATCH
-    shaped = latent_rows.reshape(images, CHANNELS, grid_side, PATCH, grid_side, PATCH)
-    shaped = jnp.transpose(shaped, (0, 2, 4, 1, 3, 5))
-    return shaped.reshape(images, grid_side * grid_side, CHANNELS * PATCH * PATCH)
+    side = GRID // PATCH
+    shaped = latent_rows.reshape(images, CHANNELS, side, PATCH, side, PATCH)
+    return jnp.transpose(shaped, (1, 3, 5, 0, 2, 4)).reshape(PATCH_IN, images * TOK)
 
 
 def position_table():
     side = GRID // PATCH
     quarter = D // 4
     omegas = 1.0 / 10000.0 ** (np.arange(quarter) / quarter)
-    places = np.arange(side * side)
-
-    def one_axis(coords):
-        angles = coords[:, None] * omegas[None, :]
-        return np.concatenate([np.sin(angles), np.cos(angles)], axis=1)
-
-    return np.concatenate([one_axis(places % side), one_axis(places // side)], axis=1).astype(np.float32)
+    angles = np.arange(side)[:, None] * omegas[None, :]
+    axis = jnp.asarray(np.concatenate([np.sin(angles), np.cos(angles)], axis=1), F32)
+    across = jnp.broadcast_to(axis[None, :, :], (side, side, 2 * quarter))
+    down = jnp.broadcast_to(axis[:, None, :], (side, side, 2 * quarter))
+    return jnp.concatenate([across, down], axis=2).reshape(side * side, D)
 
 
 def time_features(tsteps):
@@ -1448,14 +1457,14 @@
 
     alphas = mix_weights(tsteps)
     noisy = jnp.sqrt(alphas)[:, None, None] * latents + jnp.sqrt(1.0 - alphas)[:, None, None] * noise
-    patches = patchify(noisy).astype(BF16).reshape(images * TOK, PATCH_IN)
-    target = patchify(noise).reshape(images * TOK, PATCH_IN)
+    patches = patch_rows(noisy.astype(BF16))
+    target = patch_rows(noise)
 
     w_in, w_out = fetch(layer_in, layer_out)
     g_in, g_out, sums, d_mods = compute(
         patches,
         target,
-        jnp.asarray(position_table()),
+        position_table(),
         jnp.transpose(jnp.pad(mods, ((0, 8 - images), (0, 16 - kinds), (0, 0))), (1, 0, 2)),
         w_in,
         w_out.reshape(depth, FF // FFC, FFC, D),
@@ -1482,7 +1491,7 @@
     g_patch, g_head = sums[:S_HEAD], sums[S_HEAD:S_BIAS]
     g_bias = sums[S_BIAS:S_BPATCH].reshape(depth, BW)
     g_bpatch, g_bhead = sums[S_BPATCH : S_BPATCH + 1], sums[S_BHEAD : S_BHEAD + 1, :PATCH_IN]
-    sse = jnp.sum(sums[S_SSE, :PATCH_IN])
+    sse = jnp.sum(sums[S_SSE, :TOK])
 
     tok_total = every * TOK
     scale_grad = 1.0 / (PATCH_IN * math.sqrt(tok_total))
@@ -1645,10 +1654,10 @@
 
     alphas = mix_weights(tsteps)
     noisy = jnp.sqrt(alphas)[:, None, None] * latents + jnp.sqrt(1.0 - alphas)[:, None, None] * noise
-    patches = patchify(noisy).astype(BF16).reshape(images * TOK, PATCH_IN)
-    target = patchify(noise).reshape(images * TOK, PATCH_IN)
+    patches = patch_rows(noisy.astype(BF16))
+    target = patch_rows(noise)
     _, _, sums, _, out_t, out_m, d_mods = compute(
-        patches, target, jnp.asarray(position_table()), mods, w_in, w_out, w_patch, w_head, layer_bias, tbias, own
+        patches, target, position_table(), mods, w_in, w_out, w_patch, w_head, layer_bias, tbias, own
     )
     weights = (layer_in, layer_out, edge_a, layer_bias, tbias)
     stats = (

time: 355 us -> 329 us (0.927); the launches traced: 350 us -> 329 us
  Pallas kernels: 313 us -> 292 us
    pallas_call x1, Pallas kernels: 222 us -> 200 us  [compute(): pl.pallas_call(functools.partial(compute_kernel, images, group, direct),...]
    convert_element_type x4 -> x1, local copies, waits for them, and re-layouts: 4.13 us -> 0.52 us  [direct_step(): patches = patch_rows(noisy.astype(BF16))]
    unnamed x56 -> x58, local copies, waits for them, and re-layouts: 8.19 us -> 8.2 us
where the time goes in v5:
time: 329 us
  Pallas kernels  292 us (89%)
  local copies, waits for them, and re-layouts  27.9 us (8%)
  other arithmetic  7.73 us (2%)
    pallas_call x1, Pallas kernels, compute(): pl.pallas_call(functools.partial(compute_kernel, images, group, direct),...  200 us
    pallas_call x1, Pallas kernels, prologue(): pl.pallas_call(functools.partial(prologue_kernel, kinds, images), out_sha...  57.7 us
    pallas_call x1, Pallas kernels, update(): pl.pallas_call(functools.partial(update_kernel, sizes), out_shape=outs, i...  34.8 us
    unnamed x58, local copies, waits for them, and re-layouts  8.2 us

profile of v5, /device:TPU:0, one launch (start us, length us, event | category | flops | bytes accessed | tf_op | source)
XLA Modules:
  0.0 328.8 jit_solution(10992845057495271042)
XLA Ops:
  0.7 1.2 slice.92
  1.9 1.0 slice_select_fusion
  2.9 0.8 slice.91
  3.7 0.9 slice.93
  4.5 0.8 fusion.5
  5.7 0.8 pad_maximum_fusion.w_mods_ref
  6.5 0.9 slice.122.own_in_ref.refs_10_
  8.2 0.7 convert_element_type.32
  9.0 57.7 %step_prologue.1 = (bf16[384,16]{1,0:T(8,128)(2,1)}, bf16[384,16]{1,0:T(8,128)(2,1)}, bf16[384,384]{1,0:T(8,128)(2,1)}, bf16[384,3072]{1,0:T(8,128)(2,1)}, bf16[...) custom-call(bf16[48,2048]{1,0:T(8,128)(2,1)} %copy-done.4, ...), custom_call_target="tpu_custom_call" | custom-call | tf_op jit(solution)/shard_map/step_prologue/pallas_call | solution.py:1036
  68.2 2.2 copy.40
  70.4 1.1 reshape.89.refs_0_
  72.2 2.2 copy.42
  74.4 1.1 reshape.91.refs_1_
  75.5 0.9 pad_maximum_fusion.1
  77.0 199.6 %step_compute.1 = (f32[2,4,384,384]{3,2,1,0:T(8,128)}, f32[2,4,384,768]{3,2,1,0:T(8,128)}, f32[7,8,384]{2,1,0:T(8,128)}, bf16[16,8,384]{2,1,0:T(8,128)(2,1)}, f3...) custom-call(bf16[16,1536]{1,0:T(8,128)(2,1)} %reshape.89.refs_0_, ...), custom_call_target="tpu_custom_call" | custom-call | tf_op jit(solution)/shard_map/step_compute/pallas_call | solution.py:640
  276.6 0.7 broadcast_in_dim.64
  278.9 34.8 %step_update.1 = (f32[2,48,5376]{2,1,0:T(8,128)}, f32[2,192,384]{2,1,0:T(8,128)}, f32[48,2688]{1,0:T(8,128)}, f32[2,5376]{1,0:T(2,128)}, f32[1,1952]{1,0:T(1,128...) custom-call(f32[2,4,48,384]{3,2,1,0:T(8,128)} %get-tuple-element.49., ...), custom_call_target="tpu_custom_call" | custom-call | tf_op jit(solution)/shard_map/step_update/pallas_call | solution.py:1315
  313.7 0.8 slice.112
  316.6 1.0 slice.109
  317.6 0.9 slice.107
  318.5 0.7 slice.108
  319.3 0.9 concatenate.30
  321.4 1.3 copy.58
  322.7 0.8 copy.59
  (92 shorter events, 13.8 us)
Async XLA Ops:
  0.6 4.8 %copy-start = (f32[2,48,5376]{2,1,0:T(8,128)S(1)}, f32[2,48,5376]{2,1,0:T(8,128)}, u32[]{:S(2)}) copy-start(f32[2,48,5376]{2,1,0:T(8,128)} %in_ref.1) | copy-start | bytes 6193156
  5.4 1.1 copy-start.4
  5.6 1.8 copy-start.17
  5.6 1.9 copy-start.18
  5.6 2.6 copy-start.1
  6.5 61.0 %copy-start.5 = (f32[6,4,1024]{2,1,0:T(4,128)S(1)}, f32[6,4,1024]{2,1,0:T(4,128)}, u32[]{:S(2)}) copy-start(f32[6,4,1024]{2,1,0:T(4,128)} %param.21) | copy-start | bytes 294916
  6.5 61.0 %copy-start.7 = (f32[6,4,1024]{2,1,0:T(4,128)S(1)}, f32[6,4,1024]{2,1,0:T(4,128)}, u32[]{:S(2)}) copy-start(f32[6,4,1024]{2,1,0:T(4,128)} %param.18) | copy-start | bytes 294916
  72.1 3.3 copy-start.8
  72.2 4.2 %copy-start.6 = (f32[2,5376]{1,0:T(2,128)S(1)}, f32[2,5376]{1,0:T(2,128)}, u32[]{:S(2)}) copy-start(f32[2,5376]{1,0:T(2,128)} %lbias_ref.3) | copy-start | bytes 129028
  313.7 6.5 %copy-start.20 = (f32[1,128]{1,0:T(1,128)S(1)}, f32[1,128]{1,0:T(1,128)}, u32[]{:S(2)}) copy-start(f32[1,128]{1,0:T(1,128)} %get-tuple-element.59) | copy-start | bytes 1540
  313.7 7.6 %copy-start.2 = (f32[2,48,5376]{2,1,0:T(8,128)S(1)}, f32[2,48,5376]{2,1,0:T(8,128)}, u32[]{:S(2)}) copy-start(f32[2,48,5376]{2,1,0:T(8,128)} %get-tuple-element.97) | copy-start | bytes 6193156
  320.2 2.5 copy-start.3
  321.3 2.2 copy-start.11
  321.3 2.8 copy-start.13
  321.3 3.4 %copy-start.16 = (f32[2,48]{1,0:T(2,128)S(1)}, f32[2,48]{1,0:T(2,128)}, u32[]{:S(2)}) copy-start(f32[2,48]{1,0:T(2,128)} %get-tuple-element.102) | copy-start | bytes 1156
  321.3 4.0 %copy-start.10 = (f32[2,5376]{1,0:T(2,128)S(1)}, f32[2,5376]{1,0:T(2,128)}, u32[]{:S(2)}) copy-start(f32[2,5376]{1,0:T(2,128)} %get-tuple-element.103) | copy-start | bytes 129028
  321.3 4.6 %copy-start.15 = (f32[2,192]{1,0:T(2,128)S(1)}, f32[2,192]{1,0:T(2,128)}, u32[]{:S(2)}) copy-start(f32[2,192]{1,0:T(2,128)} %get-tuple-element.104) | copy-start | bytes 4612
  321.3 5.2 %copy-start.14 = (f32[2,384]{1,0:T(2,128)S(1)}, f32[2,384]{1,0:T(2,128)}, u32[]{:S(2)}) copy-start(f32[2,384]{1,0:T(2,128)} %get-tuple-element.105) | copy-start | bytes 9220
  321.3 5.7 %copy-start.19 = (f32[1,48]{1,0:T(1,128)S(1)}, f32[1,48]{1,0:T(1,128)}, u32[]{:S(2)}) copy-start(f32[1,48]{1,0:T(1,128)} %get-tuple-element.69) | copy-start | bytes 580
  321.4 6.2 %copy-start.9 = (f32[2,5376]{1,0:T(2,128)S(1)}, f32[2,5376]{1,0:T(2,128)}, u32[]{:S(2)}) copy-start(f32[2,5376]{1,0:T(2,128)} %get-tuple-element.108) | copy-start | bytes 129028
  321.4 6.8 %copy-start.12 = (f32[1,1952]{1,0:T(1,128)S(1)}, f32[1,1952]{1,0:T(1,128)}, u32[]{:S(2)}) copy-start(f32[1,1952]{1,0:T(1,128)} %get-tuple-element.72) | copy-start | bytes 23428
